TPU v7x, 32 devices: a whole 2x2x4 slice. The times are simulated.
32 devices in a mesh: slab: 8 (over z, y), batch: 4 (over x, core).
Axes of the slice: x: 2, y: 2, z: 4, core: 2. Of those that a mesh axis runs over, the one named last changes fastest.
Arguments:
- velocity_old: float32 [3, 16, 64, 128], P(None, 'slab', 'batch'), may hold values from -40 to 40
- courant: float32 [3, 16, 64, 128], P(None, 'slab', 'batch'), may hold values from -1.5 to 1.5
- cell_ids: int32 [32768], P(('slab', 'batch')), may hold values from 0 to 16383
- forces: float32 [3, 32768], P(None, ('slab', 'batch')), may hold values from -6 to 6
- weights: float32 [32768], P(('slab', 'batch')), may hold values from 0.25 to 4
Outputs:
- velocity_new: float32 [3, 16, 64, 128], P(None, 'slab', 'batch')
- residual: float32 [3, 16, 64, 128], P(None, 'slab', 'batch')
Inputs may be any that keep to these rules, and one draw needn't show every extreme that they name: `cell_ids`: each device's block of 1024 particles lists 1 * 128 particles for each destination slab in turn, slab 0 first.
All inputs are finite; a program needn't handle non-finite values.
Results may differ from a plain program's by a relative error of at most 0.0012.
Values may be sent and summed in bfloat16 or wider, within the bound.
No kernel may reach another device: no remote copies, remote signals or barrier semaphores. Data moves between devices by JAX's collectives and lax.ppermute only.
A program may use at most 64 MiB of HBM per device.

v0:
```python
import math

import jax
import jax.numpy as jnp
from jax import lax
from jax.sharding import PartitionSpec as P

ITERS = 2


diffusion_number = 1.0
diagonal_value = 7.0
deposit_block = 1024


def extended(block, sides, width):
    for axis, dim in sides:
        count = lax.axis_size(axis)
        forward = [(i, i + 1) for i in range(count - 1)]
        backward = [(target, source) for source, target in forward]
        low = lax.ppermute(
            lax.slice_in_dim(block, block.shape[dim] - width, None, axis=dim), axis, forward
        )
        high = lax.ppermute(lax.slice_in_dim(block, 0, width, axis=dim), axis, backward)
        block = jnp.concatenate([low, block, high], axis=dim)
    return block


def inner_product(left, right):
    return jnp.sum(left * right, axis=(1, 2, 3))


def expand(scalars):
    return scalars[:, None, None, None]


def factorize(upper_planes, lower_planes):
    inverses = []
    ratios = []
    for plane_index in range(len(upper_planes)):
        if plane_index == 0:
            pivot_value = diagonal_value + jnp.zeros_like(upper_planes[0])
        else:
            pivot_value = diagonal_value + lower_planes[plane_index] * ratios[-1]
        inverses.append(1.0 / pivot_value)
        ratios.append(-upper_planes[plane_index] * inverses[-1])
    return (inverses, ratios)


def solve_planes(value_planes, inverses, ratios, lower_planes):
    forward = []
    for plane_index in range(len(value_planes)):
        current = value_planes[plane_index]
        if plane_index > 0:
            current = current + lower_planes[plane_index] * forward[-1]
        forward.append(current * inverses[plane_index])
    result = [forward[-1]]
    plane_index = 0
    result.insert(0, forward[plane_index] - ratios[plane_index] * result[0])
    return result


def deposit_rows(cell_ids, momentum, row_total, planes, height, row_width):
    particle_count = cell_ids.shape[0]
    block_size = math.gcd(particle_count, deposit_block)
    row_range = lax.iota(jnp.int32, row_total)
    column_range = lax.iota(jnp.int32, row_width)

    def one_block(iteration, running):
        offset = iteration * block_size
        cell_part = lax.dynamic_slice_in_dim(cell_ids, offset, block_size, 0)
        momentum_part = lax.dynamic_slice_in_dim(momentum, offset, block_size, 1)
        plane_index = cell_part // (height * row_width)
        row_number = cell_part // row_width % height
        column = cell_part % row_width
        local_row = row_number * planes + plane_index
        row_hot = (local_row[:, None] == row_range[None, :]).astype(jnp.bfloat16)
        column_hot = column[:, None] == column_range[None, :]
        spread = jnp.where(
            column_hot[:, None, :], momentum_part.T[:, :, None], jnp.zeros((), jnp.bfloat16)
        )
        spread = spread.reshape(block_size, 3 * row_width)
        return running + jnp.einsum(
            "pr,pc->rc", row_hot, spread, preferred_element_type=jnp.float32
        )

    initial = jnp.zeros((row_total, 3 * row_width), jnp.float32)
    return lax.fori_loop(0, particle_count // block_size, one_block, initial)


def local(velocity_old, courant, cell_ids, forces, weights):
    planes = velocity_old.shape[1]
    rows_quarter = velocity_old.shape[2]
    row_width = velocity_old.shape[3]
    height = rows_quarter * lax.axis_size("batch")
    block_rows = planes * rows_quarter
    momentum = (weights[None, :] * forces).astype(jnp.bfloat16)
    ids_here = lax.all_to_all(cell_ids, "slab", split_axis=0, concat_axis=0, tiled=True)
    moved_momentum = lax.all_to_all(momentum, "slab", split_axis=1, concat_axis=1, tiled=True)
    summed = lax.psum_scatter(
        deposit_rows(
            ids_here, moved_momentum, block_rows * lax.axis_size("batch"), planes, height, row_width
        ),
        "batch",
        scatter_dimension=0,
        tiled=True,
    )
    source = summed.reshape(rows_quarter, planes, 3, row_width).transpose(2, 1, 0, 3)
    right_side = velocity_old + source
    upper = diffusion_number - 0.5 * courant
    lower = diffusion_number + 0.5 * courant
    upper_planes = [upper[0, plane_index] for plane_index in range(planes)]
    lower_planes = [lower[0, plane_index] for plane_index in range(planes)]
    inverses, ratios = factorize(upper_planes, lower_planes)

    def operate(values):
        padded = extended(values, (("slab", 1), ("batch", 2)), 1)
        edge_zeros = jnp.zeros_like(values[..., :1])
        plus_x = jnp.concatenate([values[..., 1:], edge_zeros], axis=3)
        minus_x = jnp.concatenate([edge_zeros, values[..., :-1]], axis=3)
        beside = upper[0] * padded[:, 2:, 1:-1] + lower[0] * padded[:, :-2, 1:-1]
        beside = beside + upper[1] * padded[:, 1:-1, 2:] + lower[1] * padded[:, 1:-1, :-2]
        beside = beside + upper[2] * plus_x + lower[2] * minus_x
        return diagonal_value * values - beside

    def precondition(values):
        value_planes = [values[:, plane_index] for plane_index in range(planes)]
        result = solve_planes(value_planes, inverses, ratios, lower_planes)
        return jnp.stack(result, axis=1)

    solution = jnp.zeros_like(right_side)
    residual = right_side
    direction = right_side
    rho_now = None
    for iteration in range(ITERS):
        precond_dir = precondition(direction)
        image_dir = operate(precond_dir)
        if iteration == 0:
            stacked_terms = jnp.stack(
                [inner_product(right_side, image_dir), inner_product(right_side, residual)], axis=0
            )
        else:
            stacked_terms = inner_product(right_side, image_dir)[None, :]
        gathered_sums = lax.psum(stacked_terms, ("slab", "batch"))
        along_sum = gathered_sums[0]
        if iteration == 0:
            rho_now = gathered_sums[1]
        step_alpha = rho_now / along_sum
        middle = residual - expand(step_alpha) * image_dir
        precond_mid = precondition(middle)
        turned = operate(precond_mid)
        term_list = [inner_product(turned, middle), inner_product(turned, turned)]
        if iteration + 1 < ITERS:
            term_list.append(inner_product(right_side, turned))
        closing_sums = lax.psum(jnp.stack(term_list, axis=0), ("slab", "batch"))
        cross_sum = closing_sums[0]
        square = closing_sums[1]
        shadow_turned = closing_sums[2] if iteration + 1 < ITERS else None
        step_omega = cross_sum / square
        solution = solution + expand(step_alpha) * precond_dir + expand(step_omega) * precond_mid
        residual = middle - expand(step_omega) * turned
        if iteration + 1 < ITERS:
            rho_next = rho_now - step_alpha * along_sum - step_omega * shadow_turned
            factor = rho_next / rho_now * (step_alpha / step_omega)
            direction = residual + expand(factor) * (direction - expand(step_omega) * image_dir)
            rho_now = rho_next
    return (solution, residual)


def solution(mesh):
    placed = (
        P(None, "slab", "batch", None),
        P(None, "slab", "batch", None),
        P(("slab", "batch")),
        P(None, ("slab", "batch")),
        P(("slab", "batch")),
    )
    return jax.shard_map(
        local,
        mesh=mesh,
        in_specs=placed,
        out_specs=(P(None, "slab", "batch", None), P(None, "slab", "batch", None)),
        check_vma=False,
    )
```

profile of v0, /device:TPU:0, one launch (start us, length us, event | category | flops | bytes accessed | tf_op | source)
XLA Modules:
  0.0 286.1 jit_solution(11093976552176510271)
XLA Ops:
  7.2 7.3 %all-to-all-start = ((s32[8,128,1]{1,2,0:T(1,128)}), s32[8,128,1]{1,2,0:T(1,128)S(1)}, u32[]{:S(2)}, u32[]{:S(2)}) async-start(s32[8,128,1]{1,2,0:T(1,128)} %bitcast.93), calls=%async_computation | async-start | bytes 8192 | tf_op jit(solution)/shard_map/all_to_all | solution.py:98
  16.0 5.0 %all-to-all-done = s32[8,128,1]{1,2,0:T(1,128)S(1)} async-done(((s32[8,128,1]{1,2,0:T(1,128)}), s32[8,128,1]{1,2,0:T(1,128)S(1)}, u32[]{:S(2)}, u32[]{:S(2)}) %all-to-all-start) | async-done | bytes 4128 | tf_op jit(solution)/shard_map/all_to_all | solution.py:98
  20.9 3.3 %all-to-all-start.1 = ((bf16[3,8,128]{2,0,1:T(4,128)(2,1)}), bf16[3,8,128]{2,0,1:T(4,128)(2,1)S(1)}, u32[]{:S(2)}, u32[]{:S(2)}) async-start(bf16[3,8,128]{2,0,1:T(4,128)(2,1)} %fusion.48), calls=%async_computation.1 | async-start | bytes 16384 | tf_op jit(solution)/shard_map/all_to_all | solution.py:99
  24.4 6.3 %all-to-all-done.1 = bf16[3,8,128]{2,0,1:T(4,128)(2,1)S(1)} async-done(((bf16[3,8,128]{2,0,1:T(4,128)(2,1)}), bf16[3,8,128]{2,0,1:T(4,128)(2,1)S(1)}, u32[]{:S(2)}, u32[]{:S(2)}) %all-to-all-start.1) | async-done | bytes 6176 | tf_op jit(solution)/shard_map/all_to_all | solution.py:99
  32.1 17.2 %reduce-scatter.2.cloned.1.call-done = f32[32,384]{1,0:T(8,128)} async-done(((f32[128,384]{1,0:T(8,128)}), f32[32,384]{1,0:T(8,128)}) %reduce-scatter.2.cloned.1.call-update) | async-done | bytes 49168 | tf_op jit(solution)/shard_map/reduce_scatter | solution.py:100
  50.2 1.3 collective-permute-start
  51.5 4.5 %collective-permute-start.1 = (f32[3,1,16,128]{3,0,1,2:T(4,128)S(1)}, f32[3,1,16,128]{3,0,1,2:T(4,128)S(1)}, u32[]{:S(2)}, u32[]{:S(2)}) collective-permute-start(f32[3,1,16,128]{3,0,1,2:T(4,128)S(1)} %get-tuple-element.75), channel_id=1, source_target_pairs={{0,4},{4,8},{8,12},{12,16},{16,20},{20,24},{24,28},{1,5},{5,9},{9,... | collective-permute-start | bytes 73736 | tf_op jit(solution)/shard_map/ppermute | solution.py:21
  56.2 1.4 collective-permute-done.1
  57.6 1.3 collective-permute-start.3
  58.9 1.3 collective-permute-start.2
  60.3 2.2 collective-permute-done.2
  62.7 42.7 %psum.28 = f32[2,3]{1,0:T(2,128)S(1)} all-reduce(f32[2,3]{1,0:T(2,128)S(1)} %pad_maximum_fusion.53), channel_id=1, replica_groups=mesh['slab'=8,'batch'=4] {'slab','batch'}, use_global_device_ids=true, to_apply=%region_3.4 | all-reduce | flops 6 | bytes 48 | tf_op jit(solution)/shard_map/psum | solution.py:144
  105.5 1.3 collective-permute-start.4
  106.8 4.8 %collective-permute-start.5 = (f32[3,1,16,128]{3,0,1,2:T(4,128)S(1)}, f32[3,1,16,128]{3,0,1,2:T(4,128)S(1)}, u32[]{:S(2)}, u32[]{:S(2)}) collective-permute-start(f32[3,1,16,128]{3,0,1,2:T(4,128)S(1)} %get-tuple-element.72), channel_id=1, source_target_pairs={{0,4},{4,8},{8,12},{12,16},{16,20},{20,24},{24,28},{1,5},{5,9},{9,... | collective-permute-start | bytes 73736 | tf_op jit(solution)/shard_map/ppermute | solution.py:21
  111.7 1.6 collective-permute-done.5
  113.2 1.3 collective-permute-start.7
  114.5 1.3 collective-permute-start.6
  115.9 3.9 %collective-permute-done.6 = f32[3,4,1,128]{3,0,1,2:T(4,128)S(1)} collective-permute-done((f32[3,4,1,128]{3,0,1,2:T(4,128)S(1)}, f32[3,4,1,128]{3,0,1,2:T(4,128)S(1)}, u32[]{:S(2)}, u32[]{:S(2)}) %collective-permute-start.6) | collective-permute-done | bytes 6176 | tf_op jit(solution)/shard_map/ppermute | solution.py:24
  120.2 42.8 %psum.29 = f32[3,3]{1,0:T(4,128)S(1)} all-reduce(f32[3,3]{1,0:T(4,128)S(1)} %pad_maximum_fusion.52), channel_id=1, replica_groups=mesh['slab'=8,'batch'=4] {'slab','batch'}, use_global_device_ids=true, to_apply=%region_7.8 | all-reduce | flops 9 | bytes 72 | tf_op jit(solution)/shard_map/psum | solution.py:155
  163.1 1.3 collective-permute-start.8
  164.4 4.8 %collective-permute-start.9 = (f32[3,1,16,128]{3,0,1,2:T(4,128)S(1)}, f32[3,1,16,128]{3,0,1,2:T(4,128)S(1)}, u32[]{:S(2)}, u32[]{:S(2)}) collective-permute-start(f32[3,1,16,128]{3,0,1,2:T(4,128)S(1)} %get-tuple-element.66), channel_id=1, source_target_pairs={{0,4},{4,8},{8,12},{12,16},{16,20},{20,24},{24,28},{1,5},{5,9},{9,... | collective-permute-start | bytes 73736 | tf_op jit(solution)/shard_map/ppermute | solution.py:21
  169.3 1.6 collective-permute-done.9
  170.8 1.3 collective-permute-start.11
  172.1 1.3 collective-permute-start.10
  173.5 3.9 %collective-permute-done.10 = f32[3,4,1,128]{3,0,1,2:T(4,128)S(1)} collective-permute-done((f32[3,4,1,128]{3,0,1,2:T(4,128)S(1)}, f32[3,4,1,128]{3,0,1,2:T(4,128)S(1)}, u32[]{:S(2)}, u32[]{:S(2)}) %collective-permute-start.10) | collective-permute-done | bytes 6176 | tf_op jit(solution)/shard_map/ppermute | solution.py:24
  177.7 42.8 %psum.30 = f32[3]{0:T(128)S(1)} all-reduce(f32[3]{0:T(128)S(1)} %get-tuple-element.63), channel_id=1, replica_groups=mesh['slab'=8,'batch'=4] {'slab','batch'}, use_global_device_ids=true, to_apply=%region_9.10 | all-reduce | flops 3 | bytes 24 | tf_op jit(solution)/shard_map/psum | solution.py:144
  220.6 1.3 collective-permute-start.12
  221.9 4.8 %collective-permute-start.13 = (f32[3,1,16,128]{3,0,1,2:T(4,128)S(1)}, f32[3,1,16,128]{3,0,1,2:T(4,128)S(1)}, u32[]{:S(2)}, u32[]{:S(2)}) collective-permute-start(f32[3,1,16,128]{3,0,1,2:T(4,128)S(1)} %get-tuple-element.62), channel_id=1, source_target_pairs={{0,4},{4,8},{8,12},{12,16},{16,20},{20,24},{24,28},{1,5},{5,9},{9,... | collective-permute-start | bytes 73736 | tf_op jit(solution)/shard_map/ppermute | solution.py:21
  226.7 1.6 collective-permute-done.13
  229.6 1.3 collective-permute-start.14
  231.0 3.9 %collective-permute-done.14 = f32[3,4,1,128]{3,0,1,2:T(4,128)S(1)} collective-permute-done((f32[3,4,1,128]{3,0,1,2:T(4,128)S(1)}, f32[3,4,1,128]{3,0,1,2:T(4,128)S(1)}, u32[]{:S(2)}, u32[]{:S(2)}) %collective-permute-start.14) | collective-permute-done | bytes 6176 | tf_op jit(solution)/shard_map/ppermute | solution.py:24
  235.1 42.7 %psum.31 = f32[2,3]{1,0:T(2,128)S(1)} all-reduce(f32[2,3]{1,0:T(2,128)S(1)} %pad_maximum_fusion.54), channel_id=1, replica_groups=mesh['slab'=8,'batch'=4] {'slab','batch'}, use_global_device_ids=true, to_apply=%region_12.13 | all-reduce | flops 6 | bytes 48 | tf_op jit(solution)/shard_map/psum | solution.py:155
  (63 shorter events, 8.4 us)
Async XLA Ops:
  7.2 13.7 %all-to-all-start = ((s32[8,128,1]{1,2,0:T(1,128)}), s32[8,128,1]{1,2,0:T(1,128)S(1)}, u32[]{:S(2)}, u32[]{:S(2)}) async-start(s32[8,128,1]{1,2,0:T(1,128)} %bitcast.93), calls=%async_computation | async-start | bytes 8192 | tf_op jit(solution)/shard_map/all_to_all | solution.py:98
  14.5 0.8 copy-start.1
  14.5 0.8 copy-start.2
  20.9 9.8 %all-to-all-start.1 = ((bf16[3,8,128]{2,0,1:T(4,128)(2,1)}), bf16[3,8,128]{2,0,1:T(4,128)(2,1)S(1)}, u32[]{:S(2)}, u32[]{:S(2)}) async-start(bf16[3,8,128]{2,0,1:T(4,128)(2,1)} %fusion.48), calls=%async_computation.1 | async-start | bytes 16384 | tf_op jit(solution)/shard_map/all_to_all | solution.py:99
  24.2 25.0 %reduce-scatter.2.cloned.1.call-start = ((), (), s32[]{:S(2)}) async-start(), calls=%async_computation.3 | async-start | bytes 245760 | tf_op jit(solution)/shard_map/reduce_scatter | solution.py:100
  32.1 18.0 %copy-start = (f32[3,2,16,128]{3,2,1,0:T(8,128)S(1)}, f32[3,2,16,128]{3,2,1,0:T(8,128)}, u32[]{:S(2)}) copy-start(f32[3,2,16,128]{3,2,1,0:T(8,128)} %param.5) | copy-start | bytes 147460
  50.2 6.0 %collective-permute-start = (f32[3,1,16,128]{3,0,1,2:T(4,128)S(1)}, f32[3,1,16,128]{3,0,1,2:T(4,128)S(1)}, u32[]{:S(2)}, u32[]{:S(2)}) collective-permute-start(f32[3,1,16,128]{3,0,1,2:T(4,128)S(1)} %get-tuple-element.74), channel_id=1, source_target_pairs={{4,0},{8,4},{12,8},{16,12},{20,16},{24,20},{28,24},{5,1},{9,5},{13... | collective-permute-start | bytes 73736 | tf_op jit(solution)/shard_map/ppermute | solution.py:24
  51.5 6.1 %collective-permute-start.1 = (f32[3,1,16,128]{3,0,1,2:T(4,128)S(1)}, f32[3,1,16,128]{3,0,1,2:T(4,128)S(1)}, u32[]{:S(2)}, u32[]{:S(2)}) collective-permute-start(f32[3,1,16,128]{3,0,1,2:T(4,128)S(1)} %get-tuple-element.75), channel_id=1, source_target_pairs={{0,4},{4,8},{8,12},{12,16},{16,20},{20,24},{24,28},{1,5},{5,9},{9,... | collective-permute-start | bytes 73736 | tf_op jit(solution)/shard_map/ppermute | solution.py:21
  57.6 2.7 collective-permute-start.3
  58.9 3.6 %collective-permute-start.2 = (f32[3,4,1,128]{3,0,1,2:T(4,128)S(1)}, f32[3,4,1,128]{3,0,1,2:T(4,128)S(1)}, u32[]{:S(2)}, u32[]{:S(2)}) collective-permute-start(f32[3,4,1,128]{3,0,1,2:T(4,128)S(1)} %get-tuple-element.82), channel_id=1, source_target_pairs={{1,0},{2,1},{3,2},{5,4},{6,5},{7,6},{9,8},{10,9},{11,10},{13,12},{... | collective-permute-start | bytes 18440 | tf_op jit(solution)/shard_map/ppermute | solution.py:24
  105.5 6.1 %collective-permute-start.4 = (f32[3,1,16,128]{3,0,1,2:T(4,128)S(1)}, f32[3,1,16,128]{3,0,1,2:T(4,128)S(1)}, u32[]{:S(2)}, u32[]{:S(2)}) collective-permute-start(f32[3,1,16,128]{3,0,1,2:T(4,128)S(1)} %get-tuple-element.71), channel_id=1, source_target_pairs={{4,0},{8,4},{12,8},{16,12},{20,16},{24,20},{28,24},{5,1},{9,5},{13... | collective-permute-start | bytes 73736 | tf_op jit(solution)/shard_map/ppermute | solution.py:24
  106.8 6.4 %collective-permute-start.5 = (f32[3,1,16,128]{3,0,1,2:T(4,128)S(1)}, f32[3,1,16,128]{3,0,1,2:T(4,128)S(1)}, u32[]{:S(2)}, u32[]{:S(2)}) collective-permute-start(f32[3,1,16,128]{3,0,1,2:T(4,128)S(1)} %get-tuple-element.72), channel_id=1, source_target_pairs={{0,4},{4,8},{8,12},{12,16},{16,20},{20,24},{24,28},{1,5},{5,9},{9,... | collective-permute-start | bytes 73736 | tf_op jit(solution)/shard_map/ppermute | solution.py:21
  113.2 2.7 collective-permute-start.7
  114.5 5.3 %collective-permute-start.6 = (f32[3,4,1,128]{3,0,1,2:T(4,128)S(1)}, f32[3,4,1,128]{3,0,1,2:T(4,128)S(1)}, u32[]{:S(2)}, u32[]{:S(2)}) collective-permute-start(f32[3,4,1,128]{3,0,1,2:T(4,128)S(1)} %get-tuple-element.80), channel_id=1, source_target_pairs={{1,0},{2,1},{3,2},{5,4},{6,5},{7,6},{9,8},{10,9},{11,10},{13,12},{... | collective-permute-start | bytes 18440 | tf_op jit(solution)/shard_map/ppermute | solution.py:24
  163.1 6.1 %collective-permute-start.8 = (f32[3,1,16,128]{3,0,1,2:T(4,128)S(1)}, f32[3,1,16,128]{3,0,1,2:T(4,128)S(1)}, u32[]{:S(2)}, u32[]{:S(2)}) collective-permute-start(f32[3,1,16,128]{3,0,1,2:T(4,128)S(1)} %get-tuple-element.65), channel_id=1, source_target_pairs={{4,0},{8,4},{12,8},{16,12},{20,16},{24,20},{28,24},{5,1},{9,5},{13... | collective-permute-start | bytes 73736 | tf_op jit(solution)/shard_map/ppermute | solution.py:24
  164.4 6.4 %collective-permute-start.9 = (f32[3,1,16,128]{3,0,1,2:T(4,128)S(1)}, f32[3,1,16,128]{3,0,1,2:T(4,128)S(1)}, u32[]{:S(2)}, u32[]{:S(2)}) collective-permute-start(f32[3,1,16,128]{3,0,1,2:T(4,128)S(1)} %get-tuple-element.66), channel_id=1, source_target_pairs={{0,4},{4,8},{8,12},{12,16},{16,20},{20,24},{24,28},{1,5},{5,9},{9,... | collective-permute-start | bytes 73736 | tf_op jit(solution)/shard_map/ppermute | solution.py:21
  170.8 2.7 collective-permute-start.11
  172.1 5.3 %collective-permute-start.10 = (f32[3,4,1,128]{3,0,1,2:T(4,128)S(1)}, f32[3,4,1,128]{3,0,1,2:T(4,128)S(1)}, u32[]{:S(2)}, u32[]{:S(2)}) collective-permute-start(f32[3,4,1,128]{3,0,1,2:T(4,128)S(1)} %get-tuple-element.78), channel_id=1, source_target_pairs={{1,0},{2,1},{3,2},{5,4},{6,5},{7,6},{9,8},{10,9},{11,10},{13,12},{... | collective-permute-start | bytes 18440 | tf_op jit(solution)/shard_map/ppermute | solution.py:24
  220.6 6.1 %collective-permute-start.12 = (f32[3,1,16,128]{3,0,1,2:T(4,128)S(1)}, f32[3,1,16,128]{3,0,1,2:T(4,128)S(1)}, u32[]{:S(2)}, u32[]{:S(2)}) collective-permute-start(f32[3,1,16,128]{3,0,1,2:T(4,128)S(1)} %get-tuple-element.61), channel_id=1, source_target_pairs={{4,0},{8,4},{12,8},{16,12},{20,16},{24,20},{28,24},{5,1},{9,5},{13... | collective-permute-start | bytes 73736 | tf_op jit(solution)/shard_map/ppermute | solution.py:24
  221.9 6.4 %collective-permute-start.13 = (f32[3,1,16,128]{3,0,1,2:T(4,128)S(1)}, f32[3,1,16,128]{3,0,1,2:T(4,128)S(1)}, u32[]{:S(2)}, u32[]{:S(2)}) collective-permute-start(f32[3,1,16,128]{3,0,1,2:T(4,128)S(1)} %get-tuple-element.62), channel_id=1, source_target_pairs={{0,4},{4,8},{8,12},{12,16},{16,20},{20,24},{24,28},{1,5},{5,9},{9,... | collective-permute-start | bytes 73736 | tf_op jit(solution)/shard_map/ppermute | solution.py:21
  228.3 2.7 collective-permute-start.15
  229.6 5.3 %collective-permute-start.14 = (f32[3,4,1,128]{3,0,1,2:T(4,128)S(1)}, f32[3,4,1,128]{3,0,1,2:T(4,128)S(1)}, u32[]{:S(2)}, u32[]{:S(2)}) collective-permute-start(f32[3,4,1,128]{3,0,1,2:T(4,128)S(1)} %get-tuple-element.76), channel_id=1, source_target_pairs={{1,0},{2,1},{3,2},{5,4},{6,5},{7,6},{9,8},{10,9},{11,10},{13,12},{... | collective-permute-start | bytes 18440 | tf_op jit(solution)/shard_map/ppermute | solution.py:24
Sparse Core Ops, SparseCore 0:
  32.2 17.0 reduce-scatter.1
where the time goes:
time: 287 us; the launch traced here: 286 us
  blocking collectives  171 us (60%)
  waiting for transfers between devices  48.5 us (17%)
  starting transfers between devices  45.1 us (16%)
  between operations  14.5 us (5%)
  other arithmetic  3.66 us (1%)
    psum x2, blocking collectives, local(): closing_sums = lax.psum(jnp.stack(term_list, axis=0), ('slab', 'batch'))  85.6 us
    psum x2, blocking collectives, local(): gathered_sums = lax.psum(stacked_terms, ('slab', 'batch'))  85.4 us
    ppermute x8, starting transfers between devices, extended(): lax.ppermute(lax.slice_in_dim(block, block.shape[dim] - width, None, axis...  24.1 us
    reduce_scatter x1, waiting for transfers between devices, local(): lax.psum_scatter(deposit_rows(ids_here, moved_momentum, block_rows * lax....  17.2 us
    ppermute x8, waiting for transfers between devices, extended(): lax.ppermute(lax.slice_in_dim(block, 0, width, axis=dim), axis, backward)  13.9 us
    ppermute x8, starting transfers between devices, extended(): lax.ppermute(lax.slice_in_dim(block, 0, width, axis=dim), axis, backward)  10.3 us
    all_to_all x1, starting transfers between devices, local(): lax.all_to_all(cell_ids, 'slab', split_axis=0, concat_axis=0, tiled=True)  7.32 us
    all_to_all x1, waiting for transfers between devices, local(): lax.all_to_all(momentum, 'slab', split_axis=1, concat_axis=1, tiled=True)  6.3 us
  transfers between devices with their start and end apart: 19, of which 11 were waited for; matrix products, arithmetic and copies ran while one was open for 1% of the time, Pallas kernels for 0%

commit v1 on v0

v1 whole, which is shorter than its diff:
```python
import jax
import jax.numpy as jnp
from jax import lax
from jax.experimental import pallas as pl
from jax.experimental.pallas import tpu as pltpu
from jax.sharding import PartitionSpec as P

ITERS = 2
DEPTH = 2 * ITERS
COMPS = 3
BASIS = DEPTH + 1
PAIRS = [(i, j) for i in range(BASIS) for j in range(i, BASIS)]

diffusion_number = 1.0
diagonal_value = 7.0

VMEM = pl.BlockSpec(memory_space=pltpu.VMEM)
SMEM = pl.BlockSpec(memory_space=pltpu.SMEM)
F32 = jnp.float32


def two_sum(a, b):
    s = a + b
    bb = s - a
    return s, (a - (s - bb)) + (b - bb)


def quick_two_sum(a, b):
    s = a + b
    return s, b - (s - a)


def split(a):
    t = a * 4097.0
    high = t - (t - a)
    return high, a - high


def product_error(p, a, b):
    ah, al = a
    bh, bl = b
    return ((ah * bh - p) + ah * bl + al * bh) + al * bl


def dd_add(a, b):
    s, e = two_sum(a[0], b[0])
    return quick_two_sum(s, e + (a[1] + b[1]))


def dd_neg(a):
    return -a[0], -a[1]


def dd_sub(a, b):
    return dd_add(a, dd_neg(b))


def dd_mul(a, b):
    p = a[0] * b[0]
    e = product_error(p, split(a[0]), split(b[0]))
    return quick_two_sum(p, e + (a[0] * b[1] + a[1] * b[0]))


def dd_div(a, b):
    inverse = 1.0 / b[0]
    q1 = a[0] * inverse
    zero = jnp.zeros_like(q1)
    r = dd_sub(a, dd_mul((q1, zero), b))
    q2 = r[0] * inverse
    r = dd_sub(r, dd_mul((q2, zero), b))
    q3 = r[0] * inverse
    s, e = quick_two_sum(q1, q2)
    return quick_two_sum(s, e + q3)


def solve_block(values, inverses, ratios, lower_planes):
    forward = []
    for k, current in enumerate(values):
        if k > 0:
            current = current + lower_planes[k] * forward[-1]
        forward.append(current * inverses[k])
    result = [forward[-1]]
    for k in range(len(values) - 2, -1, -1):
        result.insert(0, forward[k] - ratios[k] * result[0])
    return result


def make_message(ids, momentum, slabs, copies, row_width):
    tile = ids.shape[0] // slabs
    high = (ids // row_width).astype(jnp.bfloat16)
    low = (ids % row_width).astype(jnp.bfloat16)
    rows = jnp.concatenate(
        [momentum, high[None], low[None], jnp.zeros((3, ids.shape[0]), jnp.bfloat16)], axis=0
    )
    rows = rows.reshape(8, slabs, tile).transpose(1, 0, 2)
    rows = jnp.broadcast_to(rows[:, None], (slabs, copies, 8, tile))
    return rows.reshape(slabs * copies, 8, tile)


def setup_kernel(
    slabs, copies, group,
    place, message, velocity, velocity_halo, courant, courant_halo,
    value_out, solved_out, first_out, last_out, side_out, block_out, momentum_sum,
):
    planes, rows, width = velocity.shape[1:]
    wide = rows + 2 * DEPTH
    height = rows * copies
    slab, batch = place[0], place[1]
    start = batch * rows
    tile = message.shape[2]
    row_iota = lax.broadcasted_iota(jnp.int32, (planes * wide, tile), 0)
    column_iota = lax.broadcasted_iota(jnp.int32, (width, tile), 0)

    def deposit(step):
        row_hot, spread = [], []
        for k in range(group):
            part = message[step * group + k].astype(F32)
            cell_row = part[3:4].astype(jnp.int32)
            column = part[4:5].astype(jnp.int32)
            plane = jnp.zeros_like(cell_row)
            for p in range(1, planes):
                plane = plane + (cell_row >= p * height).astype(jnp.int32)
            away = cell_row - plane * height - start
            away = jnp.where(away < 0, away + height, away)
            spot = jnp.where(away < rows + DEPTH, away, away - height + wide)
            inside = (away < rows + DEPTH) | (away >= height - DEPTH)
            spot = jnp.where(inside, spot + plane * wide, -1)
            row_hot.append(jnp.where(row_iota == spot, 1.0, 0.0).astype(jnp.bfloat16))
            here = column_iota == column
            spread.append(
                jnp.concatenate(
                    [jnp.where(here, part[c : c + 1], 0.0) for c in range(COMPS)], axis=0
                ).astype(jnp.bfloat16)
            )
        return lax.dot_general(
            jnp.concatenate(row_hot, axis=1),
            jnp.concatenate(spread, axis=1),
            (((1,), (1,)), ((), ())),
            preferred_element_type=F32,
        )

    steps = message.shape[0] // group
    if steps <= 4:
        total = deposit(0)
        for step in range(1, steps):
            total = total + deposit(step)
        momentum_sum[...] = total
    else:
        momentum_sum[...] = jnp.zeros_like(momentum_sum)

        def one(step, carry):
            momentum_sum[...] += deposit(step)
            return carry

        lax.fori_loop(0, steps, one, 0)

    spots = lax.broadcasted_iota(jnp.int32, (wide, width), 0)
    lanes = lax.broadcasted_iota(jnp.int32, (wide, width), 1)
    lower_planes, upper_planes, inverses, ratios = [], [], [], []
    for k in range(planes):
        coefs = []
        for d in range(3):
            half = 0.5 * jnp.concatenate([courant[d, k], courant_halo[d, k]], axis=0)
            coefs.append((diffusion_number - half, diffusion_number + half))
        upper_planes.append(coefs[0][0])
        lower_planes.append(coefs[0][1])
        at_top = (spots == rows - 1) & (batch == copies - 1)
        at_bottom = (spots == 0) & (batch == 0)
        side_out[0, k] = jnp.where(at_top, 0.0, coefs[1][0])
        side_out[1, k] = jnp.where(at_bottom, 0.0, coefs[1][1])
        side_out[2, k] = jnp.where(lanes == width - 1, 0.0, coefs[2][0])
        side_out[3, k] = jnp.where(lanes == 0, 0.0, coefs[2][1])
        if k == 0:
            pivot = jnp.full((wide, width), diagonal_value, F32)
        else:
            pivot = diagonal_value + lower_planes[k] * ratios[-1]
        inverses.append(1.0 / pivot)
        ratios.append(-upper_planes[k] * inverses[-1])
        block_out[0, k] = inverses[k]
        block_out[1, k] = ratios[k]
        block_out[2, k] = lower_planes[k]
    block_out[3, 0] = jnp.where(slab == 0, 0.0, lower_planes[0])
    block_out[3, 1] = jnp.where(slab == slabs - 1, 0.0, upper_planes[planes - 1])
    for c in range(COMPS):
        values = []
        for k in range(planes):
            old = jnp.concatenate([velocity[c, k], velocity_halo[c, k]], axis=0)
            value = old + momentum_sum[k * wide : (k + 1) * wide, c * width : (c + 1) * width]
            value_out[c, k] = value
            values.append(value)
        solved = solve_block(values, inverses, ratios, lower_planes)
        for k in range(planes):
            solved_out[c, k] = solved[k]
        first_out[c] = solved[0]
        last_out[c] = solved[planes - 1]


def couple(c, solved, below, above, side, block):
    planes, wide = solved.shape[1:3]
    width = solved.shape[3]
    result = []
    for k in range(planes):
        here = solved[c, k]
        total = side[0, k] * pltpu.roll(here, wide - 1, 0) + side[1, k] * pltpu.roll(here, 1, 0)
        total = total + side[2, k] * pltpu.roll(here, width - 1, 1)
        total = total + side[3, k] * pltpu.roll(here, 1, 1)
        if k == 0:
            total = total + block[3, 0] * below[c]
        if k == planes - 1:
            total = total + block[3, 1] * above[c]
        result.append(total)
    return result


def apply_kernel(
    solved, below, above, side, block, value_out, solved_out, first_out, last_out
):
    planes = solved.shape[1]
    inverses = [block[0, k] for k in range(planes)]
    ratios = [block[1, k] for k in range(planes)]
    lower_planes = [block[2, k] for k in range(planes)]
    for c in range(COMPS):
        values = couple(c, solved, below, above, side, block)
        result = solve_block(values, inverses, ratios, lower_planes)
        for k in range(planes):
            value_out[c, k] = values[k]
            solved_out[c, k] = result[k]
        first_out[c] = result[0]
        last_out[c] = result[planes - 1]


def gram_kernel(slots, *refs):
    solved, below, above, side, block = refs[:5]
    values = refs[5 : 5 + DEPTH]
    value_out, message_out = refs[5 + DEPTH :]
    planes, wide, width = solved.shape[1:]
    rows = wide - 2 * DEPTH
    sums = []
    for c in range(COMPS):
        newest = couple(c, solved, below, above, side, block)
        for k in range(planes):
            value_out[c, k] = newest[k]
        totals = [None] * len(PAIRS)
        for k in range(planes):
            for r in range(0, rows, 8):
                pieces = [values[i][c, k, r : r + 8, :] for i in range(DEPTH)]
                pieces.append(newest[k][r : r + 8])
                halves = [split(piece) for piece in pieces]
                for n, (i, j) in enumerate(PAIRS):
                    p = pieces[i] * pieces[j]
                    e = product_error(p, halves[i], halves[j])
                    if totals[n] is None:
                        totals[n] = (p, e)
                    else:
                        s, t = two_sum(totals[n][0], p)
                        totals[n] = (s, totals[n][1] + (t + e))
        sums.append(totals)
    flat = [sums[c][n] for n in range(len(PAIRS)) for c in range(COMPS)]
    columns = []
    for part in range(2):
        stacked = jnp.concatenate([x[part] for x in flat], axis=0)
        padded = slots * 8 - stacked.shape[0]
        if padded:
            stacked = jnp.concatenate([stacked, jnp.zeros((padded, width), F32)], axis=0)
        columns.append(jnp.transpose(stacked))
    total = (columns[0][:8], columns[1][:8])
    for r in range(8, width, 8):
        total = dd_add(total, (columns[0][r : r + 8], columns[1][r : r + 8]))
    for shift in (4, 2, 1):
        total = dd_add(total, tuple(pltpu.roll(x, shift, 0) for x in total))
    size = slots * 8
    for shift in (4, 2, 1):
        total = dd_add(total, tuple(pltpu.roll(x, size - shift, 1) for x in total))
    row = jnp.concatenate([total[0][:1], total[1][:1]], axis=1)
    message_out[...] = jnp.broadcast_to(row, message_out.shape)


def finish_kernel(slots, *refs):
    gathered = refs[0]
    values = refs[1 : 1 + BASIS]
    solved = refs[1 + BASIS : 1 + BASIS + DEPTH]
    solution_out, residual_out = refs[1 + BASIS + DEPTH :]
    planes, rows, width = solution_out.shape[1:]
    size = slots * 8
    count = gathered.shape[0]
    high, low = gathered[:, :size], gathered[:, size:]
    total = (high[:8], low[:8])
    for r in range(8, count, 8):
        total = dd_add(total, (high[r : r + 8], low[r : r + 8]))
    for shift in (4, 2, 1):
        total = dd_add(total, tuple(pltpu.roll(x, shift, 0) for x in total))
    lane = lax.broadcasted_iota(jnp.int32, (8, 128), 1)
    sub = lax.broadcasted_iota(jnp.int32, (8, 128), 0)

    def entry(n):
        result = []
        for x in total:
            out = None
            for c in range(COMPS):
                at = 8 * (n * COMPS + c)
                chunk = x[:, at // 128 * 128 : at // 128 * 128 + 128]
                moved = pltpu.roll(chunk, (128 - at % 128 + c) % 128, 1)
                out = moved if out is None else jnp.where(lane == c, moved, out)
            result.append(out)
        return tuple(result)

    entries = {pair: entry(n) for n, pair in enumerate(PAIRS)}
    gram = []
    for i in range(BASIS):
        row = None
        for j in range(BASIS):
            item = entries[(min(i, j), max(i, j))]
            if row is None:
                row = item
            else:
                row = tuple(jnp.where(sub == j, x, y) for x, y in zip(item, row))
        gram.append(row)
    zero = jnp.zeros((8, 128), F32)
    nothing = (zero, zero)
    one = (zero + 1.0, zero)

    def stack(poly):
        out = (zero, zero)
        for j, item in enumerate(poly):
            out = tuple(jnp.where(sub == j, x, y) for x, y in zip(item, out))
        return out

    def over_sublanes(x):
        for shift in (4, 2, 1):
            x = dd_add(x, tuple(pltpu.roll(y, shift, 0) for y in x))
        return x

    def gram_times(poly):
        out = None
        for i, item in enumerate(poly):
            term = dd_mul(item, gram[i])
            out = term if out is None else dd_add(out, term)
        return tuple(jnp.where(sub < BASIS, x, 0.0) for x in out)

    def operate(poly):
        out = list(poly) + [nothing]
        return [out[0]] + [dd_sub(out[i], out[i - 1]) for i in range(1, len(out))]

    def combine(first, factor, second):
        out = []
        for i in range(max(len(first), len(second))):
            item = first[i] if i < len(first) else nothing
            if i < len(second):
                item = dd_add(item, dd_mul(factor, second[i]))
            out.append(item)
        return out

    shadow = tuple(jnp.where(sub < BASIS, x, 0.0) for x in gram[0])

    residual = [one]
    direction = [one]
    answer = []
    rho = entries[(0, 0)]
    for iteration in range(ITERS):
        image = operate(direction)
        alpha = dd_div(rho, over_sublanes(dd_mul(shadow, stack(image))))
        middle = combine(residual, dd_neg(alpha), image)
        turned = operate(middle)
        weighted = gram_times(turned)
        cross = over_sublanes(dd_mul(weighted, stack(middle)))
        square = over_sublanes(dd_mul(weighted, stack(turned)))
        omega = dd_div(cross, square)
        answer = combine(answer, alpha, direction)
        answer = combine(answer, omega, middle)
        residual = combine(middle, dd_neg(omega), turned)
        if iteration + 1 < ITERS:
            rho_next = over_sublanes(dd_mul(shadow, stack(residual)))
            factor = dd_mul(dd_div(rho_next, rho), dd_div(alpha, omega))
            direction = combine(direction, dd_neg(omega), image)
            direction = combine(residual, factor, direction)
            rho = rho_next
    for c in range(COMPS):
        answer_at = [item[0][:, c : c + 1] for item in answer]
        residual_at = [item[0][:, c : c + 1] for item in residual]
        for k in range(planes):
            for r in range(0, rows, 8):
                out = answer_at[0] * solved[0][c, k, r : r + 8, :]
                for i in range(1, DEPTH):
                    out = out + answer_at[i] * solved[i][c, k, r : r + 8, :]
                solution_out[c, k, r : r + 8, :] = out
                out = residual_at[0] * values[0][c, k, r : r + 8, :]
                for i in range(1, BASIS):
                    out = out + residual_at[i] * values[i][c, k, r : r + 8, :]
                residual_out[c, k, r : r + 8, :] = out


def ring(array, axis, step):
    count = lax.axis_size(axis)
    return lax.ppermute(array, axis, [(i, (i + step) % count) for i in range(count)])


def local(velocity_old, courant, cell_ids, forces, weights):
    planes, rows, width = velocity_old.shape[1:]
    slabs, copies = lax.axis_size("slab"), lax.axis_size("batch")
    everyone = ("slab", "batch")
    wide = rows + 2 * DEPTH
    height = rows * copies
    assert rows % 8 == 0 and width == 128 and planes * height <= 256 and DEPTH * 2 <= height - rows
    slots = -(-len(PAIRS) * COMPS // 16) * 16
    place = jnp.stack([lax.axis_index("slab"), lax.axis_index("batch")]).astype(jnp.int32)

    momentum = (weights[None, :] * forces).astype(jnp.bfloat16)
    message = make_message(cell_ids, momentum, slabs, copies, width)
    fields = jnp.concatenate([velocity_old, courant], axis=0)
    after = ring(fields[:, :, :DEPTH], "batch", -1)
    before = ring(fields[:, :, rows - DEPTH :], "batch", 1)
    halo = jnp.concatenate([after, before], axis=2)
    received = lax.all_to_all(message, everyone, 0, 0, tiled=True)

    field = jax.ShapeDtypeStruct((COMPS, planes, wide, width), F32)
    face = jax.ShapeDtypeStruct((COMPS, wide, width), F32)
    side_shape = jax.ShapeDtypeStruct((4, planes, wide, width), F32)
    block_shape = jax.ShapeDtypeStruct((4, planes, wide, width), F32)
    group = 8

    def setup(*refs):
        setup_kernel(slabs, copies, group, *refs)

    value, solved, first, last, side, block = pl.pallas_call(
        setup,
        out_shape=(field, field, face, face, side_shape, block_shape),
        in_specs=[SMEM] + [VMEM] * 5,
        out_specs=[VMEM] * 6,
        scratch_shapes=[pltpu.VMEM((planes * wide, COMPS * width), F32)],
        name="setup",
    )(place, received, velocity_old, halo[:COMPS], courant, halo[COMPS:])

    values, solves = [value], [solved]
    for step in range(1, DEPTH + 1):
        below = ring(last, "slab", 1)
        above = ring(first, "slab", -1)
        if step < DEPTH:
            value, solved, first, last = pl.pallas_call(
                apply_kernel,
                out_shape=(field, field, face, face),
                in_specs=[VMEM] * 5,
                out_specs=[VMEM] * 4,
                name="apply",
            )(solved, below, above, side, block)
            solves.append(solved)
        else:

            def gram(*refs):
                gram_kernel(slots, *refs)

            value, message = pl.pallas_call(
                gram,
                out_shape=(
                    field,
                    jax.ShapeDtypeStruct((slabs * copies, 2 * slots * 8), F32),
                ),
                in_specs=[VMEM] * (5 + DEPTH),
                out_specs=[VMEM] * 2,
                name="gram",
            )(solved, below, above, side, block, *values)
        values.append(value)
    gathered = lax.all_to_all(message, everyone, 0, 0, tiled=True)

    def finish(*refs):
        finish_kernel(slots, *refs)

    own = jax.ShapeDtypeStruct(velocity_old.shape, F32)
    return pl.pallas_call(
        finish,
        out_shape=(own, own),
        in_specs=[VMEM] * (1 + BASIS + DEPTH),
        out_specs=[VMEM] * 2,
        name="finish",
    )(gathered, *values, *solves)


def solution(mesh):
    placed = (
        P(None, "slab", "batch", None),
        P(None, "slab", "batch", None),
        P(("slab", "batch")),
        P(None, ("slab", "batch")),
        P(("slab", "batch")),
    )
    return jax.shard_map(
        local,
        mesh=mesh,
        in_specs=placed,
        out_specs=(P(None, "slab", "batch", None), P(None, "slab", "batch", None)),
        check_vma=False,
    )
```

time: 287 us -> 76.7 us (0.27)
  blocking collectives: 171 us -> 12.7 us
  waiting for transfers between devices: 48.5 us -> 12.1 us
  starting transfers between devices: 45.1 us -> 28 us
  between operations: 14.5 us -> 0.72 us
  Pallas kernels: 0 us -> 13.5 us
  local copies, waits for them, and re-layouts: 2.16 us -> 6.29 us
    psum x4 -> x0, blocking collectives: 171 us -> none  [the longest x2 85.6 us: local(): closing_sums = lax.psum(jnp.stack(term_list, axis=0), ('slab', 'batch'))]
    reduce_scatter x1 -> x0, waiting for transfers between devices: 17.2 us -> none  [local(): lax.psum_scatter(deposit_rows(ids_here, moved_momentum, block_rows * lax....]
    ppermute x16 -> x10, starting transfers between devices: 34.4 us -> 20.7 us  [ring(): lax.ppermute(array, axis, [(i, (i + step) % count) for i in range(count)])]
    pallas_call x0 -> x6, Pallas kernels: none -> 13.5 us  [the longest x3 5.47 us: local(): pl.pallas_call(apply_kernel, out_shape=(field, field, face, face), in_spe...]
    all_to_all x0 -> x1, blocking collectives: none -> 12.7 us  [local(): gathered = lax.all_to_all(message, everyone, 0, 0, tiled=True)]
    ppermute x16 -> x10, waiting for transfers between devices: 20.1 us -> 9.51 us  [ring(): lax.ppermute(array, axis, [(i, (i + step) % count) for i in range(count)])]
    all_to_all x2 -> x1, waiting for transfers between devices: 11.3 us -> 2.61 us  [local(): received = lax.all_to_all(message, everyone, 0, 0, tiled=True)]
    all_to_all x2 -> x1, starting transfers between devices: 10.7 us -> 7.33 us  [local(): received = lax.all_to_all(message, everyone, 0, 0, tiled=True)]
  transfers between devices with their start and end apart: 19 -> 11, of which waited for: 11 -> 6; matrix products, arithmetic and copies ran while one was open for 1% -> 2% of each run, Pallas kernels for 0% -> 0%
where the time goes in v1:
time: 76.7 us; the launch traced here: 76.1 us
  starting transfers between devices  28 us (37%)
  Pallas kernels  13.5 us (18%)
  blocking collectives  12.7 us (17%)
  waiting for transfers between devices  12.1 us (16%)
  local copies, waits for them, and re-layouts  6.29 us (8%)
  other arithmetic  2.72 us (4%)
    ppermute x10, starting transfers between devices, ring(): lax.ppermute(array, axis, [(i, (i + step) % count) for i in range(count)])  20.7 us
    all_to_all x1, blocking collectives, local(): gathered = lax.all_to_all(message, everyone, 0, 0, tiled=True)  12.7 us
    ppermute x10, waiting for transfers between devices, ring(): lax.ppermute(array, axis, [(i, (i + step) % count) for i in range(count)])  9.51 us
    all_to_all x1, starting transfers between devices, local(): received = lax.all_to_all(message, everyone, 0, 0, tiled=True)  7.33 us
    pallas_call x3, Pallas kernels, local(): pl.pallas_call(apply_kernel, out_shape=(field, field, face, face), in_spe...  5.47 us
    unnamed x27, local copies, waits for them, and re-layouts  4.56 us
    pallas_call x1, Pallas kernels, local(): pl.pallas_call(gram, out_shape=(field, jax.ShapeDtypeStruct((slabs * copi...  2.69 us
    pallas_call x1, Pallas kernels, local(): pl.pallas_call(finish, out_shape=(own, own), in_specs=[VMEM] * (1 + BASIS...  2.68 us
  transfers between devices with their start and end apart: 11, of which 6 were waited for; matrix products, arithmetic and copies ran while one was open for 2% of the time, Pallas kernels for 0%

profile of v1, /device:TPU:0, one launch (start us, length us, event | category | flops | bytes accessed | tf_op | source)
XLA Modules:
  0.0 76.1 jit_solution(1548684966730044273)
XLA Ops:
  0.6 0.7 fusion.7
  1.3 0.7 fusion.1
  2.3 0.6 broadcast_in_dim.5
  2.9 7.3 %all-to-all-start = ((bf16[32,8,128]{2,1,0:T(8,128)(2,1)}), bf16[32,8,128]{2,1,0:T(8,128)(2,1)S(1)}, u32[]{:S(2)}, u32[]{:S(2)}) async-start(bf16[32,8,128]{2,1,0:T(8,128)(2,1)} %bitcast.5), calls=%async_computation | async-start | bytes 131072 | tf_op jit(solution)/shard_map/all_to_all | solution.py:413
  10.3 0.8 %copy-done.2 = f32[3,2,16,128]{3,2,1,0:T(8,128)S(1)} copy-done((f32[3,2,16,128]{3,2,1,0:T(8,128)S(1)}, f32[3,2,16,128]{3,2,1,0:T(8,128)}, u32[]{:S(2)}) %copy-start.2) | copy-done | bytes 49176
  11.4 1.5 %collective-permute-start = (f32[6,2,4,128]{3,2,1,0:T(4,128)S(1)}, f32[6,2,4,128]{3,2,1,0:T(4,128)S(1)}, u32[]{:S(2)}, u32[]{:S(2)}) collective-permute-start(f32[6,2,4,128]{3,2,1,0:T(4,128)S(1)} %get-tuple-element.43), channel_id=1, source_target_pairs={{0,3},{1,0},{2,1},{3,2},{4,7},{5,4},{6,5},{7,6},{8,11},{9,8},{10,9... | collective-permute-start | bytes 73736 | tf_op jit(solution)/shard_map/ppermute | solution.py:394
  13.4 1.0 %collective-permute-done.1 = f32[6,2,4,128]{3,2,1,0:T(4,128)S(1)} collective-permute-done((f32[6,2,4,128]{3,2,1,0:T(4,128)S(1)}, f32[6,2,4,128]{3,2,1,0:T(4,128)S(1)}, u32[]{:S(2)}, u32[]{:S(2)}) %collective-permute-start.1) | collective-permute-done | bytes 24608 | tf_op jit(solution)/shard_map/ppermute | solution.py:394
  14.4 0.6 pad_maximum_fusion
  15.0 2.6 %all-to-all-done.refs_1_ = bf16[32,8,128]{2,1,0:T(8,128)(2,1)S(1)} async-done(((bf16[32,8,128]{2,1,0:T(8,128)(2,1)}), bf16[32,8,128]{2,1,0:T(8,128)(2,1)S(1)}, u32[]{:S(2)}, u32[]{:S(2)}) %all-to-all-start) | async-done | bytes 65568 | tf_op jit(solution)/shard_map/all_to_all | solution.py:413
  17.6 0.6 copy-done
  18.3 2.7 %setup.1 = (f32[3,2,24,128]{3,2,1,0:T(8,128)}, f32[3,2,24,128]{3,2,1,0:T(8,128)}, f32[3,24,128]{2,1,0:T(8,128)}, f32[3,24,128]{2,1,0:T(8,128)}, f32[4,2,24,128]{3,2,1,0:T(8,128)}, /*index=5*/f32[4,2,24,128]{3,2,1,0:T(8,128)}) custom-call(s32[2]{0:T(128)} %pad_add_fusion.refs_0_, bf16[32,8,128]{2,1,0:T(8,128)(2,1)} %copy-done, f32[3,2,16,128]{3,2,1,0:T(8,128)} %refs_2_.1, ...), custom_call_target="tpu_custom_call" | custom-call | tf_op jit(solution)/shard_map/setup/pallas_call | solution.py:424
  20.9 0.6 collective-permute-start.2
  21.5 4.1 %collective-permute-start.3 = (f32[3,24,128]{2,1,0:T(8,128)}, f32[3,24,128]{2,1,0:T(8,128)S(1)}, u32[]{:S(2)}, u32[]{:S(2)}) collective-permute-start(f32[3,24,128]{2,1,0:T(8,128)} %get-tuple-element.24), channel_id=1, source_target_pairs={{0,28},{4,0},{8,4},{12,8},{16,12},{20,16},{24,20},{28,24},{1,29},{... | collective-permute-start | bytes 110600 | tf_op jit(solution)/shard_map/ppermute | solution.py:394
  25.6 2.1 %collective-permute-done.2.below = f32[3,24,128]{2,1,0:T(8,128)S(1)} collective-permute-done((f32[3,24,128]{2,1,0:T(8,128)}, f32[3,24,128]{2,1,0:T(8,128)S(1)}, u32[]{:S(2)}, u32[]{:S(2)}) %collective-permute-start.2) | collective-permute-done | bytes 36896 | tf_op jit(solution)/shard_map/ppermute | solution.py:394
  27.8 0.6 copy-done.5
  28.4 1.8 %apply.3 = (f32[3,2,24,128]{3,2,1,0:T(8,128)}, f32[3,2,24,128]{3,2,1,0:T(8,128)}, f32[3,24,128]{2,1,0:T(8,128)}, f32[3,24,128]{2,1,0:T(8,128)}) custom-call(f32[3,2,24,128]{3,2,1,0:T(8,128)} %get-tuple-element.22.solved.refs_6_, f32[3,24,128]{2,1,0:T(8,128)} %copy-done.5, f32[3,24,128]{2,1,0:T(8,128)} %copy-done.8, ...), custom_call_target="tpu_custom_call" | custom-call | tf_op jit(solution)/shard_map/apply/pallas_call | solution.py:438
  30.5 4.5 %collective-permute-start.5 = (f32[3,24,128]{2,1,0:T(8,128)}, f32[3,24,128]{2,1,0:T(8,128)S(1)}, u32[]{:S(2)}, u32[]{:S(2)}) collective-permute-start(f32[3,24,128]{2,1,0:T(8,128)} %get-tuple-element.29), channel_id=1, source_target_pairs={{0,28},{4,0},{8,4},{12,8},{16,12},{20,16},{24,20},{28,24},{1,29},{... | collective-permute-start | bytes 110600 | tf_op jit(solution)/shard_map/ppermute | solution.py:394
  35.0 2.1 %collective-permute-done.4.below = f32[3,24,128]{2,1,0:T(8,128)S(1)} collective-permute-done((f32[3,24,128]{2,1,0:T(8,128)}, f32[3,24,128]{2,1,0:T(8,128)S(1)}, u32[]{:S(2)}, u32[]{:S(2)}) %collective-permute-start.4) | collective-permute-done | bytes 36896 | tf_op jit(solution)/shard_map/ppermute | solution.py:394
  37.1 0.6 copy-done.6
  37.7 1.8 %apply.4 = (f32[3,2,24,128]{3,2,1,0:T(8,128)}, f32[3,2,24,128]{3,2,1,0:T(8,128)}, f32[3,24,128]{2,1,0:T(8,128)}, f32[3,24,128]{2,1,0:T(8,128)}) custom-call(f32[3,2,24,128]{3,2,1,0:T(8,128)} %get-tuple-element.27.solved.refs_7_, f32[3,24,128]{2,1,0:T(8,128)} %copy-done.6, f32[3,24,128]{2,1,0:T(8,128)} %copy-done.9, ...), custom_call_target="tpu_custom_call" | custom-call | tf_op jit(solution)/shard_map/apply/pallas_call | solution.py:438
  39.6 4.7 %collective-permute-start.7 = (f32[3,24,128]{2,1,0:T(8,128)}, f32[3,24,128]{2,1,0:T(8,128)S(1)}, u32[]{:S(2)}, u32[]{:S(2)}) collective-permute-start(f32[3,24,128]{2,1,0:T(8,128)} %get-tuple-element.32), channel_id=1, source_target_pairs={{0,28},{4,0},{8,4},{12,8},{16,12},{20,16},{24,20},{28,24},{1,29},{... | collective-permute-start | bytes 110600 | tf_op jit(solution)/shard_map/ppermute | solution.py:394
  44.3 2.1 %collective-permute-done.6.below = f32[3,24,128]{2,1,0:T(8,128)S(1)} collective-permute-done((f32[3,24,128]{2,1,0:T(8,128)}, f32[3,24,128]{2,1,0:T(8,128)S(1)}, u32[]{:S(2)}, u32[]{:S(2)}) %collective-permute-start.6) | collective-permute-done | bytes 36896 | tf_op jit(solution)/shard_map/ppermute | solution.py:394
  46.4 0.6 copy-done.7
  47.1 1.8 %apply.5 = (f32[3,2,24,128]{3,2,1,0:T(8,128)}, f32[3,2,24,128]{3,2,1,0:T(8,128)}, f32[3,24,128]{2,1,0:T(8,128)}, f32[3,24,128]{2,1,0:T(8,128)}) custom-call(f32[3,2,24,128]{3,2,1,0:T(8,128)} %get-tuple-element.30.solved.refs_8_, f32[3,24,128]{2,1,0:T(8,128)} %copy-done.7, f32[3,24,128]{2,1,0:T(8,128)} %copy-done.10, ...), custom_call_target="tpu_custom_call" | custom-call | tf_op jit(solution)/shard_map/apply/pallas_call | solution.py:438
  48.9 4.7 %collective-permute-start.9 = (f32[3,24,128]{2,1,0:T(8,128)}, f32[3,24,128]{2,1,0:T(8,128)S(1)}, u32[]{:S(2)}, u32[]{:S(2)}) collective-permute-start(f32[3,24,128]{2,1,0:T(8,128)} %get-tuple-element.35), channel_id=1, source_target_pairs={{0,28},{4,0},{8,4},{12,8},{16,12},{20,16},{24,20},{28,24},{1,29},{... | collective-permute-start | bytes 110600 | tf_op jit(solution)/shard_map/ppermute | solution.py:394
  53.6 2.1 %collective-permute-done.8.refs_1_ = f32[3,24,128]{2,1,0:T(8,128)S(1)} collective-permute-done((f32[3,24,128]{2,1,0:T(8,128)}, f32[3,24,128]{2,1,0:T(8,128)S(1)}, u32[]{:S(2)}, u32[]{:S(2)}) %collective-permute-start.8) | collective-permute-done | bytes 36896 | tf_op jit(solution)/shard_map/ppermute | solution.py:394
  55.8 0.6 copy-done.3
  56.4 2.7 %gram.1 = (f32[3,2,24,128]{3,2,1,0:T(8,128)}, f32[32,768]{1,0:T(8,128)}) custom-call(f32[3,2,24,128]{3,2,1,0:T(8,128)} %get-tuple-element.33.refs_0_.refs_9_, f32[3,24,128]{2,1,0:T(8,128)} %copy-done.3, f32[3,24,128]{2,1,0:T(8,128)} %copy-done.4, f32[4,2,24,128]{3,2,1,0:T(8,128)} %get-tuple-element.25.side.refs_3_, ...), custom_call_target="tpu_custom_call" | custom-call | tf_op jit(solution)/shard_map/gram/pallas_call | solution.py:451
  59.1 1.0 %copy.9 = f32[32,1,768]{2,1,0:T(1,128)S(1)} copy(f32[32,1,768]{2,0,1:T(8,128)} %bitcast.19) | data formatting | bytes 196608 | tf_op jit(solution)/shard_map/all_to_all | solution.py:462
  60.1 12.7 %all_to_all.16 = f32[32,1,768]{2,1,0:T(1,128)S(1)} all-to-all(f32[32,1,768]{2,1,0:T(1,128)S(1)} %copy.9), channel_id=1, replica_groups=mesh['slab'=8,'batch'=4] {'slab','batch'}, dimensions={0} | all-to-all | bytes 196608 | tf_op jit(solution)/shard_map/all_to_all | solution.py:462
  72.7 0.6 copy.14
  73.4 2.7 %finish.1 = (f32[3,2,16,128]{3,2,1,0:T(8,128)}, f32[3,2,16,128]{3,2,1,0:T(8,128)}) custom-call(f32[32,768]{1,0:T(8,128)} %bitcast.18, f32[3,2,24,128]{3,2,1,0:T(8,128)} %get-tuple-element.36.refs_5_.refs_1_, f32[3,2,24,128]{3,2,1,0:T(8,128)} %get-tuple-element.37.refs_6_.refs_2_, f32[3,2,24,128]{3,2,1,0:T(8,128)} %get-tuple-element.38.refs_7_.refs_3_, ...), custom_call_target="tpu_custom_call" | custom-call | tf_op jit(solution)/shard_map/finish/pallas_call | solution.py:468
  (36 shorter events, 1.4 us)
Async XLA Ops:
  0.6 0.7 copy-start.11
  2.9 7.3 %copy-start.1 = (f32[3,2,16,128]{3,2,1,0:T(8,128)S(1)}, f32[3,2,16,128]{3,2,1,0:T(8,128)}, u32[]{:S(2)}) copy-start(f32[3,2,16,128]{3,2,1,0:T(8,128)} %refs_2_.1) | copy-start | bytes 147460
  2.9 14.7 %all-to-all-start = ((bf16[32,8,128]{2,1,0:T(8,128)(2,1)}), bf16[32,8,128]{2,1,0:T(8,128)(2,1)S(1)}, u32[]{:S(2)}, u32[]{:S(2)}) async-start(bf16[32,8,128]{2,1,0:T(8,128)(2,1)} %bitcast.5), calls=%async_computation | async-start | bytes 131072 | tf_op jit(solution)/shard_map/all_to_all | solution.py:413
  10.2 0.8 %copy-start.2 = (f32[3,2,16,128]{3,2,1,0:T(8,128)S(1)}, f32[3,2,16,128]{3,2,1,0:T(8,128)}, u32[]{:S(2)}) copy-start(f32[3,2,16,128]{3,2,1,0:T(8,128)} %refs_4_.1) | copy-start | bytes 147460
  11.1 3.3 %collective-permute-start.1 = (f32[6,2,4,128]{3,2,1,0:T(4,128)S(1)}, f32[6,2,4,128]{3,2,1,0:T(4,128)S(1)}, u32[]{:S(2)}, u32[]{:S(2)}) collective-permute-start(f32[6,2,4,128]{3,2,1,0:T(4,128)S(1)} %get-tuple-element.42), channel_id=1, source_target_pairs={{0,1},{1,2},{2,3},{3,0},{4,5},{5,6},{6,7},{7,4},{8,9},{9,10},{10,1... | collective-permute-start | bytes 73736 | tf_op jit(solution)/shard_map/ppermute | solution.py:394
  11.4 3.0 %collective-permute-start = (f32[6,2,4,128]{3,2,1,0:T(4,128)S(1)}, f32[6,2,4,128]{3,2,1,0:T(4,128)S(1)}, u32[]{:S(2)}, u32[]{:S(2)}) collective-permute-start(f32[6,2,4,128]{3,2,1,0:T(4,128)S(1)} %get-tuple-element.43), channel_id=1, source_target_pairs={{0,3},{1,0},{2,1},{3,2},{4,7},{5,4},{6,5},{7,6},{8,11},{9,8},{10,9... | collective-permute-start | bytes 73736 | tf_op jit(solution)/shard_map/ppermute | solution.py:394
  17.6 0.6 copy-start
  20.9 6.9 %collective-permute-start.2 = (f32[3,24,128]{2,1,0:T(8,128)}, f32[3,24,128]{2,1,0:T(8,128)S(1)}, u32[]{:S(2)}, u32[]{:S(2)}) collective-permute-start(f32[3,24,128]{2,1,0:T(8,128)} %get-tuple-element.23), channel_id=1, source_target_pairs={{0,4},{4,8},{8,12},{12,16},{16,20},{20,24},{24,28},{28,0},{1,5},{5... | collective-permute-start | bytes 110600 | tf_op jit(solution)/shard_map/ppermute | solution.py:394
  21.5 6.3 %collective-permute-start.3 = (f32[3,24,128]{2,1,0:T(8,128)}, f32[3,24,128]{2,1,0:T(8,128)S(1)}, u32[]{:S(2)}, u32[]{:S(2)}) collective-permute-start(f32[3,24,128]{2,1,0:T(8,128)} %get-tuple-element.24), channel_id=1, source_target_pairs={{0,28},{4,0},{8,4},{12,8},{16,12},{20,16},{24,20},{28,24},{1,29},{... | collective-permute-start | bytes 110600 | tf_op jit(solution)/shard_map/ppermute | solution.py:394
  27.8 0.6 copy-start.5
  27.8 0.6 copy-start.8
  30.2 6.9 %collective-permute-start.4 = (f32[3,24,128]{2,1,0:T(8,128)}, f32[3,24,128]{2,1,0:T(8,128)S(1)}, u32[]{:S(2)}, u32[]{:S(2)}) collective-permute-start(f32[3,24,128]{2,1,0:T(8,128)} %get-tuple-element.28), channel_id=1, source_target_pairs={{0,4},{4,8},{8,12},{12,16},{16,20},{20,24},{24,28},{28,0},{1,5},{5... | collective-permute-start | bytes 110600 | tf_op jit(solution)/shard_map/ppermute | solution.py:394
  30.5 6.6 %collective-permute-start.5 = (f32[3,24,128]{2,1,0:T(8,128)}, f32[3,24,128]{2,1,0:T(8,128)S(1)}, u32[]{:S(2)}, u32[]{:S(2)}) collective-permute-start(f32[3,24,128]{2,1,0:T(8,128)} %get-tuple-element.29), channel_id=1, source_target_pairs={{0,28},{4,0},{8,4},{12,8},{16,12},{20,16},{24,20},{28,24},{1,29},{... | collective-permute-start | bytes 110600 | tf_op jit(solution)/shard_map/ppermute | solution.py:394
  37.1 0.6 copy-start.6
  37.1 0.6 copy-start.9
  39.6 6.9 %collective-permute-start.6 = (f32[3,24,128]{2,1,0:T(8,128)}, f32[3,24,128]{2,1,0:T(8,128)S(1)}, u32[]{:S(2)}, u32[]{:S(2)}) collective-permute-start(f32[3,24,128]{2,1,0:T(8,128)} %get-tuple-element.31), channel_id=1, source_target_pairs={{0,4},{4,8},{8,12},{12,16},{16,20},{20,24},{24,28},{28,0},{1,5},{5... | collective-permute-start | bytes 110600 | tf_op jit(solution)/shard_map/ppermute | solution.py:394
  39.6 6.9 %collective-permute-start.7 = (f32[3,24,128]{2,1,0:T(8,128)}, f32[3,24,128]{2,1,0:T(8,128)S(1)}, u32[]{:S(2)}, u32[]{:S(2)}) collective-permute-start(f32[3,24,128]{2,1,0:T(8,128)} %get-tuple-element.32), channel_id=1, source_target_pairs={{0,28},{4,0},{8,4},{12,8},{16,12},{20,16},{24,20},{28,24},{1,29},{... | collective-permute-start | bytes 110600 | tf_op jit(solution)/shard_map/ppermute | solution.py:394
  46.4 0.6 copy-start.7
  46.4 0.6 copy-start.10
  48.9 6.9 %collective-permute-start.8 = (f32[3,24,128]{2,1,0:T(8,128)}, f32[3,24,128]{2,1,0:T(8,128)S(1)}, u32[]{:S(2)}, u32[]{:S(2)}) collective-permute-start(f32[3,24,128]{2,1,0:T(8,128)} %get-tuple-element.34), channel_id=1, source_target_pairs={{0,4},{4,8},{8,12},{12,16},{16,20},{20,24},{24,28},{28,0},{1,5},{5... | collective-permute-start | bytes 110600 | tf_op jit(solution)/shard_map/ppermute | solution.py:394
  48.9 6.9 %collective-permute-start.9 = (f32[3,24,128]{2,1,0:T(8,128)}, f32[3,24,128]{2,1,0:T(8,128)S(1)}, u32[]{:S(2)}, u32[]{:S(2)}) collective-permute-start(f32[3,24,128]{2,1,0:T(8,128)} %get-tuple-element.35), channel_id=1, source_target_pairs={{0,28},{4,0},{8,4},{12,8},{16,12},{20,16},{24,20},{28,24},{1,29},{... | collective-permute-start | bytes 110600 | tf_op jit(solution)/shard_map/ppermute | solution.py:394
  55.7 0.6 copy-start.3
  55.8 0.6 copy-start.4

commit v2 on v1

--- a/solution.py
+++ b/solution.py
@@ -5,6 +5,7 @@
 from jax.experimental.pallas import tpu as pltpu
 from jax.sharding import PartitionSpec as P
 
+
 ITERS = 2
 DEPTH = 2 * ITERS
 COMPS = 3
@@ -15,7 +16,7 @@
 diagonal_value = 7.0
 
 VMEM = pl.BlockSpec(memory_space=pltpu.VMEM)
-SMEM = pl.BlockSpec(memory_space=pltpu.SMEM)
+ANY = pl.BlockSpec(memory_space=pl.ANY)
 F32 = jnp.float32
 
 
@@ -85,28 +86,47 @@
     return result
 
 
-def make_message(ids, momentum, slabs, copies, row_width):
-    tile = ids.shape[0] // slabs
-    high = (ids // row_width).astype(jnp.bfloat16)
-    low = (ids % row_width).astype(jnp.bfloat16)
-    rows = jnp.concatenate(
-        [momentum, high[None], low[None], jnp.zeros((3, ids.shape[0]), jnp.bfloat16)], axis=0
-    )
-    rows = rows.reshape(8, slabs, tile).transpose(1, 0, 2)
-    rows = jnp.broadcast_to(rows[:, None], (slabs, copies, 8, tile))
-    return rows.reshape(slabs * copies, 8, tile)
+def pack_kernel(slabs, copies, ids_in, forces_in, weights_in, message_out, ids, forces, weights, arrived):
+    moves = [
+        pltpu.make_async_copy(source, target, arrived.at[n])
+        for n, (source, target) in enumerate(
+            [(ids_in, ids), (weights_in, weights), (forces_in, forces)]
+        )
+    ]
+    for move in moves:
+        move.start()
+    for move in moves:
+        move.wait()
+    tile = ids.shape[1]
+    width = 128
+    high = ids[...] // width
+    low = ids[...] - high * width
+    rest = [high.astype(F32), low.astype(F32)]
+    rest += [jnp.zeros_like(rest[0])] * (8 - COMPS - len(rest))
+    for s in range(slabs):
+        at = slice(s * tile, (s + 1) * tile)
+        block = jnp.concatenate(
+            [forces[:, at] * weights[s : s + 1]] + [part[s : s + 1] for part in rest], axis=0
+        )
+        for k in range(copies):
+            message_out[s * copies + k] = block.astype(jnp.bfloat16)
+
+
+def edges_kernel(velocity, courant, first_out, last_out):
+    rows = velocity.shape[2]
+    for n, field in enumerate((velocity, courant)):
+        first_out[n * COMPS : (n + 1) * COMPS] = field[:, :, :DEPTH]
+        last_out[n * COMPS : (n + 1) * COMPS] = field[:, :, rows - DEPTH :]
 
 
 def setup_kernel(
-    slabs, copies, group,
-    place, message, velocity, velocity_halo, courant, courant_halo,
-    value_out, solved_out, first_out, last_out, side_out, block_out, momentum_sum,
+    copies, group,
+    message, old, block, value_out, solved_out, up_out, down_out, momentum_sum
 ):
-    planes, rows, width = velocity.shape[1:]
-    wide = rows + 2 * DEPTH
+    planes, wide, width = old.shape[1:]
+    rows = wide - 2 * DEPTH
     height = rows * copies
-    slab, batch = place[0], place[1]
-    start = batch * rows
+    start = lax.axis_index("batch") * rows
     tile = message.shape[2]
     row_iota = lax.broadcasted_iota(jnp.int32, (planes * wide, tile), 0)
     column_iota = lax.broadcasted_iota(jnp.int32, (width, tile), 0)
@@ -154,13 +174,49 @@
 
         lax.fori_loop(0, steps, one, 0)
 
+    inverses, ratios, lower_planes = block_planes(block)
+    even = lax.axis_index("batch") % 2 == 0
+    for c in range(COMPS):
+        values = []
+        for k in range(planes):
+            deposit_part = momentum_sum[k * wide : (k + 1) * wide, c * width : (c + 1) * width]
+            value = old[c, k] + deposit_part
+            value_out[c, k] = value
+            values.append(value)
+        finish_level(c, values, inverses, ratios, lower_planes, even, solved_out, up_out, down_out)
+
+
+def block_planes(block):
+    planes = block.shape[1]
+    return tuple([block[n, k] for k in range(planes)] for n in range(3))
+
+
+def finish_level(c, values, inverses, ratios, lower_planes, even, solved_out, up_out, down_out):
+    solved = solve_block(values, inverses, ratios, lower_planes)
+    for k, item in enumerate(solved):
+        solved_out[c, k] = item
+    up_out[c] = jnp.where(even, solved[-1], solved[0])
+    down_out[c] = jnp.where(even, solved[0], solved[-1])
+
+
+def prepare_kernel(
+    slabs, copies, velocity, courant, after, before, old_out, side_out, block_out
+):
+    planes, rows, width = velocity.shape[1:]
+    wide = rows + 2 * DEPTH
+    slab, batch = lax.axis_index("slab"), lax.axis_index("batch")
+    for c in range(COMPS):
+        for k in range(planes):
+            old_out[c, k] = jnp.concatenate([velocity[c, k], after[c, k], before[c, k]], axis=0)
     spots = lax.broadcasted_iota(jnp.int32, (wide, width), 0)
     lanes = lax.broadcasted_iota(jnp.int32, (wide, width), 1)
     lower_planes, upper_planes, inverses, ratios = [], [], [], []
     for k in range(planes):
         coefs = []
         for d in range(3):
-            half = 0.5 * jnp.concatenate([courant[d, k], courant_halo[d, k]], axis=0)
+            half = 0.5 * jnp.concatenate(
+                [courant[d, k], after[COMPS + d, k], before[COMPS + d, k]], axis=0
+            )
             coefs.append((diffusion_number - half, diffusion_number + half))
         upper_planes.append(coefs[0][0])
         lower_planes.append(coefs[0][1])
@@ -181,63 +237,48 @@
         block_out[2, k] = lower_planes[k]
     block_out[3, 0] = jnp.where(slab == 0, 0.0, lower_planes[0])
     block_out[3, 1] = jnp.where(slab == slabs - 1, 0.0, upper_planes[planes - 1])
+
+
+def couple(solved, one_way, other_way, side, block):
+    planes, wide, width = solved.shape[1:]
+    even = lax.axis_index("batch") % 2 == 0
+    result = []
     for c in range(COMPS):
         values = []
         for k in range(planes):
-            old = jnp.concatenate([velocity[c, k], velocity_halo[c, k]], axis=0)
-            value = old + momentum_sum[k * wide : (k + 1) * wide, c * width : (c + 1) * width]
-            value_out[c, k] = value
-            values.append(value)
-        solved = solve_block(values, inverses, ratios, lower_planes)
-        for k in range(planes):
-            solved_out[c, k] = solved[k]
-        first_out[c] = solved[0]
-        last_out[c] = solved[planes - 1]
-
-
-def couple(c, solved, below, above, side, block):
-    planes, wide = solved.shape[1:3]
-    width = solved.shape[3]
-    result = []
-    for k in range(planes):
-        here = solved[c, k]
-        total = side[0, k] * pltpu.roll(here, wide - 1, 0) + side[1, k] * pltpu.roll(here, 1, 0)
-        total = total + side[2, k] * pltpu.roll(here, width - 1, 1)
-        total = total + side[3, k] * pltpu.roll(here, 1, 1)
-        if k == 0:
-            total = total + block[3, 0] * below[c]
-        if k == planes - 1:
-            total = total + block[3, 1] * above[c]
-        result.append(total)
+            here = solved[c, k]
+            total = side[0, k] * pltpu.roll(here, wide - 1, 0)
+            total = total + side[1, k] * pltpu.roll(here, 1, 0)
+            total = total + side[2, k] * pltpu.roll(here, width - 1, 1)
+            total = total + side[3, k] * pltpu.roll(here, 1, 1)
+            if k == 0:
+                total = total + block[3, 0] * jnp.where(even, one_way[c], other_way[c])
+            if k == planes - 1:
+                total = total + block[3, 1] * jnp.where(even, other_way[c], one_way[c])
+            values.append(total)
+        result.append(values)
     return result
 
 
 def apply_kernel(
-    solved, below, above, side, block, value_out, solved_out, first_out, last_out
+    solved, one_way, other_way, side, block, value_out, solved_out, up_out, down_out
 ):
-    planes = solved.shape[1]
-    inverses = [block[0, k] for k in range(planes)]
-    ratios = [block[1, k] for k in range(planes)]
-    lower_planes = [block[2, k] for k in range(planes)]
-    for c in range(COMPS):
-        values = couple(c, solved, below, above, side, block)
-        result = solve_block(values, inverses, ratios, lower_planes)
-        for k in range(planes):
-            value_out[c, k] = values[k]
-            solved_out[c, k] = result[k]
-        first_out[c] = result[0]
-        last_out[c] = result[planes - 1]
-
-
-def gram_kernel(slots, *refs):
-    solved, below, above, side, block = refs[:5]
+    inverses, ratios, lower_planes = block_planes(block)
+    even = lax.axis_index("batch") % 2 == 0
+    for c, values in enumerate(couple(solved, one_way, other_way, side, block)):
+        for k, item in enumerate(values):
+            value_out[c, k] = item
+        finish_level(c, values, inverses, ratios, lower_planes, even, solved_out, up_out, down_out)
+
+
+def gram_kernel(*refs):
+    solved, one_way, other_way, side, block = refs[:5]
     values = refs[5 : 5 + DEPTH]
     value_out, message_out = refs[5 + DEPTH :]
     planes, wide, width = solved.shape[1:]
     rows = wide - 2 * DEPTH
     sums = []
-    for c in range(COMPS):
-        newest = couple(c, solved, below, above, side, block)
+    for c, newest in enumerate(couple(solved, one_way, other_way, side, block)):
         for k in range(planes):
             value_out[c, k] = newest[k]
         totals = [None] * len(PAIRS)
@@ -256,53 +297,57 @@
                         totals[n] = (s, totals[n][1] + (t + e))
         sums.append(totals)
     flat = [sums[c][n] for n in range(len(PAIRS)) for c in range(COMPS)]
-    columns = []
-    for part in range(2):
-        stacked = jnp.concatenate([x[part] for x in flat], axis=0)
-        padded = slots * 8 - stacked.shape[0]
-        if padded:
-            stacked = jnp.concatenate([stacked, jnp.zeros((padded, width), F32)], axis=0)
-        columns.append(jnp.transpose(stacked))
-    total = (columns[0][:8], columns[1][:8])
+    nothing = (jnp.zeros((8, width), F32),) * 2
+    flat += [nothing] * (width // 2 - len(flat))
+    rows_of = [sum_to_sublanes(flat[n : n + 8]) for n in range(0, len(flat), 8)]
+    turned = [jnp.transpose(jnp.concatenate([x[p] for x in rows_of], axis=0)) for p in (0, 1)]
+    total = tuple(x[:8] for x in turned)
     for r in range(8, width, 8):
-        total = dd_add(total, (columns[0][r : r + 8], columns[1][r : r + 8]))
+        total = dd_add(total, tuple(x[r : r + 8] for x in turned))
     for shift in (4, 2, 1):
         total = dd_add(total, tuple(pltpu.roll(x, shift, 0) for x in total))
-    size = slots * 8
+    row = jnp.concatenate([x[:1] for x in total], axis=1)
+    message_out[...] = jnp.broadcast_to(row, message_out.shape)
+
+
+def sum_to_sublanes(parts):
+    sub = lax.broadcasted_iota(jnp.int32, parts[0][0].shape, 0)
+    level = parts
     for shift in (4, 2, 1):
-        total = dd_add(total, tuple(pltpu.roll(x, size - shift, 1) for x in total))
-    row = jnp.concatenate([total[0][:1], total[1][:1]], axis=1)
-    message_out[...] = jnp.broadcast_to(row, message_out.shape)
-
-
-def finish_kernel(slots, *refs):
+        keep = (sub & shift) == 0
+        merged = []
+        for a, b in zip(level[:shift], level[shift:]):
+            stay = tuple(jnp.where(keep, x, y) for x, y in zip(a, b))
+            swap = [jnp.where(keep, y, x) for x, y in zip(a, b)]
+            moved = tuple(
+                pltpu.roll(w, 4, 0)
+                if shift == 4
+                else jnp.where(keep, pltpu.roll(w, 8 - shift, 0), pltpu.roll(w, shift, 0))
+                for w in swap
+            )
+            merged.append(dd_add(stay, moved))
+        level = merged
+    return level[0]
+
+
+def finish_kernel(*refs):
     gathered = refs[0]
     values = refs[1 : 1 + BASIS]
     solved = refs[1 + BASIS : 1 + BASIS + DEPTH]
     solution_out, residual_out = refs[1 + BASIS + DEPTH :]
-    planes, rows, width = solution_out.shape[1:]
-    size = slots * 8
-    count = gathered.shape[0]
-    high, low = gathered[:, :size], gathered[:, size:]
-    total = (high[:8], low[:8])
-    for r in range(8, count, 8):
-        total = dd_add(total, (high[r : r + 8], low[r : r + 8]))
+    planes, rows, _ = solution_out.shape[1:]
+    count, lanes = gathered.shape
+    total = None
+    for r in range(0, count, 8):
+        high = gathered[r : r + 8]
+        item = (high, pltpu.roll(high, lanes // 2, 1))
+        total = item if total is None else dd_add(total, item)
     for shift in (4, 2, 1):
         total = dd_add(total, tuple(pltpu.roll(x, shift, 0) for x in total))
-    lane = lax.broadcasted_iota(jnp.int32, (8, 128), 1)
-    sub = lax.broadcasted_iota(jnp.int32, (8, 128), 0)
+    sub = lax.broadcasted_iota(jnp.int32, (8, lanes), 0)
 
     def entry(n):
-        result = []
-        for x in total:
-            out = None
-            for c in range(COMPS):
-                at = 8 * (n * COMPS + c)
-                chunk = x[:, at // 128 * 128 : at // 128 * 128 + 128]
-                moved = pltpu.roll(chunk, (128 - at % 128 + c) % 128, 1)
-                out = moved if out is None else jnp.where(lane == c, moved, out)
-            result.append(out)
-        return tuple(result)
+        return tuple(pltpu.roll(x, (lanes - n * COMPS) % lanes, 1) for x in total)
 
     entries = {pair: entry(n) for n, pair in enumerate(PAIRS)}
     gram = []
@@ -315,7 +360,7 @@
             else:
                 row = tuple(jnp.where(sub == j, x, y) for x, y in zip(item, row))
         gram.append(row)
-    zero = jnp.zeros((8, 128), F32)
+    zero = jnp.zeros((8, lanes), F32)
     nothing = (zero, zero)
     one = (zero + 1.0, zero)
 
@@ -394,83 +439,101 @@
     return lax.ppermute(array, axis, [(i, (i + step) % count) for i in range(count)])
 
 
+def race(array, step):
+    slabs, copies = lax.axis_size("slab"), lax.axis_size("batch")
+    pairs = []
+    for s in range(slabs):
+        for b in range(copies):
+            t = s + 1 if b % 2 == 0 else s - 1
+            target = t * copies + b if 0 <= t < slabs else s * copies + (b ^ 1)
+            pairs.append((s * copies + b, target))
+    if step < 0:
+        pairs = [(t, s) for s, t in pairs]
+    return lax.ppermute(array, ("slab", "batch"), sorted(pairs))
+
+
 def local(velocity_old, courant, cell_ids, forces, weights):
     planes, rows, width = velocity_old.shape[1:]
     slabs, copies = lax.axis_size("slab"), lax.axis_size("batch")
     everyone = ("slab", "batch")
     wide = rows + 2 * DEPTH
     height = rows * copies
-    assert rows % 8 == 0 and width == 128 and planes * height <= 256 and DEPTH * 2 <= height - rows
-    slots = -(-len(PAIRS) * COMPS // 16) * 16
-    place = jnp.stack([lax.axis_index("slab"), lax.axis_index("batch")]).astype(jnp.int32)
-
-    momentum = (weights[None, :] * forces).astype(jnp.bfloat16)
-    message = make_message(cell_ids, momentum, slabs, copies, width)
-    fields = jnp.concatenate([velocity_old, courant], axis=0)
-    after = ring(fields[:, :, :DEPTH], "batch", -1)
-    before = ring(fields[:, :, rows - DEPTH :], "batch", 1)
-    halo = jnp.concatenate([after, before], axis=2)
-    received = lax.all_to_all(message, everyone, 0, 0, tiled=True)
-
+    tile = cell_ids.shape[0] // slabs
+    assert rows % 8 == 0 and width == 128 and copies % 2 == 0
+    assert planes * height <= 256 and 2 * DEPTH <= height - rows
     field = jax.ShapeDtypeStruct((COMPS, planes, wide, width), F32)
     face = jax.ShapeDtypeStruct((COMPS, wide, width), F32)
-    side_shape = jax.ShapeDtypeStruct((4, planes, wide, width), F32)
-    block_shape = jax.ShapeDtypeStruct((4, planes, wide, width), F32)
-    group = 8
+    quad = jax.ShapeDtypeStruct((4, planes, wide, width), F32)
+    edge = jax.ShapeDtypeStruct((2 * COMPS, planes, DEPTH, width), F32)
+    own = jax.ShapeDtypeStruct(velocity_old.shape, F32)
+
+    def call(kernel, out_shape, in_specs, mib, scratch=()):
+        return pl.pallas_call(
+            kernel,
+            out_shape=out_shape,
+            in_specs=in_specs,
+            out_specs=[VMEM] * len(out_shape),
+            scratch_shapes=list(scratch),
+            compiler_params=pltpu.CompilerParams(vmem_limit_bytes=mib << 20),
+        )
+
+    def pack(*refs):
+        pack_kernel(slabs, copies, *refs)
+
+    (message,) = call(
+        pack,
+        (jax.ShapeDtypeStruct((slabs * copies, 8, tile), jnp.bfloat16),),
+        [ANY] * 3,
+        60,
+        [
+            pltpu.VMEM((slabs, tile), jnp.int32),
+            pltpu.VMEM(forces.shape, F32),
+            pltpu.VMEM((slabs, tile), F32),
+            pltpu.SemaphoreType.DMA((3,)),
+        ],
+    )(cell_ids.reshape(slabs, tile), forces, weights.reshape(slabs, tile))
+    received = lax.all_to_all(message, everyone, 0, 0, tiled=True)
+    first, last = call(edges_kernel, (edge, edge), [VMEM] * 2, 2)(velocity_old, courant)
+    after = ring(first, "batch", -1)
+    before = ring(last, "batch", 1)
+
+    def prepare(*refs):
+        prepare_kernel(slabs, copies, *refs)
+
+    old, side, block = call(
+        prepare, (field, quad, quad), [VMEM] * 4, 4
+    )(velocity_old, courant, after, before)
 
     def setup(*refs):
-        setup_kernel(slabs, copies, group, *refs)
-
-    value, solved, first, last, side, block = pl.pallas_call(
+        setup_kernel(copies, 8, *refs)
+
+    value, solved, up, down = call(
         setup,
-        out_shape=(field, field, face, face, side_shape, block_shape),
-        in_specs=[SMEM] + [VMEM] * 5,
-        out_specs=[VMEM] * 6,
-        scratch_shapes=[pltpu.VMEM((planes * wide, COMPS * width), F32)],
-        name="setup",
-    )(place, received, velocity_old, halo[:COMPS], courant, halo[COMPS:])
+        (field, field, face, face),
+        [VMEM] * 3,
+        12,
+        [pltpu.VMEM((planes * wide, COMPS * width), F32)],
+    )(received, old, block)
 
     values, solves = [value], [solved]
     for step in range(1, DEPTH + 1):
-        below = ring(last, "slab", 1)
-        above = ring(first, "slab", -1)
+        known = (solved, race(up, 1), race(down, -1), side, block)
         if step < DEPTH:
-            value, solved, first, last = pl.pallas_call(
-                apply_kernel,
-                out_shape=(field, field, face, face),
-                in_specs=[VMEM] * 5,
-                out_specs=[VMEM] * 4,
-                name="apply",
-            )(solved, below, above, side, block)
+            value, solved, up, down = call(
+                apply_kernel, (field, field, face, face), [VMEM] * 5, 2
+            )(*known)
             solves.append(solved)
         else:
-
-            def gram(*refs):
-                gram_kernel(slots, *refs)
-
-            value, message = pl.pallas_call(
-                gram,
-                out_shape=(
-                    field,
-                    jax.ShapeDtypeStruct((slabs * copies, 2 * slots * 8), F32),
-                ),
-                in_specs=[VMEM] * (5 + DEPTH),
-                out_specs=[VMEM] * 2,
-                name="gram",
-            )(solved, below, above, side, block, *values)
+            value, message = call(
+                gram_kernel,
+                (field, jax.ShapeDtypeStruct((slabs * copies, width), F32)),
+                [VMEM] * (5 + DEPTH),
+                4,
+            )(*known, *values)
         values.append(value)
     gathered = lax.all_to_all(message, everyone, 0, 0, tiled=True)
-
-    def finish(*refs):
-        finish_kernel(slots, *refs)
-
-    own = jax.ShapeDtypeStruct(velocity_old.shape, F32)
-    return pl.pallas_call(
-        finish,
-        out_shape=(own, own),
-        in_specs=[VMEM] * (1 + BASIS + DEPTH),
-        out_specs=[VMEM] * 2,
-        name="finish",
+    return call(
+        finish_kernel, (own, own), [VMEM] * (1 + BASIS + DEPTH), 4
     )(gathered, *values, *solves)
 
 

time: 76.7 us -> 52.5 us (0.68)
  starting transfers between devices: 28 us -> 15.1 us
  waiting for transfers between devices: 12.1 us -> 21.6 us
  Pallas kernels: 13.5 us -> 5.17 us
  local copies, waits for them, and re-layouts: 6.29 us -> 0.01 us
  blocking collectives: 12.7 us -> 9.56 us
  other arithmetic: 2.72 us -> 0 us
    ppermute x10 -> x2, starting transfers between devices: 20.7 us -> 1.54 us  [ring(): lax.ppermute(array, axis, [(i, (i + step) % count) for i in range(count)])]
    ppermute x0 -> x8, waiting for transfers between devices: none -> 15.8 us  [race(): return lax.ppermute(array, ('slab', 'batch'), sorted(pairs))]
    pallas_call x6 -> x9, Pallas kernels: 13.5 us -> 5.17 us  [the longest x1 1.53 us: local(): call(finish_kernel, (own, own), [VMEM] * (1 + BASIS + DEPTH), 4)]
    ppermute x10 -> x2, waiting for transfers between devices: 9.51 us -> 3.29 us  [ring(): lax.ppermute(array, axis, [(i, (i + step) % count) for i in range(count)])]
    ppermute x0 -> x8, starting transfers between devices: none -> 6.19 us  [race(): return lax.ppermute(array, ('slab', 'batch'), sorted(pairs))]
    unnamed x27 -> x4, local copies, waits for them, and re-layouts: 4.56 us -> 0.01 us
    all_to_all x1, blocking collectives: 12.7 us -> 9.56 us  [local(): gathered = lax.all_to_all(message, everyone, 0, 0, tiled=True)]
    concatenate x2 -> x0, other arithmetic: 1.33 us -> none  [the longest x1 0.7 us: make_message(): jnp.concatenate([momentum, high[None], low[None], jnp.zeros((3, ids.shape...]
  transfers between devices with their start and end apart: 11 -> 11, of which waited for: 6 -> 11; matrix products, arithmetic and copies ran while one was open for 2% -> 0% of each run, Pallas kernels for 0% -> 0%
where the time goes in v2:
time: 52.5 us; the launch traced here: 52.2 us
  waiting for transfers between devices  21.6 us (41%)
  starting transfers between devices  15.1 us (29%)
  blocking collectives  9.56 us (18%)
  Pallas kernels  5.17 us (10%)
  between operations  0.73 us (1%)
    ppermute x8, waiting for transfers between devices, race(): return lax.ppermute(array, ('slab', 'batch'), sorted(pairs))  15.8 us
    all_to_all x1, blocking collectives, local(): gathered = lax.all_to_all(message, everyone, 0, 0, tiled=True)  9.56 us
    all_to_all x1, starting transfers between devices, local(): received = lax.all_to_all(message, everyone, 0, 0, tiled=True)  7.33 us
    ppermute x8, starting transfers between devices, race(): return lax.ppermute(array, ('slab', 'batch'), sorted(pairs))  6.19 us
    ppermute x2, waiting for transfers between devices, ring(): lax.ppermute(array, axis, [(i, (i + step) % count) for i in range(count)])  3.29 us
    all_to_all x1, waiting for transfers between devices, local(): received = lax.all_to_all(message, everyone, 0, 0, tiled=True)  2.5 us
    ppermute x2, starting transfers between devices, ring(): lax.ppermute(array, axis, [(i, (i + step) % count) for i in range(count)])  1.54 us
    pallas_call x1, Pallas kernels, local(): call(finish_kernel, (own, own), [VMEM] * (1 + BASIS + DEPTH), 4)  1.53 us
  transfers between devices with their start and end apart: 11, of which 11 were waited for; matrix products, arithmetic and copies ran while one was open for 0% of the time, Pallas kernels for 0%

profile of v2, /device:TPU:0, one launch (start us, length us, event | category | flops | bytes accessed | tf_op | source)
XLA Modules:
  0.0 52.2 jit_solution(15329873569822701527)
XLA Ops:
  0.6 1.4 %shard_map.68 = bf16[32,8,128]{2,1,0:T(8,128)(2,1)} custom-call(s32[8,128]{1,0:T(8,128)} %bitcast.8, f32[3,1024]{1,0:T(4,128)} %refs_1_.2, f32[8,128]{1,0:T(8,128)} %bitcast.9), custom_call_target="tpu_custom_call" | custom-call | tf_op jit(solution)/shard_map/pallas_call | solution.py:483
  2.0 0.0 copy-start
  2.1 0.0 copy-start.1
  2.1 7.3 %all-to-all-start = ((bf16[32,8,128]{2,1,0:T(8,128)(2,1)}), bf16[32,8,128]{2,1,0:T(8,128)(2,1)S(1)}, u32[]{:S(2)}, u32[]{:S(2)}) async-start(bf16[32,8,128]{2,1,0:T(8,128)(2,1)} %shard_map.68), calls=%async_computation | async-start | bytes 131072 | tf_op jit(solution)/shard_map/all_to_all | solution.py:495
  9.4 1.5 %collective-permute-start = (f32[6,2,4,128]{3,2,1,0:T(4,128)S(1)}, f32[6,2,4,128]{3,2,1,0:T(4,128)S(1)}, u32[]{:S(2)}, u32[]{:S(2)}) collective-permute-start(f32[6,2,4,128]{3,2,1,0:T(4,128)S(1)} %get-tuple-element.25), channel_id=1, source_target_pairs={{0,3},{1,0},{2,1},{3,2},{4,7},{5,4},{6,5},{7,6},{8,11},{9,8},{10,9... | collective-permute-start | bytes 73736 | tf_op jit(solution)/shard_map/ppermute | solution.py:439
  11.0 0.0 collective-permute-start.1
  11.0 1.5 %collective-permute-done.refs_2_ = f32[6,2,4,128]{3,2,1,0:T(4,128)S(1)} collective-permute-done((f32[6,2,4,128]{3,2,1,0:T(4,128)S(1)}, f32[6,2,4,128]{3,2,1,0:T(4,128)S(1)}, u32[]{:S(2)}, u32[]{:S(2)}) %collective-permute-start) | collective-permute-done | bytes 24608 | tf_op jit(solution)/shard_map/ppermute | solution.py:439
  12.5 1.7 %collective-permute-done.1.refs_3_ = f32[6,2,4,128]{3,2,1,0:T(4,128)S(1)} collective-permute-done((f32[6,2,4,128]{3,2,1,0:T(4,128)S(1)}, f32[6,2,4,128]{3,2,1,0:T(4,128)S(1)}, u32[]{:S(2)}, u32[]{:S(2)}) %collective-permute-start.1) | collective-permute-done | bytes 24608 | tf_op jit(solution)/shard_map/ppermute | solution.py:439
  14.3 2.5 %all-to-all-done.refs_0_ = bf16[32,8,128]{2,1,0:T(8,128)(2,1)S(1)} async-done(((bf16[32,8,128]{2,1,0:T(8,128)(2,1)}), bf16[32,8,128]{2,1,0:T(8,128)(2,1)S(1)}, u32[]{:S(2)}, u32[]{:S(2)}) %all-to-all-start) | async-done | bytes 65568 | tf_op jit(solution)/shard_map/all_to_all | solution.py:495
  16.8 1.1 %shard_map.71 = (f32[3,2,24,128]{3,2,1,0:T(8,128)S(1)}, f32[3,2,24,128]{3,2,1,0:T(8,128)S(1)}, f32[3,24,128]{2,1,0:T(8,128)S(1)}, f32[3,24,128]{2,1,0:T(8,128)S(1)}) custom-call(bf16[32,8,128]{2,1,0:T(8,128)(2,1)S(1)} %all-to-all-done.refs_0_, f32[3,2,24,128]{3,2,1,0:T(8,128)S(1)} %get-tuple-element.27.refs_1_, ...), custom_call_target="tpu_custom_call" | custom-call | tf_op jit(solution)/shard_map/pallas_call | solution.py:510
  17.9 0.7 %collective-permute-start.2 = (f32[3,24,128]{2,1,0:T(8,128)S(1)}, f32[3,24,128]{2,1,0:T(8,128)S(1)}, u32[]{:S(2)}, u32[]{:S(2)}) collective-permute-start(f32[3,24,128]{2,1,0:T(8,128)S(1)} %get-tuple-element.30), channel_id=1, source_target_pairs={{0,4},{1,0},{2,6},{3,2},{4,8},{5,1},{6,10},{7,3},{8,12},{9,5},{10,... | collective-permute-start | bytes 110600 | tf_op jit(solution)/shard_map/ppermute | solution.py:452
  18.5 0.0 collective-permute-start.3
  18.5 2.1 %collective-permute-done.2.one_way = f32[3,24,128]{2,1,0:T(8,128)S(1)} collective-permute-done((f32[3,24,128]{2,1,0:T(8,128)S(1)}, f32[3,24,128]{2,1,0:T(8,128)S(1)}, u32[]{:S(2)}, u32[]{:S(2)}) %collective-permute-start.2) | collective-permute-done | bytes 36896 | tf_op jit(solution)/shard_map/ppermute | solution.py:452
  20.6 1.9 %collective-permute-done.3.other_way = f32[3,24,128]{2,1,0:T(8,128)S(1)} collective-permute-done((f32[3,24,128]{2,1,0:T(8,128)S(1)}, f32[3,24,128]{2,1,0:T(8,128)S(1)}, u32[]{:S(2)}, u32[]{:S(2)}) %collective-permute-start.3) | collective-permute-done | bytes 36896 | tf_op jit(solution)/shard_map/ppermute | solution.py:452
  22.5 0.1 shard_map.72
  22.6 2.4 %collective-permute-start.4 = (f32[3,24,128]{2,1,0:T(8,128)S(1)}, f32[3,24,128]{2,1,0:T(8,128)S(1)}, u32[]{:S(2)}, u32[]{:S(2)}) collective-permute-start(f32[3,24,128]{2,1,0:T(8,128)S(1)} %get-tuple-element.34), channel_id=1, source_target_pairs={{0,4},{1,0},{2,6},{3,2},{4,8},{5,1},{6,10},{7,3},{8,12},{9,5},{10,... | collective-permute-start | bytes 110600 | tf_op jit(solution)/shard_map/ppermute | solution.py:452
  25.0 0.0 collective-permute-start.5
  25.0 1.6 %collective-permute-done.4.one_way = f32[3,24,128]{2,1,0:T(8,128)S(1)} collective-permute-done((f32[3,24,128]{2,1,0:T(8,128)S(1)}, f32[3,24,128]{2,1,0:T(8,128)S(1)}, u32[]{:S(2)}, u32[]{:S(2)}) %collective-permute-start.4) | collective-permute-done | bytes 36896 | tf_op jit(solution)/shard_map/ppermute | solution.py:452
  26.7 2.3 %collective-permute-done.5.other_way = f32[3,24,128]{2,1,0:T(8,128)S(1)} collective-permute-done((f32[3,24,128]{2,1,0:T(8,128)S(1)}, f32[3,24,128]{2,1,0:T(8,128)S(1)}, u32[]{:S(2)}, u32[]{:S(2)}) %collective-permute-start.5) | collective-permute-done | bytes 36896 | tf_op jit(solution)/shard_map/ppermute | solution.py:452
  29.0 0.1 shard_map.73
  29.1 1.2 %collective-permute-start.6 = (f32[3,24,128]{2,1,0:T(8,128)S(1)}, f32[3,24,128]{2,1,0:T(8,128)S(1)}, u32[]{:S(2)}, u32[]{:S(2)}) collective-permute-start(f32[3,24,128]{2,1,0:T(8,128)S(1)} %get-tuple-element.37), channel_id=1, source_target_pairs={{0,4},{1,0},{2,6},{3,2},{4,8},{5,1},{6,10},{7,3},{8,12},{9,5},{10,... | collective-permute-start | bytes 110600 | tf_op jit(solution)/shard_map/ppermute | solution.py:452
  30.3 0.0 collective-permute-start.7
  30.3 1.6 %collective-permute-done.6.one_way = f32[3,24,128]{2,1,0:T(8,128)S(1)} collective-permute-done((f32[3,24,128]{2,1,0:T(8,128)S(1)}, f32[3,24,128]{2,1,0:T(8,128)S(1)}, u32[]{:S(2)}, u32[]{:S(2)}) %collective-permute-start.6) | collective-permute-done | bytes 36896 | tf_op jit(solution)/shard_map/ppermute | solution.py:452
  32.0 2.3 %collective-permute-done.7.other_way = f32[3,24,128]{2,1,0:T(8,128)S(1)} collective-permute-done((f32[3,24,128]{2,1,0:T(8,128)S(1)}, f32[3,24,128]{2,1,0:T(8,128)S(1)}, u32[]{:S(2)}, u32[]{:S(2)}) %collective-permute-start.7) | collective-permute-done | bytes 36896 | tf_op jit(solution)/shard_map/ppermute | solution.py:452
  34.3 0.1 shard_map.74
  34.4 1.9 %collective-permute-start.8 = (f32[3,24,128]{2,1,0:T(8,128)S(1)}, f32[3,24,128]{2,1,0:T(8,128)S(1)}, u32[]{:S(2)}, u32[]{:S(2)}) collective-permute-start(f32[3,24,128]{2,1,0:T(8,128)S(1)} %get-tuple-element.40), channel_id=1, source_target_pairs={{0,4},{1,0},{2,6},{3,2},{4,8},{5,1},{6,10},{7,3},{8,12},{9,5},{10,... | collective-permute-start | bytes 110600 | tf_op jit(solution)/shard_map/ppermute | solution.py:452
  36.3 0.0 collective-permute-start.9
  36.3 1.6 %collective-permute-done.8.refs_1_ = f32[3,24,128]{2,1,0:T(8,128)S(1)} collective-permute-done((f32[3,24,128]{2,1,0:T(8,128)S(1)}, f32[3,24,128]{2,1,0:T(8,128)S(1)}, u32[]{:S(2)}, u32[]{:S(2)}) %collective-permute-start.8) | collective-permute-done | bytes 36896 | tf_op jit(solution)/shard_map/ppermute | solution.py:452
  37.9 2.3 %collective-permute-done.9.refs_2_ = f32[3,24,128]{2,1,0:T(8,128)S(1)} collective-permute-done((f32[3,24,128]{2,1,0:T(8,128)S(1)}, f32[3,24,128]{2,1,0:T(8,128)S(1)}, u32[]{:S(2)}, u32[]{:S(2)}) %collective-permute-start.9) | collective-permute-done | bytes 36896 | tf_op jit(solution)/shard_map/ppermute | solution.py:452
  40.3 0.8 %shard_map.75 = (f32[3,2,24,128]{3,2,1,0:T(8,128)S(1)}, f32[32,128]{1,0:T(8,128)S(1)}) custom-call(f32[3,2,24,128]{3,2,1,0:T(8,128)S(1)} %get-tuple-element.39.refs_0_.refs_9_, f32[3,24,128]{2,1,0:T(8,128)S(1)} %collective-permute-done.8.refs_1_, f32[3,24,128]{2,1,0:T(8,128)S(1)} %collective-permute-done.9.refs_2_, ...), custom_call_target="tpu_custom_call" | custom-call | tf_op jit(solution)/shard_map/pallas_call | solution.py:527
  41.1 9.6 %all_to_all.16 = f32[32,1,128]{2,1,0:T(1,128)S(1)} all-to-all(f32[32,1,128]{2,1,0:T(1,128)S(1)} %bitcast.7), channel_id=1, replica_groups=mesh['slab'=8,'batch'=4] {'slab','batch'}, dimensions={0} | all-to-all | bytes 32768 | tf_op jit(solution)/shard_map/all_to_all | solution.py:534
  50.6 1.5 %shard_map.76 = (f32[3,2,16,128]{3,2,1,0:T(8,128)}, f32[3,2,16,128]{3,2,1,0:T(8,128)}) custom-call(f32[32,128]{1,0:T(8,128)S(1)} %bitcast.6, f32[3,2,24,128]{3,2,1,0:T(8,128)S(1)} %get-tuple-element.42.refs_5_.refs_1_, f32[3,2,24,128]{3,2,1,0:T(8,128)S(1)} %get-tuple-element.43.refs_6_.refs_2_, f32[3,2,24,128]{3,2,1,0:T(8,128)S(1)} %get-tuple-element.44.refs_7_.refs_3_, ...), custom_call_target="tpu_custom_call" | custom-call | tf_op jit(solution)/shard_map/pallas_call | solution.py:535
  (4 shorter events, 0.0 us)
Async XLA Ops:
  2.0 7.4 %copy-start = (f32[3,2,16,128]{3,2,1,0:T(8,128)S(1)}, f32[3,2,16,128]{3,2,1,0:T(8,128)}, u32[]{:S(2)}) copy-start(f32[3,2,16,128]{3,2,1,0:T(8,128)} %refs_0_.1) | copy-start | bytes 147460
  2.1 7.4 %copy-start.1 = (f32[3,2,16,128]{3,2,1,0:T(8,128)S(1)}, f32[3,2,16,128]{3,2,1,0:T(8,128)}, u32[]{:S(2)}) copy-start(f32[3,2,16,128]{3,2,1,0:T(8,128)} %refs_1_.3) | copy-start | bytes 147460
  2.1 14.7 %all-to-all-start = ((bf16[32,8,128]{2,1,0:T(8,128)(2,1)}), bf16[32,8,128]{2,1,0:T(8,128)(2,1)S(1)}, u32[]{:S(2)}, u32[]{:S(2)}) async-start(bf16[32,8,128]{2,1,0:T(8,128)(2,1)} %shard_map.68), calls=%async_computation | async-start | bytes 131072 | tf_op jit(solution)/shard_map/all_to_all | solution.py:495
  9.4 3.1 %collective-permute-start = (f32[6,2,4,128]{3,2,1,0:T(4,128)S(1)}, f32[6,2,4,128]{3,2,1,0:T(4,128)S(1)}, u32[]{:S(2)}, u32[]{:S(2)}) collective-permute-start(f32[6,2,4,128]{3,2,1,0:T(4,128)S(1)} %get-tuple-element.25), channel_id=1, source_target_pairs={{0,3},{1,0},{2,1},{3,2},{4,7},{5,4},{6,5},{7,6},{8,11},{9,8},{10,9... | collective-permute-start | bytes 73736 | tf_op jit(solution)/shard_map/ppermute | solution.py:439
  11.0 3.3 %collective-permute-start.1 = (f32[6,2,4,128]{3,2,1,0:T(4,128)S(1)}, f32[6,2,4,128]{3,2,1,0:T(4,128)S(1)}, u32[]{:S(2)}, u32[]{:S(2)}) collective-permute-start(f32[6,2,4,128]{3,2,1,0:T(4,128)S(1)} %get-tuple-element.26), channel_id=1, source_target_pairs={{0,1},{1,2},{2,3},{3,0},{4,5},{5,6},{6,7},{7,4},{8,9},{9,10},{10,1... | collective-permute-start | bytes 73736 | tf_op jit(solution)/shard_map/ppermute | solution.py:439
  17.9 2.7 %collective-permute-start.2 = (f32[3,24,128]{2,1,0:T(8,128)S(1)}, f32[3,24,128]{2,1,0:T(8,128)S(1)}, u32[]{:S(2)}, u32[]{:S(2)}) collective-permute-start(f32[3,24,128]{2,1,0:T(8,128)S(1)} %get-tuple-element.30), channel_id=1, source_target_pairs={{0,4},{1,0},{2,6},{3,2},{4,8},{5,1},{6,10},{7,3},{8,12},{9,5},{10,... | collective-permute-start | bytes 110600 | tf_op jit(solution)/shard_map/ppermute | solution.py:452
  18.5 4.0 %collective-permute-start.3 = (f32[3,24,128]{2,1,0:T(8,128)S(1)}, f32[3,24,128]{2,1,0:T(8,128)S(1)}, u32[]{:S(2)}, u32[]{:S(2)}) collective-permute-start(f32[3,24,128]{2,1,0:T(8,128)S(1)} %get-tuple-element.31), channel_id=1, source_target_pairs={{0,1},{1,5},{2,3},{3,7},{4,0},{5,9},{6,2},{7,11},{8,4},{9,13},{10,... | collective-permute-start | bytes 110600 | tf_op jit(solution)/shard_map/ppermute | solution.py:452
  22.6 4.1 %collective-permute-start.4 = (f32[3,24,128]{2,1,0:T(8,128)S(1)}, f32[3,24,128]{2,1,0:T(8,128)S(1)}, u32[]{:S(2)}, u32[]{:S(2)}) collective-permute-start(f32[3,24,128]{2,1,0:T(8,128)S(1)} %get-tuple-element.34), channel_id=1, source_target_pairs={{0,4},{1,0},{2,6},{3,2},{4,8},{5,1},{6,10},{7,3},{8,12},{9,5},{10,... | collective-permute-start | bytes 110600 | tf_op jit(solution)/shard_map/ppermute | solution.py:452
  25.0 4.0 %collective-permute-start.5 = (f32[3,24,128]{2,1,0:T(8,128)S(1)}, f32[3,24,128]{2,1,0:T(8,128)S(1)}, u32[]{:S(2)}, u32[]{:S(2)}) collective-permute-start(f32[3,24,128]{2,1,0:T(8,128)S(1)} %get-tuple-element.35), channel_id=1, source_target_pairs={{0,1},{1,5},{2,3},{3,7},{4,0},{5,9},{6,2},{7,11},{8,4},{9,13},{10,... | collective-permute-start | bytes 110600 | tf_op jit(solution)/shard_map/ppermute | solution.py:452
  29.1 2.8 %collective-permute-start.6 = (f32[3,24,128]{2,1,0:T(8,128)S(1)}, f32[3,24,128]{2,1,0:T(8,128)S(1)}, u32[]{:S(2)}, u32[]{:S(2)}) collective-permute-start(f32[3,24,128]{2,1,0:T(8,128)S(1)} %get-tuple-element.37), channel_id=1, source_target_pairs={{0,4},{1,0},{2,6},{3,2},{4,8},{5,1},{6,10},{7,3},{8,12},{9,5},{10,... | collective-permute-start | bytes 110600 | tf_op jit(solution)/shard_map/ppermute | solution.py:452
  30.3 4.0 %collective-permute-start.7 = (f32[3,24,128]{2,1,0:T(8,128)S(1)}, f32[3,24,128]{2,1,0:T(8,128)S(1)}, u32[]{:S(2)}, u32[]{:S(2)}) collective-permute-start(f32[3,24,128]{2,1,0:T(8,128)S(1)} %get-tuple-element.38), channel_id=1, source_target_pairs={{0,1},{1,5},{2,3},{3,7},{4,0},{5,9},{6,2},{7,11},{8,4},{9,13},{10,... | collective-permute-start | bytes 110600 | tf_op jit(solution)/shard_map/ppermute | solution.py:452
  34.4 3.5 %collective-permute-start.8 = (f32[3,24,128]{2,1,0:T(8,128)S(1)}, f32[3,24,128]{2,1,0:T(8,128)S(1)}, u32[]{:S(2)}, u32[]{:S(2)}) collective-permute-start(f32[3,24,128]{2,1,0:T(8,128)S(1)} %get-tuple-element.40), channel_id=1, source_target_pairs={{0,4},{1,0},{2,6},{3,2},{4,8},{5,1},{6,10},{7,3},{8,12},{9,5},{10,... | collective-permute-start | bytes 110600 | tf_op jit(solution)/shard_map/ppermute | solution.py:452
  36.3 4.0 %collective-permute-start.9 = (f32[3,24,128]{2,1,0:T(8,128)S(1)}, f32[3,24,128]{2,1,0:T(8,128)S(1)}, u32[]{:S(2)}, u32[]{:S(2)}) collective-permute-start(f32[3,24,128]{2,1,0:T(8,128)S(1)} %get-tuple-element.41), channel_id=1, source_target_pairs={{0,1},{1,5},{2,3},{3,7},{4,0},{5,9},{6,2},{7,11},{8,4},{9,13},{10,... | collective-permute-start | bytes 110600 | tf_op jit(solution)/shard_map/ppermute | solution.py:452

commit v3 on v2

--- a/solution.py
+++ b/solution.py
@@ -119,13 +119,11 @@
         last_out[n * COMPS : (n + 1) * COMPS] = field[:, :, rows - DEPTH :]
 
 
-def setup_kernel(
-    copies, group,
-    message, old, block, value_out, solved_out, up_out, down_out, momentum_sum
-):
-    planes, wide, width = old.shape[1:]
-    rows = wide - 2 * DEPTH
+def deposit_kernel(rows, copies, group, message, momentum_sum):
+    wide = rows + 2 * DEPTH
     height = rows * copies
+    planes = momentum_sum.shape[0] // wide
+    width = momentum_sum.shape[1] // COMPS
     start = lax.axis_index("batch") * rows
     tile = message.shape[2]
     row_iota = lax.broadcasted_iota(jnp.int32, (planes * wide, tile), 0)
@@ -174,118 +172,168 @@
 
         lax.fori_loop(0, steps, one, 0)
 
-    inverses, ratios, lower_planes = block_planes(block)
-    even = lax.axis_index("batch") % 2 == 0
+
+def fill_coefficients(courant, slab, slabs, batch, copies, rows, side, block):
+    planes, wide, width = side.shape[1:]
+    spots = lax.broadcasted_iota(jnp.int32, (wide, width), 0)
+    lanes = lax.broadcasted_iota(jnp.int32, (wide, width), 1)
+    at_top = (spots == rows - 1) & (batch == copies - 1)
+    at_bottom = (spots == 0) & (batch == 0)
+    ratio = None
+    for k in range(planes):
+        upper, lower = [], []
+        for d in range(3):
+            half = 0.5 * courant(d, k)
+            upper.append(diffusion_number - half)
+            lower.append(diffusion_number + half)
+        side[0, k] = jnp.where(at_top, 0.0, upper[1])
+        side[1, k] = jnp.where(at_bottom, 0.0, lower[1])
+        side[2, k] = jnp.where(lanes == width - 1, 0.0, upper[2])
+        side[3, k] = jnp.where(lanes == 0, 0.0, lower[2])
+        if k == 0:
+            pivot = jnp.full((wide, width), diagonal_value, F32)
+            block[3, 0] = jnp.where(slab <= 0, 0.0, lower[0])
+        else:
+            pivot = diagonal_value + lower[0] * ratio
+        if k == planes - 1:
+            block[3, 1] = jnp.where(slab >= slabs - 1, 0.0, upper[0])
+        inverse = 1.0 / pivot
+        ratio = -upper[0] * inverse
+        block[0, k] = inverse
+        block[1, k] = ratio
+        block[2, k] = lower[0]
+
+
+def solve(values, block):
+    planes = len(values)
+    return solve_block(values, *([block[n, k] for k in range(planes)] for n in range(3)))
+
+
+def couple(planes_here, below, above, side, block):
+    planes = len(planes_here)
+    wide, width = planes_here[0].shape
+    values = []
+    for k, here in enumerate(planes_here):
+        total = side[0, k] * pltpu.roll(here, wide - 1, 0)
+        total = total + side[1, k] * pltpu.roll(here, 1, 0)
+        total = total + side[2, k] * pltpu.roll(here, width - 1, 1)
+        total = total + side[3, k] * pltpu.roll(here, 1, 1)
+        if k == 0:
+            total = total + block[3, 0] * below
+        if k == planes - 1:
+            total = total + block[3, 1] * above
+        values.append(total)
+    return values
+
+
+def store_solved(c, solved, even, near_out, up_out, down_out):
+    for k, item in enumerate(solved):
+        near_out[c, k] = item
+    up_out[c] = jnp.where(even, solved[-1], solved[0])
+    down_out[c] = jnp.where(even, solved[0], solved[-1])
+
+
+def setup_kernel(
+    slabs, copies, velocity, courant, after, before, momentum_sum,
+    value_out, near_out, up_out, down_out, side, block,
+):
+    planes, rows, width = velocity.shape[1:]
+    wide = rows + 2 * DEPTH
+    batch = lax.axis_index("batch")
+    for d in range(3):
+        for k in range(planes):
+            near_out[COMPS + d, k] = jnp.concatenate(
+                [courant[d, k], after[COMPS + d, k], before[COMPS + d, k]], axis=0
+            )
+    fill_coefficients(
+        lambda d, k: near_out[COMPS + d, k],
+        lax.axis_index("slab"), slabs, batch, copies, rows, side, block,
+    )
     for c in range(COMPS):
         values = []
         for k in range(planes):
-            deposit_part = momentum_sum[k * wide : (k + 1) * wide, c * width : (c + 1) * width]
-            value = old[c, k] + deposit_part
+            old = jnp.concatenate([velocity[c, k], after[c, k], before[c, k]], axis=0)
+            value = old + momentum_sum[k * wide : (k + 1) * wide, c * width : (c + 1) * width]
             value_out[c, k] = value
             values.append(value)
-        finish_level(c, values, inverses, ratios, lower_planes, even, solved_out, up_out, down_out)
-
-
-def block_planes(block):
-    planes = block.shape[1]
-    return tuple([block[n, k] for k in range(planes)] for n in range(3))
-
-
-def finish_level(c, values, inverses, ratios, lower_planes, even, solved_out, up_out, down_out):
-    solved = solve_block(values, inverses, ratios, lower_planes)
-    for k, item in enumerate(solved):
-        solved_out[c, k] = item
-    up_out[c] = jnp.where(even, solved[-1], solved[0])
-    down_out[c] = jnp.where(even, solved[0], solved[-1])
-
-
-def prepare_kernel(
-    slabs, copies, velocity, courant, after, before, old_out, side_out, block_out
+        store_solved(c, solve(values, block), batch % 2 == 0, near_out, up_out, down_out)
+
+
+def two_levels(slabs, copies, solved, origin, arrived, sides, blocks):
+    near, far, first = arrived[:2], arrived[2:4], arrived[4:]
+    planes, wide = solved.shape[1:3]
+    rows = wide - 2 * DEPTH
+    slab, batch = lax.axis_index("slab"), lax.axis_index("batch")
+    even = batch % 2 == 0
+
+    def low(pair, at):
+        return jnp.where(even, pair[0][at], pair[1][at])
+
+    def high(pair, at):
+        return jnp.where(even, pair[1][at], pair[0][at])
+
+    for n, courant in enumerate(
+        (
+            lambda d, k: low(first, (COMPS + d, k)),
+            lambda d, k: origin[COMPS + d, k],
+            lambda d, k: high(first, (COMPS + d, k)),
+        )
+    ):
+        fill_coefficients(
+            courant, slab + n - 1, slabs, batch, copies, rows, sides.at[n], blocks.at[n]
+        )
+    for c in range(COMPS):
+        here = [solved[c, k] for k in range(planes)]
+        under = [low(near, (c, k)) for k in range(planes)]
+        over = [high(near, (c, k)) for k in range(planes)]
+        face_under = solve(
+            couple(under, low(far, c), here[0], sides.at[0], blocks.at[0]), blocks.at[0]
+        )[-1]
+        face_over = solve(
+            couple(over, here[-1], high(far, c), sides.at[2], blocks.at[2]), blocks.at[2]
+        )[0]
+        one = couple(here, under[-1], over[0], sides.at[1], blocks.at[1])
+        one_solved = solve(one, blocks.at[1])
+        two = couple(one_solved, face_under, face_over, sides.at[1], blocks.at[1])
+        yield c, one, one_solved, two
+
+
+def advance_kernel(
+    slabs, copies, solved, origin, near1, near2, far1, far2, first1, first2,
+    value_out, solved_out, second_out, near_out, up_out, down_out, sides, blocks,
 ):
-    planes, rows, width = velocity.shape[1:]
-    wide = rows + 2 * DEPTH
-    slab, batch = lax.axis_index("slab"), lax.axis_index("batch")
-    for c in range(COMPS):
-        for k in range(planes):
-            old_out[c, k] = jnp.concatenate([velocity[c, k], after[c, k], before[c, k]], axis=0)
-    spots = lax.broadcasted_iota(jnp.int32, (wide, width), 0)
-    lanes = lax.broadcasted_iota(jnp.int32, (wide, width), 1)
-    lower_planes, upper_planes, inverses, ratios = [], [], [], []
-    for k in range(planes):
-        coefs = []
-        for d in range(3):
-            half = 0.5 * jnp.concatenate(
-                [courant[d, k], after[COMPS + d, k], before[COMPS + d, k]], axis=0
-            )
-            coefs.append((diffusion_number - half, diffusion_number + half))
-        upper_planes.append(coefs[0][0])
-        lower_planes.append(coefs[0][1])
-        at_top = (spots == rows - 1) & (batch == copies - 1)
-        at_bottom = (spots == 0) & (batch == 0)
-        side_out[0, k] = jnp.where(at_top, 0.0, coefs[1][0])
-        side_out[1, k] = jnp.where(at_bottom, 0.0, coefs[1][1])
-        side_out[2, k] = jnp.where(lanes == width - 1, 0.0, coefs[2][0])
-        side_out[3, k] = jnp.where(lanes == 0, 0.0, coefs[2][1])
-        if k == 0:
-            pivot = jnp.full((wide, width), diagonal_value, F32)
-        else:
-            pivot = diagonal_value + lower_planes[k] * ratios[-1]
-        inverses.append(1.0 / pivot)
-        ratios.append(-upper_planes[k] * inverses[-1])
-        block_out[0, k] = inverses[k]
-        block_out[1, k] = ratios[k]
-        block_out[2, k] = lower_planes[k]
-    block_out[3, 0] = jnp.where(slab == 0, 0.0, lower_planes[0])
-    block_out[3, 1] = jnp.where(slab == slabs - 1, 0.0, upper_planes[planes - 1])
-
-
-def couple(solved, one_way, other_way, side, block):
-    planes, wide, width = solved.shape[1:]
     even = lax.axis_index("batch") % 2 == 0
-    result = []
-    for c in range(COMPS):
-        values = []
-        for k in range(planes):
-            here = solved[c, k]
-            total = side[0, k] * pltpu.roll(here, wide - 1, 0)
-            total = total + side[1, k] * pltpu.roll(here, 1, 0)
-            total = total + side[2, k] * pltpu.roll(here, width - 1, 1)
-            total = total + side[3, k] * pltpu.roll(here, 1, 1)
-            if k == 0:
-                total = total + block[3, 0] * jnp.where(even, one_way[c], other_way[c])
-            if k == planes - 1:
-                total = total + block[3, 1] * jnp.where(even, other_way[c], one_way[c])
-            values.append(total)
-        result.append(values)
-    return result
-
-
-def apply_kernel(
-    solved, one_way, other_way, side, block, value_out, solved_out, up_out, down_out
-):
-    inverses, ratios, lower_planes = block_planes(block)
-    even = lax.axis_index("batch") % 2 == 0
-    for c, values in enumerate(couple(solved, one_way, other_way, side, block)):
-        for k, item in enumerate(values):
-            value_out[c, k] = item
-        finish_level(c, values, inverses, ratios, lower_planes, even, solved_out, up_out, down_out)
-
-
-def gram_kernel(*refs):
-    solved, one_way, other_way, side, block = refs[:5]
-    values = refs[5 : 5 + DEPTH]
-    value_out, message_out = refs[5 + DEPTH :]
+    arrived = (near1, near2, far1, far2, first1, first2)
+    for c, one, one_solved, two in two_levels(
+        slabs, copies, solved, origin, arrived, sides, blocks
+    ):
+        for k in range(len(one)):
+            value_out[c, k] = one[k]
+            solved_out[c, k] = one_solved[k]
+            second_out[c, k] = two[k]
+        store_solved(c, solve(two, blocks.at[1]), even, near_out, up_out, down_out)
+
+
+def gram_kernel(slabs, copies, *refs):
+    solved, origin = refs[:2]
+    arrived = refs[2:8]
+    values = refs[8 : 7 + DEPTH]
+    value_out, solved_out, second_out, message_out, sides, blocks = refs[7 + DEPTH :]
     planes, wide, width = solved.shape[1:]
     rows = wide - 2 * DEPTH
     sums = []
-    for c, newest in enumerate(couple(solved, one_way, other_way, side, block)):
+    for c, one, one_solved, two in two_levels(
+        slabs, copies, solved, origin, arrived, sides, blocks
+    ):
         for k in range(planes):
-            value_out[c, k] = newest[k]
+            value_out[c, k] = one[k]
+            solved_out[c, k] = one_solved[k]
+            second_out[c, k] = two[k]
         totals = [None] * len(PAIRS)
         for k in range(planes):
             for r in range(0, rows, 8):
-                pieces = [values[i][c, k, r : r + 8, :] for i in range(DEPTH)]
-                pieces.append(newest[k][r : r + 8])
+                pieces = [value[c, k, r : r + 8, :] for value in values]
+                pieces += [one[k][r : r + 8], two[k][r : r + 8]]
                 halves = [split(piece) for piece in pieces]
                 for n, (i, j) in enumerate(PAIRS):
                     p = pieces[i] * pieces[j]
@@ -444,7 +492,7 @@
     pairs = []
     for s in range(slabs):
         for b in range(copies):
-            t = s + 1 if b % 2 == 0 else s - 1
+            t = s + abs(step) if b % 2 == 0 else s - abs(step)
             target = t * copies + b if 0 <= t < slabs else s * copies + (b ^ 1)
             pairs.append((s * copies + b, target))
     if step < 0:
@@ -463,7 +511,7 @@
     assert planes * height <= 256 and 2 * DEPTH <= height - rows
     field = jax.ShapeDtypeStruct((COMPS, planes, wide, width), F32)
     face = jax.ShapeDtypeStruct((COMPS, wide, width), F32)
-    quad = jax.ShapeDtypeStruct((4, planes, wide, width), F32)
+    quad = (4, planes, wide, width)
     edge = jax.ShapeDtypeStruct((2 * COMPS, planes, DEPTH, width), F32)
     own = jax.ShapeDtypeStruct(velocity_old.shape, F32)
 
@@ -484,53 +532,77 @@
         pack,
         (jax.ShapeDtypeStruct((slabs * copies, 8, tile), jnp.bfloat16),),
         [ANY] * 3,
-        60,
+        8,
         [
             pltpu.VMEM((slabs, tile), jnp.int32),
             pltpu.VMEM(forces.shape, F32),
             pltpu.VMEM((slabs, tile), F32),
             pltpu.SemaphoreType.DMA((3,)),
         ],
-    )(cell_ids.reshape(slabs, tile), forces, weights.reshape(slabs, tile))
+    )(
+        *(
+            pltpu.with_memory_space_constraint(x, pltpu.HBM)
+            for x in (cell_ids.reshape(slabs, tile), forces, weights.reshape(slabs, tile))
+        )
+    )
     received = lax.all_to_all(message, everyone, 0, 0, tiled=True)
     first, last = call(edges_kernel, (edge, edge), [VMEM] * 2, 2)(velocity_old, courant)
     after = ring(first, "batch", -1)
     before = ring(last, "batch", 1)
 
-    def prepare(*refs):
-        prepare_kernel(slabs, copies, *refs)
-
-    old, side, block = call(
-        prepare, (field, quad, quad), [VMEM] * 4, 4
-    )(velocity_old, courant, after, before)
-
-    def setup(*refs):
-        setup_kernel(copies, 8, *refs)
-
-    value, solved, up, down = call(
-        setup,
-        (field, field, face, face),
-        [VMEM] * 3,
+    def deposit(*refs):
+        deposit_kernel(rows, copies, 8, *refs)
+
+    (deposited,) = call(
+        deposit,
+        (jax.ShapeDtypeStruct((planes * wide, COMPS * width), F32),),
+        [VMEM],
         12,
-        [pltpu.VMEM((planes * wide, COMPS * width), F32)],
-    )(received, old, block)
-
-    values, solves = [value], [solved]
-    for step in range(1, DEPTH + 1):
-        known = (solved, race(up, 1), race(down, -1), side, block)
-        if step < DEPTH:
-            value, solved, up, down = call(
-                apply_kernel, (field, field, face, face), [VMEM] * 5, 2
+    )(received)
+
+    def placed(kernel):
+        return lambda *refs: kernel(slabs, copies, *refs)
+
+    near_shape = jax.ShapeDtypeStruct((2 * COMPS, planes, wide, width), F32)
+    value, near, up, down = call(
+        placed(setup_kernel),
+        (field, near_shape, face, face),
+        [VMEM] * 5,
+        2,
+        [pltpu.VMEM(quad, F32)] * 2,
+    )(velocity_old, courant, after, before, deposited)
+
+    values, solves = [value], [near]
+    origin, first_near = near, None
+    for iteration in range(ITERS):
+        nears = [race(near, 1), race(near, -1)]
+        first_near = first_near or nears
+        known = (near, origin, *nears, race(up, 2), race(down, -2), *first_near)
+        coefficients = [pltpu.VMEM((3, *quad), F32)] * 2
+        if iteration + 1 < ITERS:
+            value, solved, second, near, up, down = call(
+                placed(advance_kernel),
+                (field, field, field, field, face, face),
+                [VMEM] * 8,
+                4,
+                coefficients,
             )(*known)
-            solves.append(solved)
+            solves += [solved, near]
         else:
-            value, message = call(
-                gram_kernel,
-                (field, jax.ShapeDtypeStruct((slabs * copies, width), F32)),
-                [VMEM] * (5 + DEPTH),
+            value, solved, second, message = call(
+                placed(gram_kernel),
+                (
+                    field,
+                    field,
+                    field,
+                    jax.ShapeDtypeStruct((slabs * copies, width), F32),
+                ),
+                [VMEM] * (8 + len(values)),
                 4,
+                coefficients,
             )(*known, *values)
-        values.append(value)
+            solves += [solved]
+        values += [value, second]
     gathered = lax.all_to_all(message, everyone, 0, 0, tiled=True)
     return call(
         finish_kernel, (own, own), [VMEM] * (1 + BASIS + DEPTH), 4

time: 52.5 us -> 46 us (0.88)
  waiting for transfers between devices: 21.6 us -> 14.5 us
  starting transfers between devices: 15.1 us -> 16.2 us
  blocking collectives: 9.56 us -> 8.89 us
    ppermute x8, waiting for transfers between devices: 15.8 us -> 8.63 us  [race(): return lax.ppermute(array, ('slab', 'batch'), sorted(pairs))]
    all_to_all x1, waiting for transfers between devices: 2.5 us -> 5.83 us  [local(): received = lax.all_to_all(message, everyone, 0, 0, tiled=True)]
    ppermute x2, waiting for transfers between devices: 3.29 us -> 0.01 us  [ring(): lax.ppermute(array, axis, [(i, (i + step) % count) for i in range(count)])]
    ppermute x8, starting transfers between devices: 6.19 us -> 7.36 us  [race(): return lax.ppermute(array, ('slab', 'batch'), sorted(pairs))]
    all_to_all x1, blocking collectives: 9.56 us -> 8.89 us  [local(): gathered = lax.all_to_all(message, everyone, 0, 0, tiled=True)]
    pallas_call x6 -> x4, Pallas kernels: 2.22 us -> 2.35 us  [the longest x1 1.04 us: local(): call(deposit, (jax.ShapeDtypeStruct((planes * wide, COMPS * width), F32),...]
  transfers between devices with their start and end apart: 11 -> 11, of which waited for: 11 -> 5; matrix products, arithmetic and copies ran while one was open for 0% -> 0% of each run, Pallas kernels for 0% -> 2%
where the time goes in v3:
time: 46 us; the launch traced here: 45.7 us
  starting transfers between devices  16.2 us (35%)
  waiting for transfers between devices  14.5 us (32%)
  blocking collectives  8.89 us (19%)
  Pallas kernels  5.31 us (12%)
  between operations  0.74 us (2%)
    all_to_all x1, blocking collectives, local(): gathered = lax.all_to_all(message, everyone, 0, 0, tiled=True)  8.89 us
    ppermute x8, waiting for transfers between devices, race(): return lax.ppermute(array, ('slab', 'batch'), sorted(pairs))  8.63 us
    ppermute x8, starting transfers between devices, race(): return lax.ppermute(array, ('slab', 'batch'), sorted(pairs))  7.36 us
    all_to_all x1, starting transfers between devices, local(): received = lax.all_to_all(message, everyone, 0, 0, tiled=True)  7.33 us
    all_to_all x1, waiting for transfers between devices, local(): received = lax.all_to_all(message, everyone, 0, 0, tiled=True)  5.83 us
    ppermute x2, starting transfers between devices, ring(): lax.ppermute(array, axis, [(i, (i + step) % count) for i in range(count)])  1.54 us
    pallas_call x1, Pallas kernels, local(): call(finish_kernel, (own, own), [VMEM] * (1 + BASIS + DEPTH), 4)  1.53 us
    pallas_call x1, Pallas kernels, local(): call(pack, (jax.ShapeDtypeStruct((slabs * copies, 8, tile), jnp.bfloat16)...  1.42 us
  transfers between devices with their start and end apart: 11, of which 5 were waited for; matrix products, arithmetic and copies ran while one was open for 0% of the time, Pallas kernels for 2%

profile of v3, /device:TPU:0, one launch (start us, length us, event | category | flops | bytes accessed | tf_op | source)
XLA Modules:
  0.0 45.7 jit_solution(15032949392809488523)
XLA Ops:
  0.6 1.4 %shard_map.69 = bf16[32,8,128]{2,1,0:T(8,128)(2,1)} custom-call(s32[8,128]{1,0:T(8,128)} %bitcast.8, f32[3,1024]{1,0:T(4,128)} %refs_1_.2, f32[8,128]{1,0:T(8,128)} %bitcast.9), custom_call_target="tpu_custom_call" | custom-call | tf_op jit(solution)/shard_map/pallas_call | solution.py:531
  2.1 0.0 copy-start
  2.1 0.0 copy-start.1
  2.1 7.3 %all-to-all-start = ((bf16[32,8,128]{2,1,0:T(8,128)(2,1)}), bf16[32,8,128]{2,1,0:T(8,128)(2,1)S(1)}, u32[]{:S(2)}, u32[]{:S(2)}) async-start(bf16[32,8,128]{2,1,0:T(8,128)(2,1)} %shard_map.69), calls=%async_computation | async-start | bytes 131072 | tf_op jit(solution)/shard_map/all_to_all | solution.py:548
  9.4 0.0 copy-done
  9.4 0.0 copy-done.1
  9.5 1.5 %collective-permute-start = (f32[6,2,4,128]{3,2,1,0:T(4,128)S(1)}, f32[6,2,4,128]{3,2,1,0:T(4,128)S(1)}, u32[]{:S(2)}, u32[]{:S(2)}) collective-permute-start(f32[6,2,4,128]{3,2,1,0:T(4,128)S(1)} %get-tuple-element.18), channel_id=1, source_target_pairs={{0,3},{1,0},{2,1},{3,2},{4,7},{5,4},{6,5},{7,6},{8,11},{9,8},{10,9... | collective-permute-start | bytes 73736 | tf_op jit(solution)/shard_map/ppermute | solution.py:487
  11.0 0.0 collective-permute-start.1
  11.0 5.8 %all-to-all-done.refs_0_ = bf16[32,8,128]{2,1,0:T(8,128)(2,1)S(1)} async-done(((bf16[32,8,128]{2,1,0:T(8,128)(2,1)}), bf16[32,8,128]{2,1,0:T(8,128)(2,1)S(1)}, u32[]{:S(2)}, u32[]{:S(2)}) %all-to-all-start) | async-done | bytes 65568 | tf_op jit(solution)/shard_map/all_to_all | solution.py:548
  16.8 1.0 %shard_map.70.refs_4_ = f32[48,384]{1,0:T(8,128)S(1)} custom-call(bf16[32,8,128]{2,1,0:T(8,128)(2,1)S(1)} %all-to-all-done.refs_0_), custom_call_target="tpu_custom_call" | custom-call | tf_op jit(solution)/shard_map/pallas_call | solution.py:556
  17.9 0.0 collective-permute-done.refs_2_
  17.9 0.0 collective-permute-done.1.refs_3_
  17.9 0.2 collective-permute-start.3
  18.1 1.9 %collective-permute-start.2 = (f32[6,2,24,128]{3,2,1,0:T(8,128)S(1)}, f32[6,2,24,128]{3,2,1,0:T(8,128)S(1)}, u32[]{:S(2)}, u32[]{:S(2)}) collective-permute-start(f32[6,2,24,128]{3,2,1,0:T(8,128)S(1)} %get-tuple-element.20.refs_0_.refs_1_.refs_6_), channel_id=1, source_target_pairs={{0,4},{1,0},{2,6},{3,2},{4,8},{5,1},{6,10},{7,3},{8,12},{9,5},{10,... | collective-permute-start | bytes 442376 | tf_op jit(solution)/shard_map/ppermute | solution.py:500
  20.0 0.6 %collective-permute-start.4 = (f32[3,24,128]{2,1,0:T(8,128)S(1)}, f32[3,24,128]{2,1,0:T(8,128)S(1)}, u32[]{:S(2)}, u32[]{:S(2)}) collective-permute-start(f32[3,24,128]{2,1,0:T(8,128)S(1)} %get-tuple-element.21), channel_id=1, source_target_pairs={{0,8},{1,0},{2,10},{3,2},{4,12},{5,4},{6,14},{7,6},{8,16},{9,1},{1... | collective-permute-start | bytes 110600 | tf_op jit(solution)/shard_map/ppermute | solution.py:500
  20.6 0.0 collective-permute-start.5
  20.6 1.6 %collective-permute-done.4.refs_4_ = f32[3,24,128]{2,1,0:T(8,128)S(1)} collective-permute-done((f32[3,24,128]{2,1,0:T(8,128)S(1)}, f32[3,24,128]{2,1,0:T(8,128)S(1)}, u32[]{:S(2)}, u32[]{:S(2)}) %collective-permute-start.4) | collective-permute-done | bytes 36896 | tf_op jit(solution)/shard_map/ppermute | solution.py:500
  22.3 3.0 %collective-permute-done.5.refs_5_ = f32[3,24,128]{2,1,0:T(8,128)S(1)} collective-permute-done((f32[3,24,128]{2,1,0:T(8,128)S(1)}, f32[3,24,128]{2,1,0:T(8,128)S(1)}, u32[]{:S(2)}, u32[]{:S(2)}) %collective-permute-start.5) | collective-permute-done | bytes 36896 | tf_op jit(solution)/shard_map/ppermute | solution.py:500
  25.3 0.0 collective-permute-done.3.refs_3_.refs_7_
  25.3 0.0 collective-permute-done.2.refs_2_.refs_6_
  25.3 0.3 shard_map.72
  25.6 0.1 collective-permute-start.7
  25.7 2.3 %collective-permute-start.6 = (f32[3,2,24,128]{3,2,1,0:T(8,128)S(1)}, f32[3,2,24,128]{3,2,1,0:T(8,128)S(1)}, u32[]{:S(2)}, u32[]{:S(2)}) collective-permute-start(f32[3,2,24,128]{3,2,1,0:T(8,128)S(1)} %get-tuple-element.23.refs_0_.refs_8_), channel_id=1, source_target_pairs={{0,4},{1,0},{2,6},{3,2},{4,8},{5,1},{6,10},{7,3},{8,12},{9,5},{10,... | collective-permute-start | bytes 221192 | tf_op jit(solution)/shard_map/ppermute | solution.py:500
  28.0 2.3 %collective-permute-start.8 = (f32[3,24,128]{2,1,0:T(8,128)S(1)}, f32[3,24,128]{2,1,0:T(8,128)S(1)}, u32[]{:S(2)}, u32[]{:S(2)}) collective-permute-start(f32[3,24,128]{2,1,0:T(8,128)S(1)} %get-tuple-element.24), channel_id=1, source_target_pairs={{0,8},{1,0},{2,10},{3,2},{4,12},{5,4},{6,14},{7,6},{8,16},{9,1},{1... | collective-permute-start | bytes 110600 | tf_op jit(solution)/shard_map/ppermute | solution.py:500
  30.3 0.0 collective-permute-start.9
  30.3 1.6 %collective-permute-done.8.refs_4_ = f32[3,24,128]{2,1,0:T(8,128)S(1)} collective-permute-done((f32[3,24,128]{2,1,0:T(8,128)S(1)}, f32[3,24,128]{2,1,0:T(8,128)S(1)}, u32[]{:S(2)}, u32[]{:S(2)}) %collective-permute-start.8) | collective-permute-done | bytes 36896 | tf_op jit(solution)/shard_map/ppermute | solution.py:500
  31.9 2.3 %collective-permute-done.9.refs_5_ = f32[3,24,128]{2,1,0:T(8,128)S(1)} collective-permute-done((f32[3,24,128]{2,1,0:T(8,128)S(1)}, f32[3,24,128]{2,1,0:T(8,128)S(1)}, u32[]{:S(2)}, u32[]{:S(2)}) %collective-permute-start.9) | collective-permute-done | bytes 36896 | tf_op jit(solution)/shard_map/ppermute | solution.py:500
  34.3 0.0 collective-permute-done.7.refs_3_
  34.3 0.0 collective-permute-done.6.refs_2_
  34.3 1.0 %shard_map.73 = (f32[3,2,24,128]{3,2,1,0:T(8,128)S(1)}, f32[3,2,24,128]{3,2,1,0:T(8,128)S(1)}, f32[3,2,24,128]{3,2,1,0:T(8,128)S(1)}, f32[32,128]{1,0:T(8,128)S(1)}) custom-call(f32[3,2,24,128]{3,2,1,0:T(8,128)S(1)} %get-tuple-element.23.refs_0_.refs_8_, f32[6,2,24,128]{3,2,1,0:T(8,128)S(1)} %get-tuple-element.20.refs_0_.refs_1_.refs_6_, ...), custom_call_target="tpu_custom_call" | custom-call | tf_op jit(solution)/shard_map/pallas_call | solution.py:592
  35.2 8.9 %all_to_all.16 = f32[32,1,128]{2,1,0:T(1,128)S(1)} all-to-all(f32[32,1,128]{2,1,0:T(1,128)S(1)} %bitcast.7), channel_id=1, replica_groups=mesh['slab'=8,'batch'=4] {'slab','batch'}, dimensions={0} | all-to-all | bytes 32768 | tf_op jit(solution)/shard_map/all_to_all | solution.py:606
  44.1 1.5 %shard_map.74 = (f32[3,2,16,128]{3,2,1,0:T(8,128)}, f32[3,2,16,128]{3,2,1,0:T(8,128)}) custom-call(f32[32,128]{1,0:T(8,128)S(1)} %bitcast.6, f32[3,2,24,128]{3,2,1,0:T(8,128)S(1)} %get-tuple-element.26.refs_8_.refs_1_, f32[3,2,24,128]{3,2,1,0:T(8,128)S(1)} %get-tuple-element.27.refs_9_.refs_2_, f32[3,2,24,128]{3,2,1,0:T(8,128)S(1)} %get-tuple-element.28.refs_10_.refs_3_, ...), custom_call_target="tpu_custom_call" | custom-call | tf_op jit(solution)/shard_map/pallas_call | solution.py:607
  (2 shorter events, 0.0 us)
Async XLA Ops:
  2.1 7.4 %copy-start = (f32[3,2,16,128]{3,2,1,0:T(8,128)S(1)}, f32[3,2,16,128]{3,2,1,0:T(8,128)}, u32[]{:S(2)}) copy-start(f32[3,2,16,128]{3,2,1,0:T(8,128)} %refs_0_.1) | copy-start | bytes 147460
  2.1 7.4 %copy-start.1 = (f32[3,2,16,128]{3,2,1,0:T(8,128)S(1)}, f32[3,2,16,128]{3,2,1,0:T(8,128)}, u32[]{:S(2)}) copy-start(f32[3,2,16,128]{3,2,1,0:T(8,128)} %refs_1_.3) | copy-start | bytes 147460
  2.1 14.7 %all-to-all-start = ((bf16[32,8,128]{2,1,0:T(8,128)(2,1)}), bf16[32,8,128]{2,1,0:T(8,128)(2,1)S(1)}, u32[]{:S(2)}, u32[]{:S(2)}) async-start(bf16[32,8,128]{2,1,0:T(8,128)(2,1)} %shard_map.69), calls=%async_computation | async-start | bytes 131072 | tf_op jit(solution)/shard_map/all_to_all | solution.py:548
  9.5 8.4 %collective-permute-start = (f32[6,2,4,128]{3,2,1,0:T(4,128)S(1)}, f32[6,2,4,128]{3,2,1,0:T(4,128)S(1)}, u32[]{:S(2)}, u32[]{:S(2)}) collective-permute-start(f32[6,2,4,128]{3,2,1,0:T(4,128)S(1)} %get-tuple-element.18), channel_id=1, source_target_pairs={{0,3},{1,0},{2,1},{3,2},{4,7},{5,4},{6,5},{7,6},{8,11},{9,8},{10,9... | collective-permute-start | bytes 73736 | tf_op jit(solution)/shard_map/ppermute | solution.py:487
  11.0 6.9 %collective-permute-start.1 = (f32[6,2,4,128]{3,2,1,0:T(4,128)S(1)}, f32[6,2,4,128]{3,2,1,0:T(4,128)S(1)}, u32[]{:S(2)}, u32[]{:S(2)}) collective-permute-start(f32[6,2,4,128]{3,2,1,0:T(4,128)S(1)} %get-tuple-element.19), channel_id=1, source_target_pairs={{0,1},{1,2},{2,3},{3,0},{4,5},{5,6},{6,7},{7,4},{8,9},{9,10},{10,1... | collective-permute-start | bytes 73736 | tf_op jit(solution)/shard_map/ppermute | solution.py:487
  17.9 7.4 %collective-permute-start.3 = (f32[6,2,24,128]{3,2,1,0:T(8,128)S(1)}, f32[6,2,24,128]{3,2,1,0:T(8,128)S(1)}, u32[]{:S(2)}, u32[]{:S(2)}) collective-permute-start(f32[6,2,24,128]{3,2,1,0:T(8,128)S(1)} %get-tuple-element.20.refs_0_.refs_1_.refs_6_), channel_id=1, source_target_pairs={{0,1},{1,5},{2,3},{3,7},{4,0},{5,9},{6,2},{7,11},{8,4},{9,13},{10,... | collective-permute-start | bytes 442376 | tf_op jit(solution)/shard_map/ppermute | solution.py:500
  18.1 7.2 %collective-permute-start.2 = (f32[6,2,24,128]{3,2,1,0:T(8,128)S(1)}, f32[6,2,24,128]{3,2,1,0:T(8,128)S(1)}, u32[]{:S(2)}, u32[]{:S(2)}) collective-permute-start(f32[6,2,24,128]{3,2,1,0:T(8,128)S(1)} %get-tuple-element.20.refs_0_.refs_1_.refs_6_), channel_id=1, source_target_pairs={{0,4},{1,0},{2,6},{3,2},{4,8},{5,1},{6,10},{7,3},{8,12},{9,5},{10,... | collective-permute-start | bytes 442376 | tf_op jit(solution)/shard_map/ppermute | solution.py:500
  20.0 2.2 %collective-permute-start.4 = (f32[3,24,128]{2,1,0:T(8,128)S(1)}, f32[3,24,128]{2,1,0:T(8,128)S(1)}, u32[]{:S(2)}, u32[]{:S(2)}) collective-permute-start(f32[3,24,128]{2,1,0:T(8,128)S(1)} %get-tuple-element.21), channel_id=1, source_target_pairs={{0,8},{1,0},{2,10},{3,2},{4,12},{5,4},{6,14},{7,6},{8,16},{9,1},{1... | collective-permute-start | bytes 110600 | tf_op jit(solution)/shard_map/ppermute | solution.py:500
  20.6 4.7 %collective-permute-start.5 = (f32[3,24,128]{2,1,0:T(8,128)S(1)}, f32[3,24,128]{2,1,0:T(8,128)S(1)}, u32[]{:S(2)}, u32[]{:S(2)}) collective-permute-start(f32[3,24,128]{2,1,0:T(8,128)S(1)} %get-tuple-element.22), channel_id=1, source_target_pairs={{0,1},{1,9},{2,3},{3,11},{4,5},{5,13},{6,7},{7,15},{8,0},{9,17},{1... | collective-permute-start | bytes 110600 | tf_op jit(solution)/shard_map/ppermute | solution.py:500
  25.6 8.6 %collective-permute-start.7 = (f32[3,2,24,128]{3,2,1,0:T(8,128)S(1)}, f32[3,2,24,128]{3,2,1,0:T(8,128)S(1)}, u32[]{:S(2)}, u32[]{:S(2)}) collective-permute-start(f32[3,2,24,128]{3,2,1,0:T(8,128)S(1)} %get-tuple-element.23.refs_0_.refs_8_), channel_id=1, source_target_pairs={{0,1},{1,5},{2,3},{3,7},{4,0},{5,9},{6,2},{7,11},{8,4},{9,13},{10,... | collective-permute-start | bytes 221192 | tf_op jit(solution)/shard_map/ppermute | solution.py:500
  25.7 8.6 %collective-permute-start.6 = (f32[3,2,24,128]{3,2,1,0:T(8,128)S(1)}, f32[3,2,24,128]{3,2,1,0:T(8,128)S(1)}, u32[]{:S(2)}, u32[]{:S(2)}) collective-permute-start(f32[3,2,24,128]{3,2,1,0:T(8,128)S(1)} %get-tuple-element.23.refs_0_.refs_8_), channel_id=1, source_target_pairs={{0,4},{1,0},{2,6},{3,2},{4,8},{5,1},{6,10},{7,3},{8,12},{9,5},{10,... | collective-permute-start | bytes 221192 | tf_op jit(solution)/shard_map/ppermute | solution.py:500
  28.0 3.9 %collective-permute-start.8 = (f32[3,24,128]{2,1,0:T(8,128)S(1)}, f32[3,24,128]{2,1,0:T(8,128)S(1)}, u32[]{:S(2)}, u32[]{:S(2)}) collective-permute-start(f32[3,24,128]{2,1,0:T(8,128)S(1)} %get-tuple-element.24), channel_id=1, source_target_pairs={{0,8},{1,0},{2,10},{3,2},{4,12},{5,4},{6,14},{7,6},{8,16},{9,1},{1... | collective-permute-start | bytes 110600 | tf_op jit(solution)/shard_map/ppermute | solution.py:500
  30.3 4.0 %collective-permute-start.9 = (f32[3,24,128]{2,1,0:T(8,128)S(1)}, f32[3,24,128]{2,1,0:T(8,128)S(1)}, u32[]{:S(2)}, u32[]{:S(2)}) collective-permute-start(f32[3,24,128]{2,1,0:T(8,128)S(1)} %get-tuple-element.25), channel_id=1, source_target_pairs={{0,1},{1,9},{2,3},{3,11},{4,5},{5,13},{6,7},{7,15},{8,0},{9,17},{1... | collective-permute-start | bytes 110600 | tf_op jit(solution)/shard_map/ppermute | solution.py:500

commit v4 on v3

v4 whole, which is shorter than its diff:
```python
import jax
import jax.numpy as jnp
from jax import lax
from jax.experimental import pallas as pl
from jax.experimental.pallas import tpu as pltpu
from jax.sharding import PartitionSpec as P


ITERS = 2
DEPTH = 2 * ITERS
COMPS = 3
BASIS = DEPTH + 1
EARLY = DEPTH - 1
PAIRS = sorted(((i, j) for j in range(BASIS) for i in range(j + 1)), key=lambda p: p[1] >= EARLY)
EARLY_PAIRS = [p for p in PAIRS if p[1] < EARLY]
LATE_PAIRS = [p for p in PAIRS if p[1] >= EARLY]
EARLY_ROWS = -(-len(EARLY_PAIRS) * COMPS // 8) * 8

diffusion_number = 1.0
diagonal_value = 7.0

VMEM = pl.BlockSpec(memory_space=pltpu.VMEM)
ANY = pl.BlockSpec(memory_space=pl.ANY)
F32 = jnp.float32


def two_sum(a, b):
    s = a + b
    bb = s - a
    return s, (a - (s - bb)) + (b - bb)


def quick_two_sum(a, b):
    s = a + b
    return s, b - (s - a)


def split(a):
    t = a * 4097.0
    high = t - (t - a)
    return high, a - high


def product_error(p, a, b):
    ah, al = a
    bh, bl = b
    return ((ah * bh - p) + ah * bl + al * bh) + al * bl


def dd_add(a, b):
    if isinstance(b, int):
        a, b = b, a
    if isinstance(a, int):
        if isinstance(b, int):
            return a + b
        if a == 0:
            return b
        a = (jnp.full_like(b[0], a), jnp.zeros_like(b[0]))
    s, e = two_sum(a[0], b[0])
    return quick_two_sum(s, e + (a[1] + b[1]))


def dd_neg(a):
    return -a if isinstance(a, int) else (-a[0], -a[1])


def dd_sub(a, b):
    return dd_add(a, dd_neg(b))


def dd_mul(a, b):
    if isinstance(b, int):
        a, b = b, a
    if isinstance(a, int):
        if isinstance(b, int):
            return a * b
        return {0: 0, 1: b, -1: dd_neg(b)}[a]
    p = a[0] * b[0]
    e = product_error(p, split(a[0]), split(b[0]))
    return quick_two_sum(p, e + (a[0] * b[1] + a[1] * b[0]))


def dd_div(a, b):
    inverse = 1.0 / b[0]
    q1 = a[0] * inverse
    zero = jnp.zeros_like(q1)
    r = dd_sub(a, dd_mul((q1, zero), b))
    q2 = r[0] * inverse
    return quick_two_sum(q1, q2)


def solve_block(values, inverses, ratios, lower_planes):
    forward = []
    for k, current in enumerate(values):
        if k > 0:
            current = current + lower_planes[k] * forward[-1]
        forward.append(current * inverses[k])
    result = [forward[-1]]
    for k in range(len(values) - 2, -1, -1):
        result.insert(0, forward[k] - ratios[k] * result[0])
    return result


def pack_kernel(slabs, copies, ids_in, forces_in, weights_in, message_out, ids, forces, weights, arrived):
    moves = [
        pltpu.make_async_copy(source, target, arrived.at[n])
        for n, (source, target) in enumerate(
            [(ids_in, ids), (weights_in, weights), (forces_in, forces)]
        )
    ]
    for move in moves:
        move.start()
    for move in moves:
        move.wait()
    tile = ids.shape[1]
    width = 128
    high = ids[...] // width
    low = ids[...] - high * width
    rest = [high.astype(F32), low.astype(F32)]
    rest += [jnp.zeros_like(rest[0])] * (8 - COMPS - len(rest))
    for s in range(slabs):
        at = slice(s * tile, (s + 1) * tile)
        block = jnp.concatenate(
            [forces[:, at] * weights[s : s + 1]] + [part[s : s + 1] for part in rest], axis=0
        )
        for k in range(copies):
            message_out[s * copies + k] = block.astype(jnp.bfloat16)


def edges_kernel(velocity, courant, first_out, last_out):
    rows = velocity.shape[2]
    for n, field in enumerate((velocity, courant)):
        first_out[n * COMPS : (n + 1) * COMPS] = field[:, :, :DEPTH]
        last_out[n * COMPS : (n + 1) * COMPS] = field[:, :, rows - DEPTH :]


def deposit_kernel(rows, copies, group, message, momentum_sum):
    wide = rows + 2 * DEPTH
    height = rows * copies
    planes = momentum_sum.shape[0] // (COMPS * wide)
    width = momentum_sum.shape[1]
    start = lax.axis_index("batch") * rows
    tile = message.shape[2]
    narrow = jnp.bfloat16
    count = lax.broadcasted_iota(jnp.int32, (16, tile), 0).astype(F32)
    counts = [(count + 16.0 * g).astype(narrow) for g in range(width // 16)]
    nothing = jnp.zeros((16, tile), narrow)
    one = jnp.ones((16, tile), narrow)

    def over_sixteen(row):
        return jnp.broadcast_to(row, (16, tile)).astype(narrow)

    def deposit(step):
        row_values, column_hot = [], []
        for k in range(group):
            part = message[step * group + k].astype(F32)
            cell_row = part[3:4].astype(jnp.int32)
            plane = jnp.zeros_like(cell_row)
            for p in range(1, planes):
                plane = plane + (cell_row >= p * height).astype(jnp.int32)
            away = cell_row - plane * height - start
            away = jnp.where(away < 0, away + height, away)
            spot = jnp.where(away < rows + DEPTH, away, away - height + wide)
            inside = (away < rows + DEPTH) | (away >= height - DEPTH)
            spot = over_sixteen(jnp.where(inside, spot + plane * wide, -1).astype(F32))
            column = over_sixteen(part[4:5])
            values = [over_sixteen(part[c : c + 1]) for c in range(COMPS)]
            here = [counts[g] == spot for g in range(planes * wide // 16)]
            row_values.append(
                jnp.concatenate(
                    [jnp.where(at, value, nothing) for value in values for at in here], axis=0
                )
            )
            column_hot.append(
                jnp.concatenate([jnp.where(n == column, one, nothing) for n in counts], axis=0)
            )
        return lax.dot_general(
            jnp.concatenate(row_values, axis=1),
            jnp.concatenate(column_hot, axis=1),
            (((1,), (1,)), ((), ())),
            preferred_element_type=F32,
        )

    steps = message.shape[0] // group
    if steps <= 4:
        total = deposit(0)
        for step in range(1, steps):
            total = total + deposit(step)
        momentum_sum[...] = total
    else:
        momentum_sum[...] = jnp.zeros_like(momentum_sum)

        def add_step(step, carry):
            momentum_sum[...] += deposit(step)
            return carry

        lax.fori_loop(0, steps, add_step, 0)


def fill_coefficients(courant, slab, slabs, batch, copies, rows, side, block):
    planes, wide, width = side.shape[1:]
    spots = lax.broadcasted_iota(jnp.int32, (wide, width), 0)
    lanes = lax.broadcasted_iota(jnp.int32, (wide, width), 1)
    at_top = (spots == rows - 1) & (batch == copies - 1)
    at_bottom = (spots == 0) & (batch == 0)
    ratio = None
    for k in range(planes):
        upper, lower = [], []
        for d in range(3):
            half = 0.5 * courant(d, k)
            upper.append(diffusion_number - half)
            lower.append(diffusion_number + half)
        side[0, k] = jnp.where(at_top, 0.0, upper[1])
        side[1, k] = jnp.where(at_bottom, 0.0, lower[1])
        side[2, k] = jnp.where(lanes == width - 1, 0.0, upper[2])
        side[3, k] = jnp.where(lanes == 0, 0.0, lower[2])
        if k == 0:
            pivot = jnp.full((wide, width), diagonal_value, F32)
            block[3, 0] = jnp.where(slab <= 0, 0.0, lower[0])
        else:
            pivot = diagonal_value + lower[0] * ratio
        if k == planes - 1:
            block[3, 1] = jnp.where(slab >= slabs - 1, 0.0, upper[0])
        inverse = 1.0 / pivot
        ratio = -upper[0] * inverse
        block[0, k] = inverse
        block[1, k] = ratio
        block[2, k] = lower[0]


def solve(values, block):
    planes = len(values)
    return solve_block(values, *([block[n, k] for k in range(planes)] for n in range(3)))


def in_plane(planes_here, side):
    wide, width = planes_here[0].shape
    values = []
    for k, here in enumerate(planes_here):
        total = side[0, k] * pltpu.roll(here, wide - 1, 0)
        total = total + side[1, k] * pltpu.roll(here, 1, 0)
        total = total + side[2, k] * pltpu.roll(here, width - 1, 1)
        total = total + side[3, k] * pltpu.roll(here, 1, 1)
        values.append(total)
    return values


def add_outside(values, below, above, block):
    values = list(values)
    values[0] = values[0] + block[3, 0] * below
    values[-1] = values[-1] + block[3, 1] * above
    return values


def store_messages(c, solved, nearby, rows, even, near_out, far_out):
    wide = solved[0].shape[0]
    one, other = (jnp.where(even, x[-1], x[0]) for x in (solved, nearby))
    at, beside = (jnp.where(even, x[0], x[-1]) for x in (solved, nearby))
    for n, (face, part) in enumerate(((one, other), (at, beside))):
        near_out[n][c * wide : (c + 1) * wide] = face
        start = COMPS * wide + c * rows
        near_out[n][start : start + rows] = part[:rows]
        far_out[n][c] = face[: far_out[n].shape[1]]


def setup_kernel(
    slabs, copies, velocity, courant, after, before, momentum_sum,
    value_out, solved_out, inner_out, near1, near2, far1, far2, side, block, wide_courant,
):
    planes, rows, width = velocity.shape[1:]
    wide = rows + 2 * DEPTH
    batch = lax.axis_index("batch")
    even = batch % 2 == 0
    for d in range(3):
        for k in range(planes):
            wide_courant[d, k] = jnp.concatenate(
                [courant[d, k], after[COMPS + d, k], before[COMPS + d, k]], axis=0
            )
    fill_coefficients(
        lambda d, k: wide_courant[d, k],
        lax.axis_index("slab"), slabs, batch, copies, rows, side, block,
    )
    zero = jnp.zeros((wide, width), F32)
    from_below = solve([block[3, 0]] + [zero] * (planes - 1), block)
    from_above = solve([zero] * (planes - 1) + [block[3, 1]], block)
    start = 2 * COMPS * wide
    for n, part in enumerate((from_below, from_above)):
        at = slice(start + n * wide, start + (n + 1) * wide)
        near1[at] = jnp.where(even, part[-1], part[0])
        near2[at] = jnp.where(even, part[0], part[-1])
    for c in range(COMPS):
        values = []
        for k in range(planes):
            old = jnp.concatenate([velocity[c, k], after[c, k], before[c, k]], axis=0)
            at = (c * planes + k) * wide
            value = old + momentum_sum[at : at + wide]
            value_out[c, k] = value
            values.append(value)
        solved = solve(values, block)
        inner = in_plane(solved, side)
        for k in range(planes):
            solved_out[c, k] = solved[k]
            inner_out[c, k] = inner[k]
        store_messages(c, solved, solve(inner, block), wide, even, (near1, near2), (far1, far2))


def two_levels(solved, inner, near1, near2, far1, far2, first1, first2, side, block):
    planes, wide = solved.shape[1:3]
    rows = far1.shape[1]
    even = lax.axis_index("batch") % 2 == 0

    def low(one, other):
        return jnp.where(even, one, other)

    def high(one, other):
        return jnp.where(even, other, one)

    def part(pick, start, count):
        at = slice(start, start + count)
        return pick(near1[at], near2[at])

    def response(pick, n):
        at = slice((2 * COMPS + n) * wide, (2 * COMPS + n) * wide + rows)
        return pick(first1[at], first2[at])

    low_below, low_above = response(low, 0), response(low, 1)
    high_below, high_above = response(high, 0), response(high, 1)
    pad = jnp.zeros((wide - rows, solved.shape[3]), F32)

    def widen(x):
        return x if rows == wide else jnp.concatenate([x, pad], axis=0)

    for c in range(COMPS):
        own = COMPS * wide + c * rows
        below, above = part(low, c * wide, wide), part(high, c * wide, wide)
        one = add_outside([inner[c, k] for k in range(planes)], below, above, block)
        one_solved = solve(one, block)
        next_below = (
            part(low, own, rows)
            + low_above * solved[c, 0][:rows]
            + low_below * low(far1[c], far2[c])
        )
        next_above = (
            part(high, own, rows)
            + high_below * solved[c, planes - 1][:rows]
            + high_above * high(far1[c], far2[c])
        )
        two = add_outside(
            in_plane(one_solved, side), widen(next_below), widen(next_above), block
        )
        yield c, one, one_solved, two


def advance_kernel(
    solved, inner, near1, near2, far1, far2, first1, first2, side, block,
    value_out, solved_out, second_out, last_out, inner_out, to1, to2, beyond1, beyond2,
):
    even = lax.axis_index("batch") % 2 == 0
    for c, one, one_solved, two in two_levels(
        solved, inner, near1, near2, far1, far2, first1, first2, side, block
    ):
        two_solved = solve(two, block)
        within = in_plane(two_solved, side)
        for k in range(len(one)):
            value_out[c, k] = one[k]
            solved_out[c, k] = one_solved[k]
            second_out[c, k] = two[k]
            last_out[c, k] = two_solved[k]
            inner_out[c, k] = within[k]
        rows = beyond1.shape[1]
        store_messages(c, two_solved, solve(within, block), rows, even, (to1, to2), (beyond1, beyond2))


def gram_sums(pieces, pairs, totals):
    halves = [split(piece) for piece in pieces]
    for n, (i, j) in enumerate(pairs):
        p = pieces[i] * pieces[j]
        e = product_error(p, halves[i], halves[j])
        if totals[n] is None:
            totals[n] = (p, e)
        else:
            s, t = two_sum(totals[n][0], p)
            totals[n] = (s, totals[n][1] + (t + e))


def stack_sums(sums, count):
    flat = [sums[c][n] for n in range(len(sums[0])) for c in range(COMPS)]
    flat += [(jnp.zeros_like(flat[0][0]),) * 2] * (count - len(flat))
    rows_of = [sum_to_sublanes(flat[n : n + 8]) for n in range(0, count, 8)]
    return [jnp.concatenate([x[p] for x in rows_of], axis=0) for p in (0, 1)]


def early_kernel(rows, *refs):
    values, (high_out, low_out) = refs[:EARLY], refs[EARLY:]
    sums = []
    for c in range(COMPS):
        totals = [None] * len(EARLY_PAIRS)
        for k in range(values[0].shape[1]):
            for r in range(0, rows, 8):
                gram_sums([v[c, k, r : r + 8, :] for v in values], EARLY_PAIRS, totals)
        sums.append(totals)
    high_out[...], low_out[...] = stack_sums(sums, EARLY_ROWS)


def gram_kernel(*refs):
    known = refs[:10]
    values = refs[10 : 10 + EARLY]
    early = refs[10 + EARLY : 12 + EARLY]
    value_out, solved_out, second_out, message_out = refs[12 + EARLY :]
    planes, wide, width = value_out.shape[1:]
    rows = wide - 2 * DEPTH
    sums = []
    for c, one, one_solved, two in two_levels(*known):
        totals = [None] * len(LATE_PAIRS)
        for k in range(planes):
            value_out[c, k] = one[k]
            solved_out[c, k] = one_solved[k]
            second_out[c, k] = two[k]
            for r in range(0, rows, 8):
                pieces = [value[c, k, r : r + 8, :] for value in values]
                gram_sums(pieces + [one[k][r : r + 8], two[k][r : r + 8]], LATE_PAIRS, totals)
        sums.append(totals)
    late = stack_sums(sums, width // 2 - EARLY_ROWS)
    turned = [jnp.transpose(jnp.concatenate([e[...], x], axis=0)) for e, x in zip(early, late)]
    total = tuple(x[:8] for x in turned)
    for r in range(8, width, 8):
        total = dd_add(total, tuple(x[r : r + 8] for x in turned))
    for shift in (4, 2, 1):
        total = dd_add(total, tuple(pltpu.roll(x, shift, 0) for x in total))
    row = jnp.concatenate([x[:1] for x in total], axis=1)
    message_out[...] = jnp.broadcast_to(row, message_out.shape)


def sum_to_sublanes(parts):
    sub = lax.broadcasted_iota(jnp.int32, parts[0][0].shape, 0)
    level = parts
    for shift in (4, 2, 1):
        keep = (sub & shift) == 0
        merged = []
        for a, b in zip(level[:shift], level[shift:]):
            stay = tuple(jnp.where(keep, x, y) for x, y in zip(a, b))
            swap = [jnp.where(keep, y, x) for x, y in zip(a, b)]
            moved = tuple(
                pltpu.roll(w, 4, 0)
                if shift == 4
                else jnp.where(keep, pltpu.roll(w, 8 - shift, 0), pltpu.roll(w, shift, 0))
                for w in swap
            )
            merged.append(dd_add(stay, moved))
        level = merged
    return level[0]


def finish_kernel(*refs):
    gathered = refs[0]
    values = refs[1 : 1 + BASIS]
    solved = refs[1 + BASIS : 1 + BASIS + DEPTH]
    solution_out, residual_out, solution_here, residual_here, sent = refs[1 + BASIS + DEPTH :]
    planes, rows, _ = solution_here.shape[1:]
    count, lanes = gathered.shape
    total = None
    for r in range(0, count, 8):
        high = gathered[r : r + 8]
        item = (high, pltpu.roll(high, lanes // 2, 1))
        total = item if total is None else dd_add(total, item)
    for shift in (4, 2, 1):
        total = dd_add(total, tuple(pltpu.roll(x, shift, 0) for x in total))
    sub = lax.broadcasted_iota(jnp.int32, (8, lanes), 0)

    def entry(n):
        start = n * COMPS
        if n >= len(EARLY_PAIRS):
            start = EARLY_ROWS + (n - len(EARLY_PAIRS)) * COMPS
        return tuple(pltpu.roll(x, (lanes - start) % lanes, 1) for x in total)

    entries = {pair: entry(n) for n, pair in enumerate(PAIRS)}
    gram = []
    for i in range(BASIS):
        row = None
        for j in range(BASIS):
            item = entries[(min(i, j), max(i, j))]
            if row is None:
                row = item
            else:
                row = tuple(jnp.where(sub == j, x, y) for x, y in zip(item, row))
        gram.append(row)
    zero = jnp.zeros((8, lanes), F32)

    def stack(poly):
        out = (zero, zero)
        for j, item in enumerate(poly):
            if isinstance(item, int):
                item = (zero + item, zero)
            out = tuple(jnp.where(sub == j, x, y) for x, y in zip(item, out))
        return out

    def over_sublanes(x):
        for shift in (4, 2, 1):
            x = dd_add(x, tuple(pltpu.roll(y, shift, 0) for y in x))
        return x

    def gram_times(poly):
        out = 0
        for i, item in enumerate(poly):
            out = dd_add(out, dd_mul(item, gram[i]))
        return tuple(jnp.where(sub < BASIS, x, 0.0) for x in out)

    def with_shadow(poly):
        terms = [dd_mul(item, entries[(0, i)]) for i, item in enumerate(poly)]
        while len(terms) > 1:
            pairs = [dd_add(*terms[i : i + 2]) for i in range(0, len(terms) - 1, 2)]
            terms = pairs + terms[len(pairs) * 2 :]
        return terms[0]

    def operate(poly):
        out = list(poly) + [0]
        return [out[0]] + [dd_sub(out[i], out[i - 1]) for i in range(1, len(out))]

    def combine(first, factor, second):
        out = []
        for i in range(max(len(first), len(second))):
            item = first[i] if i < len(first) else 0
            if i < len(second):
                item = dd_add(item, dd_mul(factor, second[i]))
            out.append(item)
        return out

    residual = [1]
    direction = [1]
    answer = []
    rho = entries[(0, 0)]
    for iteration in range(ITERS):
        image = operate(direction)
        alpha = dd_div(rho, with_shadow(image))
        middle = combine(residual, dd_neg(alpha), image)
        turned = operate(middle)
        weighted = gram_times(turned)
        cross = over_sublanes(dd_mul(weighted, stack(middle)))
        square = over_sublanes(dd_mul(weighted, stack(turned)))
        omega = dd_div(cross, square)
        answer = combine(answer, alpha, direction)
        answer = combine(answer, omega, middle)
        residual = combine(middle, dd_neg(omega), turned)
        if iteration + 1 < ITERS:
            rho_next = with_shadow(residual)
            factor = dd_mul(dd_div(rho_next, rho), dd_div(alpha, omega))
            direction = combine(direction, dd_neg(omega), image)
            direction = combine(residual, factor, direction)
            rho = rho_next
    moves = []
    for c in range(COMPS):
        for n, (poly, basis, here, out) in enumerate(
            (
                (answer, solved, solution_here, solution_out),
                (residual, values, residual_here, residual_out),
            )
        ):
            scales = [item[0][:, c : c + 1] for item in poly]
            for k in range(planes):
                for r in range(0, rows, 8):
                    total = scales[0] * basis[0][c, k, r : r + 8, :]
                    for i in range(1, len(scales)):
                        total = total + scales[i] * basis[i][c, k, r : r + 8, :]
                    here[c, k, r : r + 8, :] = total
            moves.append(pltpu.make_async_copy(here.at[c], out.at[c], sent.at[n * COMPS + c]))
            moves[-1].start()
    for move in moves:
        move.wait()


def ring(array, axis, step):
    count = lax.axis_size(axis)
    return lax.ppermute(array, axis, [(i, (i + step) % count) for i in range(count)])


def race(array, step):
    slabs, copies = lax.axis_size("slab"), lax.axis_size("batch")
    pairs = []
    for s in range(slabs):
        for b in range(copies):
            t = s + abs(step) if b % 2 == 0 else s - abs(step)
            target = t * copies + b if 0 <= t < slabs else s * copies + (b ^ 1)
            pairs.append((s * copies + b, target))
    if step < 0:
        pairs = [(t, s) for s, t in pairs]
    return lax.ppermute(array, ("slab", "batch"), sorted(pairs))


def local(velocity_old, courant, cell_ids, forces, weights):
    planes, rows, width = velocity_old.shape[1:]
    slabs, copies = lax.axis_size("slab"), lax.axis_size("batch")
    everyone = ("slab", "batch")
    wide = rows + 2 * DEPTH
    height = rows * copies
    tile = cell_ids.shape[0] // slabs
    assert rows % 8 == 0 and width == 128 and copies % 2 == 0
    assert planes * height <= 256 and 2 * DEPTH <= height - rows
    field = jax.ShapeDtypeStruct((COMPS, planes, wide, width), F32)
    quad = jax.ShapeDtypeStruct((4, planes, wide, width), F32)
    edge = jax.ShapeDtypeStruct((2 * COMPS, planes, DEPTH, width), F32)
    own = jax.ShapeDtypeStruct(velocity_old.shape, F32)

    def call(kernel, out_shape, in_specs, mib, scratch=(), out_space=VMEM, cost=None):
        if cost is not None:
            cost = pl.CostEstimate(flops=cost, bytes_accessed=0, transcendentals=0)
        return pl.pallas_call(
            kernel,
            out_shape=out_shape,
            in_specs=in_specs,
            out_specs=[out_space] * len(out_shape),
            cost_estimate=cost,
            scratch_shapes=list(scratch),
            compiler_params=pltpu.CompilerParams(vmem_limit_bytes=mib << 20),
        )

    def pack(*refs):
        pack_kernel(slabs, copies, *refs)

    (message,) = call(
        pack,
        (jax.ShapeDtypeStruct((slabs * copies, 8, tile), jnp.bfloat16),),
        [ANY] * 3,
        8,
        [
            pltpu.VMEM((slabs, tile), jnp.int32),
            pltpu.VMEM(forces.shape, F32),
            pltpu.VMEM((slabs, tile), F32),
            pltpu.SemaphoreType.DMA((3,)),
        ],
    )(
        *(
            pltpu.with_memory_space_constraint(x, pltpu.HBM)
            for x in (cell_ids.reshape(slabs, tile), forces, weights.reshape(slabs, tile))
        )
    )
    received = lax.all_to_all(message, everyone, 0, 0, tiled=True)
    first, last = call(edges_kernel, (edge, edge), [VMEM] * 2, 2)(velocity_old, courant)
    after = ring(first, "batch", -1)
    before = ring(last, "batch", 1)

    def deposit(*refs):
        deposit_kernel(rows, copies, 8, *refs)

    (deposited,) = call(
        deposit, (jax.ShapeDtypeStruct((COMPS * planes * wide, width), F32),), [VMEM], 12
    )(received)

    def setup(*refs):
        setup_kernel(slabs, copies, *refs)

    def flat(count):
        return jax.ShapeDtypeStruct((count, width), F32)

    def faces(count):
        return jax.ShapeDtypeStruct((COMPS, count, width), F32)

    value, solved, inner, *sent, side, block = call(
        setup,
        (field,) * 3 + (flat((2 * COMPS + 2) * wide),) * 2 + (faces(wide),) * 2 + (quad,) * 2,
        [VMEM] * 5,
        2,
        [pltpu.VMEM((3, planes, wide, width), F32)],
    )(velocity_old, courant, after, before, deposited)

    values, solves = [value], [solved]
    first = None
    for iteration in range(ITERS):
        near = [race(sent[0], 1), race(sent[1], -1)]
        far = [race(sent[2], 2), race(sent[3], -2)]
        first = first or near
        known = (solved, inner, *near, *far, *first, side, block)
        if iteration + 1 < ITERS:
            reach = wide if iteration + 2 < ITERS else rows
            value, one_solved, second, solved, inner, *sent = call(
                advance_kernel,
                (field,) * 5 + (flat(COMPS * (wide + reach)),) * 2 + (faces(reach),) * 2,
                [VMEM] * 10,
                2,
            )(*known)
            solves += [one_solved, solved]
        else:
            def early(*refs):
                early_kernel(rows, *refs)

            sums = call(early, (flat(EARLY_ROWS),) * 2, [VMEM] * EARLY, 2, cost=4000000)(*values)
            value, one_solved, second, message = call(
                gram_kernel, (field,) * 3 + (flat(slabs * copies),), [VMEM] * (12 + EARLY), 4
            )(*known, *values, *sums)
            solves += [one_solved]
        values += [value, second]
    gathered = lax.all_to_all(message, everyone, 0, 0, tiled=True)
    return call(
        finish_kernel,
        (own, own),
        [VMEM] * (1 + BASIS + DEPTH),
        4,
        [pltpu.VMEM(own.shape, F32)] * 2 + [pltpu.SemaphoreType.DMA((2 * COMPS,))],
        ANY,
    )(gathered, *values, *solves)


def solution(mesh):
    placed = (
        P(None, "slab", "batch", None),
        P(None, "slab", "batch", None),
        P(("slab", "batch")),
        P(None, ("slab", "batch")),
        P(("slab", "batch")),
    )
    return jax.shard_map(
        local,
        mesh=mesh,
        in_specs=placed,
        out_specs=(P(None, "slab", "batch", None), P(None, "slab", "batch", None)),
        check_vma=False,
    )
```

time: 46 us -> 44 us (0.957)
  waiting for transfers between devices: 14.5 us -> 13.4 us
  Pallas kernels: 5.31 us -> 4.55 us
    ppermute x8, waiting for transfers between devices: 8.63 us -> 7.56 us  [race(): return lax.ppermute(array, ('slab', 'batch'), sorted(pairs))]
    pallas_call x5 -> x6, Pallas kernels: 3.88 us -> 3.12 us  [the longest x1 1.4 us: local(): call(finish_kernel, (own, own), [VMEM] * (1 + BASIS + DEPTH), 4, [pltpu.V...]
where the time goes in v4:
time: 44 us; the launch traced here: 43.6 us
  starting transfers between devices  16.1 us (37%)
  waiting for transfers between devices  13.4 us (30%)
  blocking collectives  8.86 us (20%)
  Pallas kernels  4.55 us (10%)
  between operations  0.73 us (2%)
    all_to_all x1, blocking collectives, local(): gathered = lax.all_to_all(message, everyone, 0, 0, tiled=True)  8.86 us
    ppermute x8, waiting for transfers between devices, race(): return lax.ppermute(array, ('slab', 'batch'), sorted(pairs))  7.56 us
    all_to_all x1, starting transfers between devices, local(): received = lax.all_to_all(message, everyone, 0, 0, tiled=True)  7.33 us
    ppermute x8, starting transfers between devices, race(): return lax.ppermute(array, ('slab', 'batch'), sorted(pairs))  7.2 us
    all_to_all x1, waiting for transfers between devices, local(): received = lax.all_to_all(message, everyone, 0, 0, tiled=True)  5.83 us
    ppermute x2, starting transfers between devices, ring(): lax.ppermute(array, axis, [(i, (i + step) % count) for i in range(count)])  1.54 us
    pallas_call x1, Pallas kernels, local(): call(pack, (jax.ShapeDtypeStruct((slabs * copies, 8, tile), jnp.bfloat16)...  1.43 us
    pallas_call x1, Pallas kernels, local(): call(finish_kernel, (own, own), [VMEM] * (1 + BASIS + DEPTH), 4, [pltpu.V...  1.4 us
  transfers between devices with their start and end apart: 11, of which 5 were waited for; matrix products, arithmetic and copies ran while one was open for 0% of the time, Pallas kernels for 2%

profile of v4, /device:TPU:0, one launch (start us, length us, event | category | flops | bytes accessed | tf_op | source)
XLA Modules:
  0.0 43.6 jit_solution(470539889712888375)
XLA Ops:
  0.6 1.4 %shard_map.69 = bf16[32,8,128]{2,1,0:T(8,128)(2,1)} custom-call(s32[8,128]{1,0:T(8,128)} %bitcast.8, f32[3,1024]{1,0:T(4,128)} %refs_1_.2, f32[8,128]{1,0:T(8,128)} %bitcast.9), custom_call_target="tpu_custom_call" | custom-call | tf_op jit(solution)/shard_map/pallas_call | solution.py:619
  2.1 0.0 copy-start
  2.1 0.0 copy-start.1
  2.1 7.3 %all-to-all-start = ((bf16[32,8,128]{2,1,0:T(8,128)(2,1)}), bf16[32,8,128]{2,1,0:T(8,128)(2,1)S(1)}, u32[]{:S(2)}, u32[]{:S(2)}) async-start(bf16[32,8,128]{2,1,0:T(8,128)(2,1)} %shard_map.69), calls=%async_computation | async-start | bytes 131072 | tf_op jit(solution)/shard_map/all_to_all | solution.py:636
  9.5 1.5 %collective-permute-start = (f32[6,2,4,128]{3,2,1,0:T(4,128)S(1)}, f32[6,2,4,128]{3,2,1,0:T(4,128)S(1)}, u32[]{:S(2)}, u32[]{:S(2)}) collective-permute-start(f32[6,2,4,128]{3,2,1,0:T(4,128)S(1)} %get-tuple-element.28), channel_id=1, source_target_pairs={{0,3},{1,0},{2,1},{3,2},{4,7},{5,4},{6,5},{7,6},{8,11},{9,8},{10,9... | collective-permute-start | bytes 73736 | tf_op jit(solution)/shard_map/ppermute | solution.py:573
  11.0 0.0 collective-permute-start.1
  11.0 5.8 %all-to-all-done.refs_0_ = bf16[32,8,128]{2,1,0:T(8,128)(2,1)S(1)} async-done(((bf16[32,8,128]{2,1,0:T(8,128)(2,1)}), bf16[32,8,128]{2,1,0:T(8,128)(2,1)S(1)}, u32[]{:S(2)}, u32[]{:S(2)}) %all-to-all-start) | async-done | bytes 65568 | tf_op jit(solution)/shard_map/all_to_all | solution.py:636
  16.8 0.5 %shard_map.70.refs_4_ = f32[144,128]{1,0:T(8,128)S(1)} custom-call(bf16[32,8,128]{2,1,0:T(8,128)(2,1)S(1)} %all-to-all-done.refs_0_), custom_call_target="tpu_custom_call" | custom-call | tf_op jit(solution)/shard_map/pallas_call | solution.py:644
  17.3 0.0 collective-permute-done.refs_2_
  17.3 0.0 collective-permute-done.1.refs_3_
  17.3 0.1 shard_map.71
  17.5 0.7 %collective-permute-start.2 = (f32[192,128]{1,0:T(8,128)S(1)}, f32[192,128]{1,0:T(8,128)S(1)}, u32[]{:S(2)}, u32[]{:S(2)}) collective-permute-start(f32[192,128]{1,0:T(8,128)S(1)} %get-tuple-element.32), channel_id=1, source_target_pairs={{0,4},{1,0},{2,6},{3,2},{4,8},{5,1},{6,10},{7,3},{8,12},{9,5},{10,... | collective-permute-start | bytes 294920 | tf_op jit(solution)/shard_map/ppermute | solution.py:586
  18.1 0.0 collective-permute-start.3
  18.1 2.9 %collective-permute-start.4 = (f32[3,24,128]{2,1,0:T(8,128)S(1)}, f32[3,24,128]{2,1,0:T(8,128)S(1)}, u32[]{:S(2)}, u32[]{:S(2)}) collective-permute-start(f32[3,24,128]{2,1,0:T(8,128)S(1)} %get-tuple-element.34), channel_id=1, source_target_pairs={{0,8},{1,0},{2,10},{3,2},{4,12},{5,4},{6,14},{7,6},{8,16},{9,1},{1... | collective-permute-start | bytes 110600 | tf_op jit(solution)/shard_map/ppermute | solution.py:586
  21.1 0.0 collective-permute-start.5
  21.1 1.6 %collective-permute-done.4.far1 = f32[3,24,128]{2,1,0:T(8,128)S(1)} collective-permute-done((f32[3,24,128]{2,1,0:T(8,128)S(1)}, f32[3,24,128]{2,1,0:T(8,128)S(1)}, u32[]{:S(2)}, u32[]{:S(2)}) %collective-permute-start.4) | collective-permute-done | bytes 36896 | tf_op jit(solution)/shard_map/ppermute | solution.py:586
  22.7 2.3 %collective-permute-done.5.far2 = f32[3,24,128]{2,1,0:T(8,128)S(1)} collective-permute-done((f32[3,24,128]{2,1,0:T(8,128)S(1)}, f32[3,24,128]{2,1,0:T(8,128)S(1)}, u32[]{:S(2)}, u32[]{:S(2)}) %collective-permute-start.5) | collective-permute-done | bytes 36896 | tf_op jit(solution)/shard_map/ppermute | solution.py:586
  25.0 0.0 collective-permute-done.2.near1.first1.refs_6_
  25.0 0.0 collective-permute-done.3.near2.first2.refs_7_
  25.0 0.2 shard_map.72
  25.3 0.9 %collective-permute-start.6 = (f32[120,128]{1,0:T(8,128)S(1)}, f32[120,128]{1,0:T(8,128)S(1)}, u32[]{:S(2)}, u32[]{:S(2)}) collective-permute-start(f32[120,128]{1,0:T(8,128)S(1)} %get-tuple-element.40), channel_id=1, source_target_pairs={{0,4},{1,0},{2,6},{3,2},{4,8},{5,1},{6,10},{7,3},{8,12},{9,5},{10,... | collective-permute-start | bytes 184328 | tf_op jit(solution)/shard_map/ppermute | solution.py:586
  26.1 0.0 collective-permute-start.7
  26.1 2.7 %collective-permute-start.8 = (f32[3,16,128]{2,1,0:T(8,128)S(1)}, f32[3,16,128]{2,1,0:T(8,128)S(1)}, u32[]{:S(2)}, u32[]{:S(2)}) collective-permute-start(f32[3,16,128]{2,1,0:T(8,128)S(1)} %get-tuple-element.42), channel_id=1, source_target_pairs={{0,8},{1,0},{2,10},{3,2},{4,12},{5,4},{6,14},{7,6},{8,16},{9,1},{1... | collective-permute-start | bytes 73736 | tf_op jit(solution)/shard_map/ppermute | solution.py:586
  28.9 0.0 collective-permute-start.9
  28.9 0.2 shard_map.73
  29.1 1.3 %collective-permute-done.8.refs_4_ = f32[3,16,128]{2,1,0:T(8,128)S(1)} collective-permute-done((f32[3,16,128]{2,1,0:T(8,128)S(1)}, f32[3,16,128]{2,1,0:T(8,128)S(1)}, u32[]{:S(2)}, u32[]{:S(2)}) %collective-permute-start.8) | collective-permute-done | bytes 24608 | tf_op jit(solution)/shard_map/ppermute | solution.py:586
  30.4 2.3 %collective-permute-done.9.refs_5_ = f32[3,16,128]{2,1,0:T(8,128)S(1)} collective-permute-done((f32[3,16,128]{2,1,0:T(8,128)S(1)}, f32[3,16,128]{2,1,0:T(8,128)S(1)}, u32[]{:S(2)}, u32[]{:S(2)}) %collective-permute-start.9) | collective-permute-done | bytes 24608 | tf_op jit(solution)/shard_map/ppermute | solution.py:586
  32.7 0.0 collective-permute-done.6.refs_2_
  32.7 0.0 collective-permute-done.7.refs_3_
  32.7 0.7 %shard_map.74 = (f32[3,2,24,128]{3,2,1,0:T(8,128)S(1)}, f32[3,2,24,128]{3,2,1,0:T(8,128)S(1)}, f32[3,2,24,128]{3,2,1,0:T(8,128)S(1)}, f32[32,128]{1,0:T(8,128)S(1)}) custom-call(f32[3,2,24,128]{3,2,1,0:T(8,128)S(1)} %get-tuple-element.38.refs_0_.refs_8_, f32[3,2,24,128]{3,2,1,0:T(8,128)S(1)} %get-tuple-element.39.refs_1_, ...), custom_call_target="tpu_custom_call" | custom-call | tf_op jit(solution)/shard_map/pallas_call | solution.py:686
  33.4 8.9 %all_to_all.16 = f32[32,1,128]{2,1,0:T(1,128)S(1)} all-to-all(f32[32,1,128]{2,1,0:T(1,128)S(1)} %bitcast.7), channel_id=1, replica_groups=mesh['slab'=8,'batch'=4] {'slab','batch'}, dimensions={0} | all-to-all | bytes 32768 | tf_op jit(solution)/shard_map/all_to_all | solution.py:691
  42.2 1.4 %shard_map.75 = (f32[3,2,16,128]{3,2,1,0:T(8,128)}, f32[3,2,16,128]{3,2,1,0:T(8,128)}) custom-call(f32[32,128]{1,0:T(8,128)S(1)} %bitcast.6, f32[3,2,24,128]{3,2,1,0:T(8,128)S(1)} %get-tuple-element.44.refs_0_.refs_10_.refs_1_, f32[3,2,24,128]{3,2,1,0:T(8,128)S(1)} %get-tuple-element.45.refs_1_.refs_11_.refs_2_, ...), custom_call_target="tpu_custom_call" | custom-call | tf_op jit(solution)/shard_map/pallas_call | solution.py:692
  (3 shorter events, 0.0 us)
Async XLA Ops:
  2.1 7.4 %copy-start = (f32[3,2,16,128]{3,2,1,0:T(8,128)S(1)}, f32[3,2,16,128]{3,2,1,0:T(8,128)}, u32[]{:S(2)}) copy-start(f32[3,2,16,128]{3,2,1,0:T(8,128)} %refs_0_.1) | copy-start | bytes 147460
  2.1 7.4 %copy-start.1 = (f32[3,2,16,128]{3,2,1,0:T(8,128)S(1)}, f32[3,2,16,128]{3,2,1,0:T(8,128)}, u32[]{:S(2)}) copy-start(f32[3,2,16,128]{3,2,1,0:T(8,128)} %refs_1_.3) | copy-start | bytes 147460
  2.1 14.7 %all-to-all-start = ((bf16[32,8,128]{2,1,0:T(8,128)(2,1)}), bf16[32,8,128]{2,1,0:T(8,128)(2,1)S(1)}, u32[]{:S(2)}, u32[]{:S(2)}) async-start(bf16[32,8,128]{2,1,0:T(8,128)(2,1)} %shard_map.69), calls=%async_computation | async-start | bytes 131072 | tf_op jit(solution)/shard_map/all_to_all | solution.py:636
  9.5 7.9 %collective-permute-start = (f32[6,2,4,128]{3,2,1,0:T(4,128)S(1)}, f32[6,2,4,128]{3,2,1,0:T(4,128)S(1)}, u32[]{:S(2)}, u32[]{:S(2)}) collective-permute-start(f32[6,2,4,128]{3,2,1,0:T(4,128)S(1)} %get-tuple-element.28), channel_id=1, source_target_pairs={{0,3},{1,0},{2,1},{3,2},{4,7},{5,4},{6,5},{7,6},{8,11},{9,8},{10,9... | collective-permute-start | bytes 73736 | tf_op jit(solution)/shard_map/ppermute | solution.py:573
  11.0 6.3 %collective-permute-start.1 = (f32[6,2,4,128]{3,2,1,0:T(4,128)S(1)}, f32[6,2,4,128]{3,2,1,0:T(4,128)S(1)}, u32[]{:S(2)}, u32[]{:S(2)}) collective-permute-start(f32[6,2,4,128]{3,2,1,0:T(4,128)S(1)} %get-tuple-element.29), channel_id=1, source_target_pairs={{0,1},{1,2},{2,3},{3,0},{4,5},{5,6},{6,7},{7,4},{8,9},{9,10},{10,1... | collective-permute-start | bytes 73736 | tf_op jit(solution)/shard_map/ppermute | solution.py:573
  17.5 7.6 %collective-permute-start.2 = (f32[192,128]{1,0:T(8,128)S(1)}, f32[192,128]{1,0:T(8,128)S(1)}, u32[]{:S(2)}, u32[]{:S(2)}) collective-permute-start(f32[192,128]{1,0:T(8,128)S(1)} %get-tuple-element.32), channel_id=1, source_target_pairs={{0,4},{1,0},{2,6},{3,2},{4,8},{5,1},{6,10},{7,3},{8,12},{9,5},{10,... | collective-permute-start | bytes 294920 | tf_op jit(solution)/shard_map/ppermute | solution.py:586
  18.1 6.9 %collective-permute-start.3 = (f32[192,128]{1,0:T(8,128)S(1)}, f32[192,128]{1,0:T(8,128)S(1)}, u32[]{:S(2)}, u32[]{:S(2)}) collective-permute-start(f32[192,128]{1,0:T(8,128)S(1)} %get-tuple-element.33), channel_id=1, source_target_pairs={{0,1},{1,5},{2,3},{3,7},{4,0},{5,9},{6,2},{7,11},{8,4},{9,13},{10,... | collective-permute-start | bytes 294920 | tf_op jit(solution)/shard_map/ppermute | solution.py:586
  18.1 4.6 %collective-permute-start.4 = (f32[3,24,128]{2,1,0:T(8,128)S(1)}, f32[3,24,128]{2,1,0:T(8,128)S(1)}, u32[]{:S(2)}, u32[]{:S(2)}) collective-permute-start(f32[3,24,128]{2,1,0:T(8,128)S(1)} %get-tuple-element.34), channel_id=1, source_target_pairs={{0,8},{1,0},{2,10},{3,2},{4,12},{5,4},{6,14},{7,6},{8,16},{9,1},{1... | collective-permute-start | bytes 110600 | tf_op jit(solution)/shard_map/ppermute | solution.py:586
  21.1 4.0 %collective-permute-start.5 = (f32[3,24,128]{2,1,0:T(8,128)S(1)}, f32[3,24,128]{2,1,0:T(8,128)S(1)}, u32[]{:S(2)}, u32[]{:S(2)}) collective-permute-start(f32[3,24,128]{2,1,0:T(8,128)S(1)} %get-tuple-element.35), channel_id=1, source_target_pairs={{0,1},{1,9},{2,3},{3,11},{4,5},{5,13},{6,7},{7,15},{8,0},{9,17},{1... | collective-permute-start | bytes 110600 | tf_op jit(solution)/shard_map/ppermute | solution.py:586
  25.3 7.4 %collective-permute-start.6 = (f32[120,128]{1,0:T(8,128)S(1)}, f32[120,128]{1,0:T(8,128)S(1)}, u32[]{:S(2)}, u32[]{:S(2)}) collective-permute-start(f32[120,128]{1,0:T(8,128)S(1)} %get-tuple-element.40), channel_id=1, source_target_pairs={{0,4},{1,0},{2,6},{3,2},{4,8},{5,1},{6,10},{7,3},{8,12},{9,5},{10,... | collective-permute-start | bytes 184328 | tf_op jit(solution)/shard_map/ppermute | solution.py:586
  26.1 6.6 %collective-permute-start.7 = (f32[120,128]{1,0:T(8,128)S(1)}, f32[120,128]{1,0:T(8,128)S(1)}, u32[]{:S(2)}, u32[]{:S(2)}) collective-permute-start(f32[120,128]{1,0:T(8,128)S(1)} %get-tuple-element.41), channel_id=1, source_target_pairs={{0,1},{1,5},{2,3},{3,7},{4,0},{5,9},{6,2},{7,11},{8,4},{9,13},{10,... | collective-permute-start | bytes 184328 | tf_op jit(solution)/shard_map/ppermute | solution.py:586
  26.1 4.3 %collective-permute-start.8 = (f32[3,16,128]{2,1,0:T(8,128)S(1)}, f32[3,16,128]{2,1,0:T(8,128)S(1)}, u32[]{:S(2)}, u32[]{:S(2)}) collective-permute-start(f32[3,16,128]{2,1,0:T(8,128)S(1)} %get-tuple-element.42), channel_id=1, source_target_pairs={{0,8},{1,0},{2,10},{3,2},{4,12},{5,4},{6,14},{7,6},{8,16},{9,1},{1... | collective-permute-start | bytes 73736 | tf_op jit(solution)/shard_map/ppermute | solution.py:586
  28.9 3.8 %collective-permute-start.9 = (f32[3,16,128]{2,1,0:T(8,128)S(1)}, f32[3,16,128]{2,1,0:T(8,128)S(1)}, u32[]{:S(2)}, u32[]{:S(2)}) collective-permute-start(f32[3,16,128]{2,1,0:T(8,128)S(1)} %get-tuple-element.43), channel_id=1, source_target_pairs={{0,1},{1,9},{2,3},{3,11},{4,5},{5,13},{6,7},{7,15},{8,0},{9,17},{1... | collective-permute-start | bytes 73736 | tf_op jit(solution)/shard_map/ppermute | solution.py:586

commit v5 on v4

--- a/solution.py
+++ b/solution.py
@@ -80,13 +80,12 @@
     return quick_two_sum(p, e + (a[0] * b[1] + a[1] * b[0]))
 
 
-def dd_div(a, b):
-    inverse = 1.0 / b[0]
-    q1 = a[0] * inverse
-    zero = jnp.zeros_like(q1)
-    r = dd_sub(a, dd_mul((q1, zero), b))
-    q2 = r[0] * inverse
-    return quick_two_sum(q1, q2)
+def dd_scale(factor, b):
+    if isinstance(b, int):
+        return 0 if b == 0 else (b * factor, jnp.zeros_like(factor))
+    p = factor * b[0]
+    e = product_error(p, split(factor), split(b[0]))
+    return quick_two_sum(p, e + factor * b[1])
 
 
 def solve_block(values, inverses, ratios, lower_planes):
@@ -521,32 +520,42 @@
         for i in range(max(len(first), len(second))):
             item = first[i] if i < len(first) else 0
             if i < len(second):
-                item = dd_add(item, dd_mul(factor, second[i]))
+                item = dd_add(item, dd_scale(factor, second[i]))
             out.append(item)
         return out
 
+    def rounded(poly):
+        return [zero + item if isinstance(item, int) else item[0] for item in poly]
+
     residual = [1]
     direction = [1]
-    answer = []
     rho = entries[(0, 0)]
+    steps = []
     for iteration in range(ITERS):
         image = operate(direction)
-        alpha = dd_div(rho, with_shadow(image))
-        middle = combine(residual, dd_neg(alpha), image)
+        alpha = rho[0] / with_shadow(image)[0]
+        middle = combine(residual, -alpha, image)
         turned = operate(middle)
         weighted = gram_times(turned)
         cross = over_sublanes(dd_mul(weighted, stack(middle)))
         square = over_sublanes(dd_mul(weighted, stack(turned)))
-        omega = dd_div(cross, square)
-        answer = combine(answer, alpha, direction)
-        answer = combine(answer, omega, middle)
-        residual = combine(middle, dd_neg(omega), turned)
+        omega = cross[0] / square[0]
+        steps += [(alpha, rounded(direction)), (omega, rounded(middle))]
+        residual = combine(middle, -omega, turned)
         if iteration + 1 < ITERS:
             rho_next = with_shadow(residual)
-            factor = dd_mul(dd_div(rho_next, rho), dd_div(alpha, omega))
-            direction = combine(direction, dd_neg(omega), image)
+            factor = (rho_next[0] / rho[0]) * (alpha / omega)
+            direction = combine(direction, -omega, image)
             direction = combine(residual, factor, direction)
             rho = rho_next
+    residual = rounded(residual)
+    answer = []
+    for step, poly in steps:
+        for i, item in enumerate(poly):
+            if i == len(answer):
+                answer.append(step * item)
+            else:
+                answer[i] = answer[i] + step * item
     moves = []
     for c in range(COMPS):
         for n, (poly, basis, here, out) in enumerate(
@@ -555,7 +564,7 @@
                 (residual, values, residual_here, residual_out),
             )
         ):
-            scales = [item[0][:, c : c + 1] for item in poly]
+            scales = [item[:, c : c + 1] for item in poly]
             for k in range(planes):
                 for r in range(0, rows, 8):
                     total = scales[0] * basis[0][c, k, r : r + 8, :]
@@ -665,8 +674,10 @@
     values, solves = [value], [solved]
     first = None
     for iteration in range(ITERS):
-        near = [race(sent[0], 1), race(sent[1], -1)]
-        far = [race(sent[2], 2), race(sent[3], -2)]
+        near, far = [], []
+        for n, sign in enumerate((1, -1)):
+            near.append(race(sent[n], sign))
+            far.append(race(sent[2 + n], 2 * sign))
         first = first or near
         known = (solved, inner, *near, *far, *first, side, block)
         if iteration + 1 < ITERS:

time: 44 us -> 43.8 us (level)
  no operation moved by 1% of the time
where the time goes in v5:
time: 43.8 us; the launch traced here: 43.5 us
  starting transfers between devices  16.1 us (37%)
  waiting for transfers between devices  13.4 us (31%)
  blocking collectives  8.86 us (20%)
  Pallas kernels  4.42 us (10%)
  between operations  0.73 us (2%)
    all_to_all x1, blocking collectives, local(): gathered = lax.all_to_all(message, everyone, 0, 0, tiled=True)  8.86 us
    ppermute x8, waiting for transfers between devices, race(): return lax.ppermute(array, ('slab', 'batch'), sorted(pairs))  7.56 us
    all_to_all x1, starting transfers between devices, local(): received = lax.all_to_all(message, everyone, 0, 0, tiled=True)  7.33 us
    ppermute x8, starting transfers between devices, race(): return lax.ppermute(array, ('slab', 'batch'), sorted(pairs))  7.2 us
    all_to_all x1, waiting for transfers between devices, local(): received = lax.all_to_all(message, everyone, 0, 0, tiled=True)  5.83 us
    ppermute x2, starting transfers between devices, ring(): lax.ppermute(array, axis, [(i, (i + step) % count) for i in range(count)])  1.54 us
    pallas_call x1, Pallas kernels, local(): call(pack, (jax.ShapeDtypeStruct((slabs * copies, 8, tile), jnp.bfloat16)...  1.43 us
    pallas_call x1, Pallas kernels, local(): call(finish_kernel, (own, own), [VMEM] * (1 + BASIS + DEPTH), 4, [pltpu.V...  1.27 us
  transfers between devices with their start and end apart: 11, of which 5 were waited for; matrix products, arithmetic and copies ran while one was open for 0% of the time, Pallas kernels for 2%

profile of v5, /device:TPU:0, one launch (start us, length us, event | category | flops | bytes accessed | tf_op | source)
XLA Modules:
  0.0 43.5 jit_solution(7948918093869636238)
XLA Ops:
  0.6 1.4 %shard_map.69 = bf16[32,8,128]{2,1,0:T(8,128)(2,1)} custom-call(s32[8,128]{1,0:T(8,128)} %bitcast.8, f32[3,1024]{1,0:T(4,128)} %refs_1_.2, f32[8,128]{1,0:T(8,128)} %bitcast.9), custom_call_target="tpu_custom_call" | custom-call | tf_op jit(solution)/shard_map/pallas_call | solution.py:628
  2.1 0.0 copy-start
  2.1 0.0 copy-start.1
  2.1 7.3 %all-to-all-start = ((bf16[32,8,128]{2,1,0:T(8,128)(2,1)}), bf16[32,8,128]{2,1,0:T(8,128)(2,1)S(1)}, u32[]{:S(2)}, u32[]{:S(2)}) async-start(bf16[32,8,128]{2,1,0:T(8,128)(2,1)} %shard_map.69), calls=%async_computation | async-start | bytes 131072 | tf_op jit(solution)/shard_map/all_to_all | solution.py:645
  9.5 1.5 %collective-permute-start = (f32[6,2,4,128]{3,2,1,0:T(4,128)S(1)}, f32[6,2,4,128]{3,2,1,0:T(4,128)S(1)}, u32[]{:S(2)}, u32[]{:S(2)}) collective-permute-start(f32[6,2,4,128]{3,2,1,0:T(4,128)S(1)} %get-tuple-element.28), channel_id=1, source_target_pairs={{0,3},{1,0},{2,1},{3,2},{4,7},{5,4},{6,5},{7,6},{8,11},{9,8},{10,9... | collective-permute-start | bytes 73736 | tf_op jit(solution)/shard_map/ppermute | solution.py:582
  11.0 0.0 collective-permute-start.1
  11.0 5.8 %all-to-all-done.refs_0_ = bf16[32,8,128]{2,1,0:T(8,128)(2,1)S(1)} async-done(((bf16[32,8,128]{2,1,0:T(8,128)(2,1)}), bf16[32,8,128]{2,1,0:T(8,128)(2,1)S(1)}, u32[]{:S(2)}, u32[]{:S(2)}) %all-to-all-start) | async-done | bytes 65568 | tf_op jit(solution)/shard_map/all_to_all | solution.py:645
  16.8 0.5 %shard_map.70.refs_4_ = f32[144,128]{1,0:T(8,128)S(1)} custom-call(bf16[32,8,128]{2,1,0:T(8,128)(2,1)S(1)} %all-to-all-done.refs_0_), custom_call_target="tpu_custom_call" | custom-call | tf_op jit(solution)/shard_map/pallas_call | solution.py:653
  17.3 0.0 collective-permute-done.refs_2_
  17.3 0.0 collective-permute-done.1.refs_3_
  17.3 0.1 shard_map.71
  17.5 0.7 %collective-permute-start.2 = (f32[192,128]{1,0:T(8,128)S(1)}, f32[192,128]{1,0:T(8,128)S(1)}, u32[]{:S(2)}, u32[]{:S(2)}) collective-permute-start(f32[192,128]{1,0:T(8,128)S(1)} %get-tuple-element.32), channel_id=1, source_target_pairs={{0,4},{1,0},{2,6},{3,2},{4,8},{5,1},{6,10},{7,3},{8,12},{9,5},{10,... | collective-permute-start | bytes 294920 | tf_op jit(solution)/shard_map/ppermute | solution.py:595
  18.1 0.0 collective-permute-start.3
  18.1 2.9 %collective-permute-start.4 = (f32[3,24,128]{2,1,0:T(8,128)S(1)}, f32[3,24,128]{2,1,0:T(8,128)S(1)}, u32[]{:S(2)}, u32[]{:S(2)}) collective-permute-start(f32[3,24,128]{2,1,0:T(8,128)S(1)} %get-tuple-element.34), channel_id=1, source_target_pairs={{0,8},{1,0},{2,10},{3,2},{4,12},{5,4},{6,14},{7,6},{8,16},{9,1},{1... | collective-permute-start | bytes 110600 | tf_op jit(solution)/shard_map/ppermute | solution.py:595
  21.1 0.0 collective-permute-start.5
  21.1 1.6 %collective-permute-done.4.far1 = f32[3,24,128]{2,1,0:T(8,128)S(1)} collective-permute-done((f32[3,24,128]{2,1,0:T(8,128)S(1)}, f32[3,24,128]{2,1,0:T(8,128)S(1)}, u32[]{:S(2)}, u32[]{:S(2)}) %collective-permute-start.4) | collective-permute-done | bytes 36896 | tf_op jit(solution)/shard_map/ppermute | solution.py:595
  22.7 2.3 %collective-permute-done.5.far2 = f32[3,24,128]{2,1,0:T(8,128)S(1)} collective-permute-done((f32[3,24,128]{2,1,0:T(8,128)S(1)}, f32[3,24,128]{2,1,0:T(8,128)S(1)}, u32[]{:S(2)}, u32[]{:S(2)}) %collective-permute-start.5) | collective-permute-done | bytes 36896 | tf_op jit(solution)/shard_map/ppermute | solution.py:595
  25.0 0.0 collective-permute-done.2.near1.first1.refs_6_
  25.0 0.0 collective-permute-done.3.near2.first2.refs_7_
  25.0 0.2 shard_map.72
  25.3 0.9 %collective-permute-start.6 = (f32[120,128]{1,0:T(8,128)S(1)}, f32[120,128]{1,0:T(8,128)S(1)}, u32[]{:S(2)}, u32[]{:S(2)}) collective-permute-start(f32[120,128]{1,0:T(8,128)S(1)} %get-tuple-element.40), channel_id=1, source_target_pairs={{0,4},{1,0},{2,6},{3,2},{4,8},{5,1},{6,10},{7,3},{8,12},{9,5},{10,... | collective-permute-start | bytes 184328 | tf_op jit(solution)/shard_map/ppermute | solution.py:595
  26.1 0.0 collective-permute-start.7
  26.1 2.7 %collective-permute-start.8 = (f32[3,16,128]{2,1,0:T(8,128)S(1)}, f32[3,16,128]{2,1,0:T(8,128)S(1)}, u32[]{:S(2)}, u32[]{:S(2)}) collective-permute-start(f32[3,16,128]{2,1,0:T(8,128)S(1)} %get-tuple-element.42), channel_id=1, source_target_pairs={{0,8},{1,0},{2,10},{3,2},{4,12},{5,4},{6,14},{7,6},{8,16},{9,1},{1... | collective-permute-start | bytes 73736 | tf_op jit(solution)/shard_map/ppermute | solution.py:595
  28.9 0.0 collective-permute-start.9
  28.9 0.2 shard_map.73
  29.1 1.3 %collective-permute-done.8.refs_4_ = f32[3,16,128]{2,1,0:T(8,128)S(1)} collective-permute-done((f32[3,16,128]{2,1,0:T(8,128)S(1)}, f32[3,16,128]{2,1,0:T(8,128)S(1)}, u32[]{:S(2)}, u32[]{:S(2)}) %collective-permute-start.8) | collective-permute-done | bytes 24608 | tf_op jit(solution)/shard_map/ppermute | solution.py:595
  30.4 2.3 %collective-permute-done.9.refs_5_ = f32[3,16,128]{2,1,0:T(8,128)S(1)} collective-permute-done((f32[3,16,128]{2,1,0:T(8,128)S(1)}, f32[3,16,128]{2,1,0:T(8,128)S(1)}, u32[]{:S(2)}, u32[]{:S(2)}) %collective-permute-start.9) | collective-permute-done | bytes 24608 | tf_op jit(solution)/shard_map/ppermute | solution.py:595
  32.7 0.0 collective-permute-done.6.refs_2_
  32.7 0.0 collective-permute-done.7.refs_3_
  32.7 0.7 %shard_map.74 = (f32[3,2,24,128]{3,2,1,0:T(8,128)S(1)}, f32[3,2,24,128]{3,2,1,0:T(8,128)S(1)}, f32[3,2,24,128]{3,2,1,0:T(8,128)S(1)}, f32[32,128]{1,0:T(8,128)S(1)}) custom-call(f32[3,2,24,128]{3,2,1,0:T(8,128)S(1)} %get-tuple-element.38.refs_0_.refs_8_, f32[3,2,24,128]{3,2,1,0:T(8,128)S(1)} %get-tuple-element.39.refs_1_, ...), custom_call_target="tpu_custom_call" | custom-call | tf_op jit(solution)/shard_map/pallas_call | solution.py:697
  33.4 8.9 %all_to_all.16 = f32[32,1,128]{2,1,0:T(1,128)S(1)} all-to-all(f32[32,1,128]{2,1,0:T(1,128)S(1)} %bitcast.7), channel_id=1, replica_groups=mesh['slab'=8,'batch'=4] {'slab','batch'}, dimensions={0} | all-to-all | bytes 32768 | tf_op jit(solution)/shard_map/all_to_all | solution.py:702
  42.2 1.3 %shard_map.75 = (f32[3,2,16,128]{3,2,1,0:T(8,128)}, f32[3,2,16,128]{3,2,1,0:T(8,128)}) custom-call(f32[32,128]{1,0:T(8,128)S(1)} %bitcast.6, f32[3,2,24,128]{3,2,1,0:T(8,128)S(1)} %get-tuple-element.44.refs_0_.refs_10_.refs_1_, f32[3,2,24,128]{3,2,1,0:T(8,128)S(1)} %get-tuple-element.45.refs_1_.refs_11_.refs_2_, ...), custom_call_target="tpu_custom_call" | custom-call | tf_op jit(solution)/shard_map/pallas_call | solution.py:703
  (3 shorter events, 0.0 us)
Async XLA Ops:
  2.1 7.4 %copy-start = (f32[3,2,16,128]{3,2,1,0:T(8,128)S(1)}, f32[3,2,16,128]{3,2,1,0:T(8,128)}, u32[]{:S(2)}) copy-start(f32[3,2,16,128]{3,2,1,0:T(8,128)} %refs_0_.1) | copy-start | bytes 147460
  2.1 7.4 %copy-start.1 = (f32[3,2,16,128]{3,2,1,0:T(8,128)S(1)}, f32[3,2,16,128]{3,2,1,0:T(8,128)}, u32[]{:S(2)}) copy-start(f32[3,2,16,128]{3,2,1,0:T(8,128)} %refs_1_.3) | copy-start | bytes 147460
  2.1 14.7 %all-to-all-start = ((bf16[32,8,128]{2,1,0:T(8,128)(2,1)}), bf16[32,8,128]{2,1,0:T(8,128)(2,1)S(1)}, u32[]{:S(2)}, u32[]{:S(2)}) async-start(bf16[32,8,128]{2,1,0:T(8,128)(2,1)} %shard_map.69), calls=%async_computation | async-start | bytes 131072 | tf_op jit(solution)/shard_map/all_to_all | solution.py:645
  9.5 7.9 %collective-permute-start = (f32[6,2,4,128]{3,2,1,0:T(4,128)S(1)}, f32[6,2,4,128]{3,2,1,0:T(4,128)S(1)}, u32[]{:S(2)}, u32[]{:S(2)}) collective-permute-start(f32[6,2,4,128]{3,2,1,0:T(4,128)S(1)} %get-tuple-element.28), channel_id=1, source_target_pairs={{0,3},{1,0},{2,1},{3,2},{4,7},{5,4},{6,5},{7,6},{8,11},{9,8},{10,9... | collective-permute-start | bytes 73736 | tf_op jit(solution)/shard_map/ppermute | solution.py:582
  11.0 6.3 %collective-permute-start.1 = (f32[6,2,4,128]{3,2,1,0:T(4,128)S(1)}, f32[6,2,4,128]{3,2,1,0:T(4,128)S(1)}, u32[]{:S(2)}, u32[]{:S(2)}) collective-permute-start(f32[6,2,4,128]{3,2,1,0:T(4,128)S(1)} %get-tuple-element.29), channel_id=1, source_target_pairs={{0,1},{1,2},{2,3},{3,0},{4,5},{5,6},{6,7},{7,4},{8,9},{9,10},{10,1... | collective-permute-start | bytes 73736 | tf_op jit(solution)/shard_map/ppermute | solution.py:582
  17.5 7.6 %collective-permute-start.2 = (f32[192,128]{1,0:T(8,128)S(1)}, f32[192,128]{1,0:T(8,128)S(1)}, u32[]{:S(2)}, u32[]{:S(2)}) collective-permute-start(f32[192,128]{1,0:T(8,128)S(1)} %get-tuple-element.32), channel_id=1, source_target_pairs={{0,4},{1,0},{2,6},{3,2},{4,8},{5,1},{6,10},{7,3},{8,12},{9,5},{10,... | collective-permute-start | bytes 294920 | tf_op jit(solution)/shard_map/ppermute | solution.py:595
  18.1 6.9 %collective-permute-start.3 = (f32[192,128]{1,0:T(8,128)S(1)}, f32[192,128]{1,0:T(8,128)S(1)}, u32[]{:S(2)}, u32[]{:S(2)}) collective-permute-start(f32[192,128]{1,0:T(8,128)S(1)} %get-tuple-element.33), channel_id=1, source_target_pairs={{0,1},{1,5},{2,3},{3,7},{4,0},{5,9},{6,2},{7,11},{8,4},{9,13},{10,... | collective-permute-start | bytes 294920 | tf_op jit(solution)/shard_map/ppermute | solution.py:595
  18.1 4.6 %collective-permute-start.4 = (f32[3,24,128]{2,1,0:T(8,128)S(1)}, f32[3,24,128]{2,1,0:T(8,128)S(1)}, u32[]{:S(2)}, u32[]{:S(2)}) collective-permute-start(f32[3,24,128]{2,1,0:T(8,128)S(1)} %get-tuple-element.34), channel_id=1, source_target_pairs={{0,8},{1,0},{2,10},{3,2},{4,12},{5,4},{6,14},{7,6},{8,16},{9,1},{1... | collective-permute-start | bytes 110600 | tf_op jit(solution)/shard_map/ppermute | solution.py:595
  21.1 4.0 %collective-permute-start.5 = (f32[3,24,128]{2,1,0:T(8,128)S(1)}, f32[3,24,128]{2,1,0:T(8,128)S(1)}, u32[]{:S(2)}, u32[]{:S(2)}) collective-permute-start(f32[3,24,128]{2,1,0:T(8,128)S(1)} %get-tuple-element.35), channel_id=1, source_target_pairs={{0,1},{1,9},{2,3},{3,11},{4,5},{5,13},{6,7},{7,15},{8,0},{9,17},{1... | collective-permute-start | bytes 110600 | tf_op jit(solution)/shard_map/ppermute | solution.py:595
  25.3 7.4 %collective-permute-start.6 = (f32[120,128]{1,0:T(8,128)S(1)}, f32[120,128]{1,0:T(8,128)S(1)}, u32[]{:S(2)}, u32[]{:S(2)}) collective-permute-start(f32[120,128]{1,0:T(8,128)S(1)} %get-tuple-element.40), channel_id=1, source_target_pairs={{0,4},{1,0},{2,6},{3,2},{4,8},{5,1},{6,10},{7,3},{8,12},{9,5},{10,... | collective-permute-start | bytes 184328 | tf_op jit(solution)/shard_map/ppermute | solution.py:595
  26.1 6.6 %collective-permute-start.7 = (f32[120,128]{1,0:T(8,128)S(1)}, f32[120,128]{1,0:T(8,128)S(1)}, u32[]{:S(2)}, u32[]{:S(2)}) collective-permute-start(f32[120,128]{1,0:T(8,128)S(1)} %get-tuple-element.41), channel_id=1, source_target_pairs={{0,1},{1,5},{2,3},{3,7},{4,0},{5,9},{6,2},{7,11},{8,4},{9,13},{10,... | collective-permute-start | bytes 184328 | tf_op jit(solution)/shard_map/ppermute | solution.py:595
  26.1 4.3 %collective-permute-start.8 = (f32[3,16,128]{2,1,0:T(8,128)S(1)}, f32[3,16,128]{2,1,0:T(8,128)S(1)}, u32[]{:S(2)}, u32[]{:S(2)}) collective-permute-start(f32[3,16,128]{2,1,0:T(8,128)S(1)} %get-tuple-element.42), channel_id=1, source_target_pairs={{0,8},{1,0},{2,10},{3,2},{4,12},{5,4},{6,14},{7,6},{8,16},{9,1},{1... | collective-permute-start | bytes 73736 | tf_op jit(solution)/shard_map/ppermute | solution.py:595
  28.9 3.8 %collective-permute-start.9 = (f32[3,16,128]{2,1,0:T(8,128)S(1)}, f32[3,16,128]{2,1,0:T(8,128)S(1)}, u32[]{:S(2)}, u32[]{:S(2)}) collective-permute-start(f32[3,16,128]{2,1,0:T(8,128)S(1)} %get-tuple-element.43), channel_id=1, source_target_pairs={{0,1},{1,9},{2,3},{3,11},{4,5},{5,13},{6,7},{7,15},{8,0},{9,17},{1... | collective-permute-start | bytes 73736 | tf_op jit(solution)/shard_map/ppermute | solution.py:595

commit v6 on v5

--- a/solution.py
+++ b/solution.py
@@ -100,16 +100,25 @@
     return result
 
 
-def pack_kernel(slabs, copies, ids_in, forces_in, weights_in, message_out, ids, forces, weights, arrived):
+def pack_kernel(
+    slabs, copies, ids_in, forces_in, weights_in, velocity_in, courant_in,
+    message_out, fields_out, ids, forces, weights, arrived,
+):
     moves = [
         pltpu.make_async_copy(source, target, arrived.at[n])
         for n, (source, target) in enumerate(
-            [(ids_in, ids), (weights_in, weights), (forces_in, forces)]
+            [
+                (ids_in, ids),
+                (weights_in, weights),
+                (forces_in, forces),
+                (velocity_in, fields_out.at[0]),
+                (courant_in, fields_out.at[1]),
+            ]
         )
     ]
     for move in moves:
         move.start()
-    for move in moves:
+    for move in moves[:3]:
         move.wait()
     tile = ids.shape[1]
     width = 128
@@ -117,27 +126,39 @@
     low = ids[...] - high * width
     rest = [high.astype(F32), low.astype(F32)]
     rest += [jnp.zeros_like(rest[0])] * (8 - COMPS - len(rest))
-    for s in range(slabs):
-        at = slice(s * tile, (s + 1) * tile)
-        block = jnp.concatenate(
-            [forces[:, at] * weights[s : s + 1]] + [part[s : s + 1] for part in rest], axis=0
-        )
-        for k in range(copies):
-            message_out[s * copies + k] = block.astype(jnp.bfloat16)
-
-
-def edges_kernel(velocity, courant, first_out, last_out):
-    rows = velocity.shape[2]
-    for n, field in enumerate((velocity, courant)):
-        first_out[n * COMPS : (n + 1) * COMPS] = field[:, :, :DEPTH]
-        last_out[n * COMPS : (n + 1) * COMPS] = field[:, :, rows - DEPTH :]
+    for pair in range(0, slabs, 2):
+        blocks = []
+        for s in (pair, pair + 1):
+            at = slice(s * tile, (s + 1) * tile)
+            blocks += [forces[:, at] * weights[s : s + 1]] + [part[s : s + 1] for part in rest]
+        block = jnp.concatenate(blocks, axis=0).astype(jnp.bfloat16)
+        for k in range(2 * copies):
+            message_out[pair * copies + k] = block
+    for move in moves[3:]:
+        move.wait()
+
+
+def own_block():
+    return lax.axis_index("slab") % 2
+
+
+def edges_kernel(here, beside, first_out, last_out):
+    rows = here.shape[3]
+    own = own_block()
+    for block in range(2):
+        for n in range(2):
+            for d in range(COMPS):
+                for out, at in ((first_out, slice(0, DEPTH)), (last_out, slice(rows - DEPTH, rows))):
+                    out[block, n * COMPS + d] = jnp.where(
+                        own == block, here[n, d, :, at], beside[n, d, :, at]
+                    )
 
 
 def deposit_kernel(rows, copies, group, message, momentum_sum):
     wide = rows + 2 * DEPTH
     height = rows * copies
-    planes = momentum_sum.shape[0] // (COMPS * wide)
-    width = momentum_sum.shape[1]
+    planes = momentum_sum.shape[1] // (COMPS * wide)
+    width = momentum_sum.shape[2]
     start = lax.axis_index("batch") * rows
     tile = message.shape[2]
     narrow = jnp.bfloat16
@@ -149,10 +170,10 @@
     def over_sixteen(row):
         return jnp.broadcast_to(row, (16, tile)).astype(narrow)
 
-    def deposit(step):
+    def deposit(block, step):
         row_values, column_hot = [], []
         for k in range(group):
-            part = message[step * group + k].astype(F32)
+            part = message[step * group + k, 8 * block : 8 * block + 8].astype(F32)
             cell_row = part[3:4].astype(jnp.int32)
             plane = jnp.zeros_like(cell_row)
             for p in range(1, planes):
@@ -181,19 +202,20 @@
         )
 
     steps = message.shape[0] // group
-    if steps <= 4:
-        total = deposit(0)
-        for step in range(1, steps):
-            total = total + deposit(step)
-        momentum_sum[...] = total
-    else:
-        momentum_sum[...] = jnp.zeros_like(momentum_sum)
-
-        def add_step(step, carry):
-            momentum_sum[...] += deposit(step)
-            return carry
-
-        lax.fori_loop(0, steps, add_step, 0)
+    for block in range(2):
+        if steps <= 4:
+            total = deposit(block, 0)
+            for step in range(1, steps):
+                total = total + deposit(block, step)
+            momentum_sum[block] = total
+        else:
+            momentum_sum[block] = jnp.zeros(momentum_sum.shape[1:], F32)
+
+            def add_step(step, carry):
+                momentum_sum[block] += deposit(block, step)
+                return carry
+
+            lax.fori_loop(0, steps, add_step, 0)
 
 
 def fill_coefficients(courant, slab, slabs, batch, copies, rows, side, block):
@@ -244,68 +266,105 @@
     return values
 
 
-def add_outside(values, below, above, block):
-    values = list(values)
-    values[0] = values[0] + block[3, 0] * below
-    values[-1] = values[-1] + block[3, 1] * above
-    return values
-
-
-def store_messages(c, solved, nearby, rows, even, near_out, far_out):
-    wide = solved[0].shape[0]
-    one, other = (jnp.where(even, x[-1], x[0]) for x in (solved, nearby))
-    at, beside = (jnp.where(even, x[0], x[-1]) for x in (solved, nearby))
-    for n, (face, part) in enumerate(((one, other), (at, beside))):
-        near_out[n][c * wide : (c + 1) * wide] = face
-        start = COMPS * wide + c * rows
-        near_out[n][start : start + rows] = part[:rows]
-        far_out[n][c] = face[: far_out[n].shape[1]]
+def add_below(values, face, block):
+    return [values[0] + block[3, 0] * face] + list(values[1:])
+
+
+def add_above(values, face, block):
+    return list(values[:-1]) + [values[-1] + block[3, 1] * face]
+
+
+def inside_pair(lower, upper, side, block):
+    return (
+        add_above(in_plane(lower, side.at[0]), upper[0], block.at[0]),
+        add_below(in_plane(upper, side.at[1]), lower[-1], block.at[1]),
+    )
+
+
+def store_pair(c, pair, out):
+    for n, values in enumerate(pair):
+        for k, item in enumerate(values):
+            out[n, c, k] = item
+
+
+def store_own(c, pair, out):
+    own = own_block()
+    for k, (one, other) in enumerate(zip(*pair)):
+        out[c, k] = jnp.where(own == 0, one, other)
+
+
+def store_messages(c, solved, inner, block, rows, near_out):
+    even = lax.axis_index("batch") % 2 == 0
+    wide = solved[0][0].shape[0]
+    up = (solved[1][-1], solve(inner[1], block.at[1])[-1])
+    down = (solved[0][0], solve(inner[0], block.at[0])[0])
+    start = COMPS * wide + c * rows
+    for n, (one, other) in enumerate(((up, down), (down, up))):
+        near_out[n][c * wide : (c + 1) * wide] = jnp.where(even, one[0], other[0])
+        near_out[n][start : start + rows] = jnp.where(even, one[1], other[1])[:rows]
 
 
 def setup_kernel(
-    slabs, copies, velocity, courant, after, before, momentum_sum,
-    value_out, solved_out, inner_out, near1, near2, far1, far2, side, block, wide_courant,
+    slabs, copies,
+    here, beside, after, before, momentum_sum,
+    value_out, own_out, solved_out, inner_out, near1, near2, side, block, wide_courant,
 ):
-    planes, rows, width = velocity.shape[1:]
+    planes, rows, width = here.shape[2:]
     wide = rows + 2 * DEPTH
     batch = lax.axis_index("batch")
     even = batch % 2 == 0
-    for d in range(3):
-        for k in range(planes):
-            wide_courant[d, k] = jnp.concatenate(
-                [courant[d, k], after[COMPS + d, k], before[COMPS + d, k]], axis=0
-            )
-    fill_coefficients(
-        lambda d, k: wide_courant[d, k],
-        lax.axis_index("slab"), slabs, batch, copies, rows, side, block,
-    )
+    slab, own = lax.axis_index("slab"), own_block()
+    for n in range(2):
+        for d in range(3):
+            for k in range(planes):
+                wide_courant[n, d, k] = jnp.concatenate(
+                    [
+                        jnp.where(own == n, here[1, d, k], beside[1, d, k]),
+                        after[n, COMPS + d, k],
+                        before[n, COMPS + d, k],
+                    ],
+                    axis=0,
+                )
+        fill_coefficients(
+            lambda d, k: wide_courant[n, d, k],
+            slab - own + n, slabs, batch, copies, rows, side.at[n], block.at[n],
+        )
     zero = jnp.zeros((wide, width), F32)
-    from_below = solve([block[3, 0]] + [zero] * (planes - 1), block)
-    from_above = solve([zero] * (planes - 1) + [block[3, 1]], block)
-    start = 2 * COMPS * wide
-    for n, part in enumerate((from_below, from_above)):
-        at = slice(start + n * wide, start + (n + 1) * wide)
-        near1[at] = jnp.where(even, part[-1], part[0])
-        near2[at] = jnp.where(even, part[0], part[-1])
+    from_below = solve([block[0, 3, 0]] + [zero] * (planes - 1), block.at[0])[0]
+    from_above = solve([zero] * (planes - 1) + [block[1, 3, 1]], block.at[1])[-1]
+    at = slice(2 * COMPS * wide, (2 * COMPS + 1) * wide)
+    near1[at] = jnp.where(even, from_above, from_below)
+    near2[at] = jnp.where(even, from_below, from_above)
     for c in range(COMPS):
-        values = []
-        for k in range(planes):
-            old = jnp.concatenate([velocity[c, k], after[c, k], before[c, k]], axis=0)
-            at = (c * planes + k) * wide
-            value = old + momentum_sum[at : at + wide]
-            value_out[c, k] = value
-            values.append(value)
-        solved = solve(values, block)
-        inner = in_plane(solved, side)
-        for k in range(planes):
-            solved_out[c, k] = solved[k]
-            inner_out[c, k] = inner[k]
-        store_messages(c, solved, solve(inner, block), wide, even, (near1, near2), (far1, far2))
-
-
-def two_levels(solved, inner, near1, near2, far1, far2, first1, first2, side, block):
-    planes, wide = solved.shape[1:3]
-    rows = far1.shape[1]
+        pair, solved = [], []
+        for n in range(2):
+            values = []
+            for k in range(planes):
+                old = jnp.concatenate(
+                    [
+                        jnp.where(own == n, here[0, c, k], beside[0, c, k]),
+                        after[n, c, k],
+                        before[n, c, k],
+                    ],
+                    axis=0,
+                )
+                at = (c * planes + k) * wide
+                values.append(old + momentum_sum[n, at : at + wide])
+            pair.append(values)
+            solved.append(solve(values, block.at[n]))
+        inner = inside_pair(*solved, side, block)
+        store_own(c, pair, value_out)
+        store_own(c, solved, own_out)
+        store_pair(c, solved, solved_out)
+        store_pair(c, inner, inner_out)
+        store_messages(c, solved, inner, block, wide, (near1, near2))
+
+
+def next_level(solved, inner, near1, near2, first1, first2, block):
+    planes, wide = solved.shape[2:4]
+    rows = near1.shape[0] // COMPS - wide
+    if near1 is first1:
+        rows = wide
     even = lax.axis_index("batch") % 2 == 0
 
     def low(one, other):
@@ -318,56 +377,53 @@
         at = slice(start, start + count)
         return pick(near1[at], near2[at])
 
-    def response(pick, n):
-        at = slice((2 * COMPS + n) * wide, (2 * COMPS + n) * wide + rows)
-        return pick(first1[at], first2[at])
-
-    low_below, low_above = response(low, 0), response(low, 1)
-    high_below, high_above = response(high, 0), response(high, 1)
-    pad = jnp.zeros((wide - rows, solved.shape[3]), F32)
+    at = slice(2 * COMPS * wide, 2 * COMPS * wide + rows)
+    low_response, high_response = (pick(first1[at], first2[at]) for pick in (low, high))
+    pad = jnp.zeros((wide - rows, solved.shape[4]), F32)
 
     def widen(x):
         return x if rows == wide else jnp.concatenate([x, pad], axis=0)
 
     for c in range(COMPS):
         own = COMPS * wide + c * rows
-        below, above = part(low, c * wide, wide), part(high, c * wide, wide)
-        one = add_outside([inner[c, k] for k in range(planes)], below, above, block)
-        one_solved = solve(one, block)
-        next_below = (
-            part(low, own, rows)
-            + low_above * solved[c, 0][:rows]
-            + low_below * low(far1[c], far2[c])
+        lower = [inner[0, c, k] for k in range(planes)]
+        upper = [inner[1, c, k] for k in range(planes)]
+        one = (
+            add_below(lower, part(low, c * wide, wide), block.at[0]),
+            add_above(upper, part(high, c * wide, wide), block.at[1]),
         )
-        next_above = (
-            part(high, own, rows)
-            + high_below * solved[c, planes - 1][:rows]
-            + high_above * high(far1[c], far2[c])
+        one_solved = tuple(solve(one[n], block.at[n]) for n in range(2))
+        below = part(low, own, rows) + low_response * solved[0, c, 0][:rows]
+        above = part(high, own, rows) + high_response * solved[1, c, planes - 1][:rows]
+        yield c, one, one_solved, widen(below), widen(above)
+
+
+def advance_kernel(
+    repeat, *refs,
+):
+    solved, inner, near1, near2, first1, first2, side, block = refs[:8]
+    if repeat:
+        first1, first2 = near1, near2
+    value_out, own_out, second_out, last_out, solved_out, inner_out, to1, to2 = refs[8:]
+    wide = solved.shape[3]
+    rows = to1.shape[0] // COMPS - wide
+    for c, one, one_solved, below, above in next_level(
+        solved, inner, near1, near2, first1, first2, block
+    ):
+        within = inside_pair(*one_solved, side, block)
+        two = (
+            add_below(within[0], below, block.at[0]),
+            add_above(within[1], above, block.at[1]),
         )
-        two = add_outside(
-            in_plane(one_solved, side), widen(next_below), widen(next_above), block
-        )
-        yield c, one, one_solved, two
-
-
-def advance_kernel(
-    solved, inner, near1, near2, far1, far2, first1, first2, side, block,
-    value_out, solved_out, second_out, last_out, inner_out, to1, to2, beyond1, beyond2,
-):
-    even = lax.axis_index("batch") % 2 == 0
-    for c, one, one_solved, two in two_levels(
-        solved, inner, near1, near2, far1, far2, first1, first2, side, block
-    ):
-        two_solved = solve(two, block)
-        within = in_plane(two_solved, side)
-        for k in range(len(one)):
-            value_out[c, k] = one[k]
-            solved_out[c, k] = one_solved[k]
-            second_out[c, k] = two[k]
-            last_out[c, k] = two_solved[k]
-            inner_out[c, k] = within[k]
-        rows = beyond1.shape[1]
-        store_messages(c, two_solved, solve(within, block), rows, even, (to1, to2), (beyond1, beyond2))
+        two_solved = tuple(solve(two[n], block.at[n]) for n in range(2))
+        inner_next = inside_pair(*two_solved, side, block)
+        store_own(c, one, value_out)
+        store_own(c, one_solved, own_out)
+        store_own(c, two, second_out)
+        store_own(c, two_solved, last_out)
+        store_pair(c, two_solved, solved_out)
+        store_pair(c, inner_next, inner_out)
+        store_messages(c, two_solved, inner_next, block, rows, (to1, to2))
 
 
 def gram_sums(pieces, pairs, totals):
@@ -402,14 +458,23 @@
 
 
 def gram_kernel(*refs):
-    known = refs[:10]
-    values = refs[10 : 10 + EARLY]
-    early = refs[10 + EARLY : 12 + EARLY]
-    value_out, solved_out, second_out, message_out = refs[12 + EARLY :]
+    solved, inner, near1, near2, first1, first2, side, block = refs[:8]
+    values = refs[8 : 8 + EARLY]
+    early = refs[8 + EARLY : 10 + EARLY]
+    value_out, solved_out, second_out, message_out = refs[10 + EARLY :]
+    own = own_block()
     planes, wide, width = value_out.shape[1:]
     rows = wide - 2 * DEPTH
     sums = []
-    for c, one, one_solved, two in two_levels(*known):
+    for c, ones, one_pair, below, above in next_level(
+        solved, inner, near1, near2, first1, first2, block
+    ):
+        one, one_solved = (
+            [jnp.where(own == 0, x, y) for x, y in zip(*pair)] for pair in (ones, one_pair)
+        )
+        two = in_plane(one_solved, side.at[own])
+        two = add_below(two, jnp.where(own == 0, below, one_pair[0][-1]), block.at[own])
+        two = add_above(two, jnp.where(own == 0, one_pair[1][0], above), block.at[own])
         totals = [None] * len(LATE_PAIRS)
         for k in range(planes):
             value_out[c, k] = one[k]
@@ -602,11 +667,12 @@
     wide = rows + 2 * DEPTH
     height = rows * copies
     tile = cell_ids.shape[0] // slabs
-    assert rows % 8 == 0 and width == 128 and copies % 2 == 0
+    assert rows % 8 == 0 and width == 128 and copies % 2 == 0 and slabs % 2 == 0
     assert planes * height <= 256 and 2 * DEPTH <= height - rows
     field = jax.ShapeDtypeStruct((COMPS, planes, wide, width), F32)
-    quad = jax.ShapeDtypeStruct((4, planes, wide, width), F32)
-    edge = jax.ShapeDtypeStruct((2 * COMPS, planes, DEPTH, width), F32)
+    quad = jax.ShapeDtypeStruct((2, 4, planes, wide, width), F32)
+    both = jax.ShapeDtypeStruct((2, COMPS, planes, wide, width), F32)
+    edge = jax.ShapeDtypeStruct((2, 2 * COMPS, planes, DEPTH, width), F32)
     own = jax.ShapeDtypeStruct(velocity_old.shape, F32)
 
     def call(kernel, out_shape, in_specs, mib, scratch=(), out_space=VMEM, cost=None):
@@ -625,25 +691,35 @@
     def pack(*refs):
         pack_kernel(slabs, copies, *refs)
 
-    (message,) = call(
+    message, fields = call(
         pack,
-        (jax.ShapeDtypeStruct((slabs * copies, 8, tile), jnp.bfloat16),),
-        [ANY] * 3,
+        (
+            jax.ShapeDtypeStruct((slabs * copies, 16, tile), jnp.bfloat16),
+            jax.ShapeDtypeStruct((2, *velocity_old.shape), F32),
+        ),
+        [ANY] * 5,
         8,
         [
             pltpu.VMEM((slabs, tile), jnp.int32),
             pltpu.VMEM(forces.shape, F32),
             pltpu.VMEM((slabs, tile), F32),
-            pltpu.SemaphoreType.DMA((3,)),
+            pltpu.SemaphoreType.DMA((5,)),
         ],
     )(
         *(
             pltpu.with_memory_space_constraint(x, pltpu.HBM)
-            for x in (cell_ids.reshape(slabs, tile), forces, weights.reshape(slabs, tile))
+            for x in (
+                cell_ids.reshape(slabs, tile),
+                forces,
+                weights.reshape(slabs, tile),
+                velocity_old,
+                courant,
+            )
         )
     )
+    beside = lax.ppermute(fields, "slab", [(s, s ^ 1) for s in range(slabs)])
     received = lax.all_to_all(message, everyone, 0, 0, tiled=True)
-    first, last = call(edges_kernel, (edge, edge), [VMEM] * 2, 2)(velocity_old, courant)
+    first, last = call(edges_kernel, (edge, edge), [VMEM] * 2, 2)(fields, beside)
     after = ring(first, "batch", -1)
     before = ring(last, "batch", 1)
 
@@ -651,7 +727,7 @@
         deposit_kernel(rows, copies, 8, *refs)
 
     (deposited,) = call(
-        deposit, (jax.ShapeDtypeStruct((COMPS * planes * wide, width), F32),), [VMEM], 12
+        deposit, (jax.ShapeDtypeStruct((2, COMPS * planes * wide, width), F32),), [VMEM], 12
     )(received)
 
     def setup(*refs):
@@ -660,42 +736,42 @@
     def flat(count):
         return jax.ShapeDtypeStruct((count, width), F32)
 
-    def faces(count):
-        return jax.ShapeDtypeStruct((COMPS, count, width), F32)
-
-    value, solved, inner, *sent, side, block = call(
+    value, own_solved, solved, inner, *sent, side, block = call(
         setup,
-        (field,) * 3 + (flat((2 * COMPS + 2) * wide),) * 2 + (faces(wide),) * 2 + (quad,) * 2,
+        (field,) * 2 + (both,) * 2 + (flat((2 * COMPS + 1) * wide),) * 2 + (quad,) * 2,
         [VMEM] * 5,
         2,
-        [pltpu.VMEM((3, planes, wide, width), F32)],
-    )(velocity_old, courant, after, before, deposited)
-
-    values, solves = [value], [solved]
+        [pltpu.VMEM((2, 3, planes, wide, width), F32)],
+    )(fields, beside, after, before, deposited)
+
+    values, solves = [value], [own_solved]
     first = None
     for iteration in range(ITERS):
-        near, far = [], []
-        for n, sign in enumerate((1, -1)):
-            near.append(race(sent[n], sign))
-            far.append(race(sent[2 + n], 2 * sign))
+        near = [race(sent[0], 2), race(sent[1], -2)]
+        repeat = first is None
         first = first or near
-        known = (solved, inner, *near, *far, *first, side, block)
+        known = (solved, inner, *near, *first, side, block)
         if iteration + 1 < ITERS:
             reach = wide if iteration + 2 < ITERS else rows
-            value, one_solved, second, solved, inner, *sent = call(
-                advance_kernel,
-                (field,) * 5 + (flat(COMPS * (wide + reach)),) * 2 + (faces(reach),) * 2,
-                [VMEM] * 10,
-                2,
+
+            def advance(*refs):
+                advance_kernel(repeat, *refs)
+
+            value, one_solved, second, last_solved, solved, inner, *sent = call(
+                advance,
+                (field,) * 4 + (both,) * 2 + (flat(COMPS * (wide + reach)),) * 2,
+                [VMEM] * 8,
+                3,
             )(*known)
-            solves += [one_solved, solved]
+            solves += [one_solved, last_solved]
         else:
+
             def early(*refs):
                 early_kernel(rows, *refs)
 
             sums = call(early, (flat(EARLY_ROWS),) * 2, [VMEM] * EARLY, 2, cost=4000000)(*values)
             value, one_solved, second, message = call(
-                gram_kernel, (field,) * 3 + (flat(slabs * copies),), [VMEM] * (12 + EARLY), 4
+                gram_kernel, (field,) * 3 + (flat(slabs * copies),), [VMEM] * (10 + EARLY), 4
             )(*known, *values, *sums)
             solves += [one_solved]
         values += [value, second]

time: 43.8 us -> 44.1 us (level)
  starting transfers between devices: 16.1 us -> 13.3 us
  waiting for transfers between devices: 13.4 us -> 15.5 us
  Pallas kernels: 4.42 us -> 4.99 us
  blocking collectives: 8.86 us -> 9.41 us
    all_to_all x1, waiting for transfers between devices: 5.83 us -> 1.61 us  [local(): received = lax.all_to_all(message, everyone, 0, 0, tiled=True)]
    ppermute x0 -> x1, waiting for transfers between devices: none -> 3.98 us  [local(): beside = lax.ppermute(fields, 'slab', [(s, s ^ 1) for s in range(slabs)])]
    ppermute x8 -> x4, starting transfers between devices: 7.2 us -> 3.43 us  [race(): return lax.ppermute(array, ('slab', 'batch'), sorted(pairs))]
    ppermute x0 -> x1, starting transfers between devices: none -> 1.83 us  [local(): beside = lax.ppermute(fields, 'slab', [(s, s ^ 1) for s in range(slabs)])]
    ppermute x2, waiting for transfers between devices: 0.01 us -> 1.26 us  [ring(): lax.ppermute(array, axis, [(i, (i + step) % count) for i in range(count)])]
    ppermute x8 -> x4, waiting for transfers between devices: 7.56 us -> 8.62 us  [race(): return lax.ppermute(array, ('slab', 'batch'), sorted(pairs))]
    ppermute x2, starting transfers between devices: 1.54 us -> 0.74 us  [ring(): lax.ppermute(array, axis, [(i, (i + step) % count) for i in range(count)])]
    pallas_call x6, Pallas kernels: 2.93 us -> 3.49 us  [the longest x1 1.56 us: local(): call(pack, (jax.ShapeDtypeStruct((slabs * copies, 16, tile), jnp.bfloat16...]
  transfers between devices with their start and end apart: 11 -> 8, of which waited for: 5 -> 7; matrix products, arithmetic and copies ran while one was open for 0% -> 0% of each run, Pallas kernels for 2% -> 2%
where the time goes in v6:
time: 44.1 us; the launch traced here: 43.9 us
  waiting for transfers between devices  15.5 us (35%)
  starting transfers between devices  13.3 us (30%)
  blocking collectives  9.41 us (21%)
  Pallas kernels  4.99 us (11%)
  between operations  0.69 us (2%)
    all_to_all x1, blocking collectives, local(): gathered = lax.all_to_all(message, everyone, 0, 0, tiled=True)  9.41 us
    ppermute x4, waiting for transfers between devices, race(): return lax.ppermute(array, ('slab', 'batch'), sorted(pairs))  8.62 us
    all_to_all x1, starting transfers between devices, local(): received = lax.all_to_all(message, everyone, 0, 0, tiled=True)  7.33 us
    ppermute x1, waiting for transfers between devices, local(): beside = lax.ppermute(fields, 'slab', [(s, s ^ 1) for s in range(slabs)])  3.98 us
    ppermute x4, starting transfers between devices, race(): return lax.ppermute(array, ('slab', 'batch'), sorted(pairs))  3.43 us
    ppermute x1, starting transfers between devices, local(): beside = lax.ppermute(fields, 'slab', [(s, s ^ 1) for s in range(slabs)])  1.83 us
    all_to_all x1, waiting for transfers between devices, local(): received = lax.all_to_all(message, everyone, 0, 0, tiled=True)  1.61 us
    pallas_call x1, Pallas kernels, local(): call(pack, (jax.ShapeDtypeStruct((slabs * copies, 16, tile), jnp.bfloat16...  1.56 us
  transfers between devices with their start and end apart: 8, of which 7 were waited for; matrix products, arithmetic and copies ran while one was open for 0% of the time, Pallas kernels for 2%

profile of v6, /device:TPU:0, one launch (start us, length us, event | category | flops | bytes accessed | tf_op | source)
XLA Modules:
  0.0 43.9 jit_solution(5885200532820335202)
XLA Ops:
  0.6 1.6 %shard_map.68 = (bf16[32,16,128]{2,1,0:T(8,128)(2,1)}, f32[2,3,2,16,128]{4,3,2,1,0:T(8,128)S(1)}) custom-call(s32[8,128]{1,0:T(8,128)} %bitcast.8, f32[3,1024]{1,0:T(4,128)} %refs_1_.1, f32[8,128]{1,0:T(8,128)} %bitcast.9, f32[3,2,16,128]{3,2,1,0:T(8,128)} %refs_3_.1, f32[3,2,16,128]{3,2,1,0:T(8,128)} %refs_4_.1), custom_call_target="tpu_custom_call" | custom-call | tf_op jit(solution)/shard_map/pallas_call | solution.py:694
  2.2 7.3 %all-to-all-start = ((bf16[32,16,128]{2,1,0:T(8,128)(2,1)}), bf16[32,16,128]{2,1,0:T(8,128)(2,1)S(1)}, u32[]{:S(2)}, u32[]{:S(2)}) async-start(bf16[32,16,128]{2,1,0:T(8,128)(2,1)} %get-tuple-element.31), calls=%async_computation | async-start | bytes 262144 | tf_op jit(solution)/shard_map/all_to_all | solution.py:721
  9.5 1.8 %collective-permute-start = (f32[2,3,2,16,128]{4,3,2,1,0:T(8,128)S(1)}, f32[2,3,2,16,128]{4,3,2,1,0:T(8,128)S(1)}, u32[]{:S(2)}, u32[]{:S(2)}) collective-permute-start(f32[2,3,2,16,128]{4,3,2,1,0:T(8,128)S(1)} %get-tuple-element.28.here.refs_0_), channel_id=1, source_target_pairs={{0,4},{4,0},{8,12},{12,8},{16,20},{20,16},{24,28},{28,24},{1,5},{5... | collective-permute-start | bytes 294920 | tf_op jit(solution)/shard_map/ppermute | solution.py:720
  11.4 4.0 %collective-permute-done.beside.refs_1_ = f32[2,3,2,16,128]{4,3,2,1,0:T(8,128)S(1)} collective-permute-done((f32[2,3,2,16,128]{4,3,2,1,0:T(8,128)S(1)}, f32[2,3,2,16,128]{4,3,2,1,0:T(8,128)S(1)}, u32[]{:S(2)}, u32[]{:S(2)}) %collective-permute-start) | collective-permute-done | bytes 98336 | tf_op jit(solution)/shard_map/ppermute | solution.py:720
  15.4 0.7 %collective-permute-start.1 = (f32[2,6,2,4,128]{4,3,2,1,0:T(4,128)S(1)}, f32[2,6,2,4,128]{4,3,2,1,0:T(4,128)S(1)}, u32[]{:S(2)}, u32[]{:S(2)}) collective-permute-start(f32[2,6,2,4,128]{4,3,2,1,0:T(4,128)S(1)} %get-tuple-element.29), channel_id=1, source_target_pairs={{0,3},{1,0},{2,1},{3,2},{4,7},{5,4},{6,5},{7,6},{8,11},{9,8},{10,9... | collective-permute-start | bytes 147464 | tf_op jit(solution)/shard_map/ppermute | solution.py:647
  16.1 0.0 collective-permute-start.2
  16.1 1.6 %all-to-all-done.refs_0_ = bf16[32,16,128]{2,1,0:T(8,128)(2,1)S(1)} async-done(((bf16[32,16,128]{2,1,0:T(8,128)(2,1)}), bf16[32,16,128]{2,1,0:T(8,128)(2,1)S(1)}, u32[]{:S(2)}, u32[]{:S(2)}) %all-to-all-start) | async-done | bytes 131104 | tf_op jit(solution)/shard_map/all_to_all | solution.py:721
  17.7 0.8 %shard_map.70.refs_4_ = f32[2,144,128]{2,1,0:T(8,128)S(1)} custom-call(bf16[32,16,128]{2,1,0:T(8,128)(2,1)S(1)} %all-to-all-done.refs_0_), custom_call_target="tpu_custom_call" | custom-call | tf_op jit(solution)/shard_map/pallas_call | solution.py:729
  18.5 0.0 collective-permute-done.1.refs_2_
  18.5 1.3 %collective-permute-done.2.refs_3_ = f32[2,6,2,4,128]{4,3,2,1,0:T(4,128)S(1)} collective-permute-done((f32[2,6,2,4,128]{4,3,2,1,0:T(4,128)S(1)}, f32[2,6,2,4,128]{4,3,2,1,0:T(4,128)S(1)}, u32[]{:S(2)}, u32[]{:S(2)}) %collective-permute-start.2) | collective-permute-done | bytes 49184 | tf_op jit(solution)/shard_map/ppermute | solution.py:647
  19.8 0.2 shard_map.71
  20.0 1.7 %collective-permute-start.3 = (f32[168,128]{1,0:T(8,128)S(1)}, f32[168,128]{1,0:T(8,128)S(1)}, u32[]{:S(2)}, u32[]{:S(2)}) collective-permute-start(f32[168,128]{1,0:T(8,128)S(1)} %get-tuple-element.34), channel_id=1, source_target_pairs={{0,8},{1,0},{2,10},{3,2},{4,12},{5,4},{6,14},{7,6},{8,16},{9,1},{1... | collective-permute-start | bytes 258056 | tf_op jit(solution)/shard_map/ppermute | solution.py:660
  21.6 0.0 collective-permute-start.4
  21.6 2.1 %collective-permute-done.3.refs_2_.refs_4_ = f32[168,128]{1,0:T(8,128)S(1)} collective-permute-done((f32[168,128]{1,0:T(8,128)S(1)}, f32[168,128]{1,0:T(8,128)S(1)}, u32[]{:S(2)}, u32[]{:S(2)}) %collective-permute-start.3) | collective-permute-done | bytes 86048 | tf_op jit(solution)/shard_map/ppermute | solution.py:660
  23.7 2.5 %collective-permute-done.4.refs_3_.refs_5_ = f32[168,128]{1,0:T(8,128)S(1)} collective-permute-done((f32[168,128]{1,0:T(8,128)S(1)}, f32[168,128]{1,0:T(8,128)S(1)}, u32[]{:S(2)}, u32[]{:S(2)}) %collective-permute-start.4) | collective-permute-done | bytes 86048 | tf_op jit(solution)/shard_map/ppermute | solution.py:660
  26.3 0.3 shard_map.72
  26.6 1.8 %collective-permute-start.5 = (f32[120,128]{1,0:T(8,128)S(1)}, f32[120,128]{1,0:T(8,128)S(1)}, u32[]{:S(2)}, u32[]{:S(2)}) collective-permute-start(f32[120,128]{1,0:T(8,128)S(1)} %get-tuple-element.40), channel_id=1, source_target_pairs={{0,8},{1,0},{2,10},{3,2},{4,12},{5,4},{6,14},{7,6},{8,16},{9,1},{1... | collective-permute-start | bytes 184328 | tf_op jit(solution)/shard_map/ppermute | solution.py:660
  28.3 0.0 collective-permute-start.6
  28.3 0.2 shard_map.73
  28.5 1.6 %collective-permute-done.5.refs_2_ = f32[120,128]{1,0:T(8,128)S(1)} collective-permute-done((f32[120,128]{1,0:T(8,128)S(1)}, f32[120,128]{1,0:T(8,128)S(1)}, u32[]{:S(2)}, u32[]{:S(2)}) %collective-permute-start.5) | collective-permute-done | bytes 61472 | tf_op jit(solution)/shard_map/ppermute | solution.py:660
  30.2 2.4 %collective-permute-done.6.refs_3_ = f32[120,128]{1,0:T(8,128)S(1)} collective-permute-done((f32[120,128]{1,0:T(8,128)S(1)}, f32[120,128]{1,0:T(8,128)S(1)}, u32[]{:S(2)}, u32[]{:S(2)}) %collective-permute-start.6) | collective-permute-done | bytes 61472 | tf_op jit(solution)/shard_map/ppermute | solution.py:660
  32.5 0.7 %shard_map.74 = (f32[3,2,24,128]{3,2,1,0:T(8,128)S(1)}, f32[3,2,24,128]{3,2,1,0:T(8,128)S(1)}, f32[3,2,24,128]{3,2,1,0:T(8,128)S(1)}, f32[32,128]{1,0:T(8,128)S(1)}) custom-call(f32[2,3,2,24,128]{4,3,2,1,0:T(8,128)S(1)} %get-tuple-element.38.refs_0_, f32[2,3,2,24,128]{4,3,2,1,0:T(8,128)S(1)} %get-tuple-element.39.refs_1_, ...), custom_call_target="tpu_custom_call" | custom-call | tf_op jit(solution)/shard_map/pallas_call | solution.py:773
  33.2 9.4 %all_to_all.16 = f32[32,1,128]{2,1,0:T(1,128)S(1)} all-to-all(f32[32,1,128]{2,1,0:T(1,128)S(1)} %bitcast.7), channel_id=1, replica_groups=mesh['slab'=8,'batch'=4] {'slab','batch'}, dimensions={0} | all-to-all | bytes 32768 | tf_op jit(solution)/shard_map/all_to_all | solution.py:778
  42.6 1.3 %shard_map.75 = (f32[3,2,16,128]{3,2,1,0:T(8,128)}, f32[3,2,16,128]{3,2,1,0:T(8,128)}) custom-call(f32[32,128]{1,0:T(8,128)S(1)} %bitcast.6, f32[3,2,24,128]{3,2,1,0:T(8,128)S(1)} %get-tuple-element.42.refs_0_.refs_8_.refs_1_, f32[3,2,24,128]{3,2,1,0:T(8,128)S(1)} %get-tuple-element.43.refs_1_.refs_9_.refs_2_, ...), custom_call_target="tpu_custom_call" | custom-call | tf_op jit(solution)/shard_map/pallas_call | solution.py:779
  (1 shorter events, 0.0 us)
Async XLA Ops:
  2.2 15.5 %all-to-all-start = ((bf16[32,16,128]{2,1,0:T(8,128)(2,1)}), bf16[32,16,128]{2,1,0:T(8,128)(2,1)S(1)}, u32[]{:S(2)}, u32[]{:S(2)}) async-start(bf16[32,16,128]{2,1,0:T(8,128)(2,1)} %get-tuple-element.31), calls=%async_computation | async-start | bytes 262144 | tf_op jit(solution)/shard_map/all_to_all | solution.py:721
  9.5 5.8 %collective-permute-start = (f32[2,3,2,16,128]{4,3,2,1,0:T(8,128)S(1)}, f32[2,3,2,16,128]{4,3,2,1,0:T(8,128)S(1)}, u32[]{:S(2)}, u32[]{:S(2)}) collective-permute-start(f32[2,3,2,16,128]{4,3,2,1,0:T(8,128)S(1)} %get-tuple-element.28.here.refs_0_), channel_id=1, source_target_pairs={{0,4},{4,0},{8,12},{12,8},{16,20},{20,16},{24,28},{28,24},{1,5},{5... | collective-permute-start | bytes 294920 | tf_op jit(solution)/shard_map/ppermute | solution.py:720
  15.4 3.1 %collective-permute-start.1 = (f32[2,6,2,4,128]{4,3,2,1,0:T(4,128)S(1)}, f32[2,6,2,4,128]{4,3,2,1,0:T(4,128)S(1)}, u32[]{:S(2)}, u32[]{:S(2)}) collective-permute-start(f32[2,6,2,4,128]{4,3,2,1,0:T(4,128)S(1)} %get-tuple-element.29), channel_id=1, source_target_pairs={{0,3},{1,0},{2,1},{3,2},{4,7},{5,4},{6,5},{7,6},{8,11},{9,8},{10,9... | collective-permute-start | bytes 147464 | tf_op jit(solution)/shard_map/ppermute | solution.py:647
  16.1 3.7 %collective-permute-start.2 = (f32[2,6,2,4,128]{4,3,2,1,0:T(4,128)S(1)}, f32[2,6,2,4,128]{4,3,2,1,0:T(4,128)S(1)}, u32[]{:S(2)}, u32[]{:S(2)}) collective-permute-start(f32[2,6,2,4,128]{4,3,2,1,0:T(4,128)S(1)} %get-tuple-element.30), channel_id=1, source_target_pairs={{0,1},{1,2},{2,3},{3,0},{4,5},{5,6},{6,7},{7,4},{8,9},{9,10},{10,1... | collective-permute-start | bytes 147464 | tf_op jit(solution)/shard_map/ppermute | solution.py:647
  20.0 3.8 %collective-permute-start.3 = (f32[168,128]{1,0:T(8,128)S(1)}, f32[168,128]{1,0:T(8,128)S(1)}, u32[]{:S(2)}, u32[]{:S(2)}) collective-permute-start(f32[168,128]{1,0:T(8,128)S(1)} %get-tuple-element.34), channel_id=1, source_target_pairs={{0,8},{1,0},{2,10},{3,2},{4,12},{5,4},{6,14},{7,6},{8,16},{9,1},{1... | collective-permute-start | bytes 258056 | tf_op jit(solution)/shard_map/ppermute | solution.py:660
  21.6 4.6 %collective-permute-start.4 = (f32[168,128]{1,0:T(8,128)S(1)}, f32[168,128]{1,0:T(8,128)S(1)}, u32[]{:S(2)}, u32[]{:S(2)}) collective-permute-start(f32[168,128]{1,0:T(8,128)S(1)} %get-tuple-element.35), channel_id=1, source_target_pairs={{0,1},{1,9},{2,3},{3,11},{4,5},{5,13},{6,7},{7,15},{8,0},{9,17},{1... | collective-permute-start | bytes 258056 | tf_op jit(solution)/shard_map/ppermute | solution.py:660
  26.6 3.6 %collective-permute-start.5 = (f32[120,128]{1,0:T(8,128)S(1)}, f32[120,128]{1,0:T(8,128)S(1)}, u32[]{:S(2)}, u32[]{:S(2)}) collective-permute-start(f32[120,128]{1,0:T(8,128)S(1)} %get-tuple-element.40), channel_id=1, source_target_pairs={{0,8},{1,0},{2,10},{3,2},{4,12},{5,4},{6,14},{7,6},{8,16},{9,1},{1... | collective-permute-start | bytes 184328 | tf_op jit(solution)/shard_map/ppermute | solution.py:660
  28.3 4.2 %collective-permute-start.6 = (f32[120,128]{1,0:T(8,128)S(1)}, f32[120,128]{1,0:T(8,128)S(1)}, u32[]{:S(2)}, u32[]{:S(2)}) collective-permute-start(f32[120,128]{1,0:T(8,128)S(1)} %get-tuple-element.41), channel_id=1, source_target_pairs={{0,1},{1,9},{2,3},{3,11},{4,5},{5,13},{6,7},{7,15},{8,0},{9,17},{1... | collective-permute-start | bytes 184328 | tf_op jit(solution)/shard_map/ppermute | solution.py:660

commit v7 on v6

--- a/solution.py
+++ b/solution.py
@@ -11,6 +11,7 @@
 COMPS = 3
 BASIS = DEPTH + 1
 EARLY = DEPTH - 1
+LOWEST = -63
 PAIRS = sorted(((i, j) for j in range(BASIS) for i in range(j + 1)), key=lambda p: p[1] >= EARLY)
 EARLY_PAIRS = [p for p in PAIRS if p[1] < EARLY]
 LATE_PAIRS = [p for p in PAIRS if p[1] >= EARLY]
@@ -123,14 +124,16 @@
     tile = ids.shape[1]
     width = 128
     high = ids[...] // width
-    low = ids[...] - high * width
-    rest = [high.astype(F32), low.astype(F32)]
-    rest += [jnp.zeros_like(rest[0])] * (8 - COMPS - len(rest))
+    code = 1.0 + (ids[...] - high * width).astype(F32) * (1.0 / width)
+    code = code * 2.0**LOWEST
+    for k in range(7):
+        code = code * jnp.where((high >> k) & 1 == 1, 2.0 ** (2**k), 1.0)
     for pair in range(0, slabs, 2):
         blocks = []
         for s in (pair, pair + 1):
             at = slice(s * tile, (s + 1) * tile)
-            blocks += [forces[:, at] * weights[s : s + 1]] + [part[s : s + 1] for part in rest]
+            blocks.append(forces[:, at] * weights[s : s + 1])
+        blocks.append(code[pair : pair + 2])
         block = jnp.concatenate(blocks, axis=0).astype(jnp.bfloat16)
         for k in range(2 * copies):
             message_out[pair * copies + k] = block
@@ -170,11 +173,17 @@
     def over_sixteen(row):
         return jnp.broadcast_to(row, (16, tile)).astype(narrow)
 
-    def deposit(block, step):
-        row_values, column_hot = [], []
+    def deposit(step):
+        row_values, column_hot = [[], []], [[], []]
         for k in range(group):
-            part = message[step * group + k, 8 * block : 8 * block + 8].astype(F32)
-            cell_row = part[3:4].astype(jnp.int32)
+            part = message[step * group + k].astype(F32)
+            rest = part * 2.0**-LOWEST
+            cell_row = jnp.zeros(part.shape, jnp.int32)
+            for bit in range(6, -1, -1):
+                more = rest >= 2.0 ** (2**bit)
+                rest = jnp.where(more, rest * 2.0 ** -(2**bit), rest)
+                cell_row = cell_row + jnp.where(more, 2**bit, 0)
+            columns = (rest - 1.0) * width
             plane = jnp.zeros_like(cell_row)
             for p in range(1, planes):
                 plane = plane + (cell_row >= p * height).astype(jnp.int32)
@@ -182,40 +191,48 @@
             away = jnp.where(away < 0, away + height, away)
             spot = jnp.where(away < rows + DEPTH, away, away - height + wide)
             inside = (away < rows + DEPTH) | (away >= height - DEPTH)
-            spot = over_sixteen(jnp.where(inside, spot + plane * wide, -1).astype(F32))
-            column = over_sixteen(part[4:5])
-            values = [over_sixteen(part[c : c + 1]) for c in range(COMPS)]
-            here = [counts[g] == spot for g in range(planes * wide // 16)]
-            row_values.append(
-                jnp.concatenate(
-                    [jnp.where(at, value, nothing) for value in values for at in here], axis=0
+            spots = jnp.where(inside, spot + plane * wide, -1).astype(F32)
+            for block in range(2):
+                at = 2 * COMPS + block
+                spot = over_sixteen(spots[at : at + 1])
+                column = over_sixteen(columns[at : at + 1])
+                here = [counts[g] == spot for g in range(planes * wide // 16)]
+                first = block * COMPS
+                values = [over_sixteen(part[c : c + 1]) for c in range(first, first + COMPS)]
+                row_values[block].append(
+                    jnp.concatenate(
+                        [jnp.where(at, value, nothing) for value in values for at in here], axis=0
+                    )
                 )
+                column_hot[block].append(
+                    jnp.concatenate([jnp.where(n == column, one, nothing) for n in counts], axis=0)
+                )
+        return [
+            lax.dot_general(
+                jnp.concatenate(row_values[block], axis=1),
+                jnp.concatenate(column_hot[block], axis=1),
+                (((1,), (1,)), ((), ())),
+                preferred_element_type=F32,
             )
-            column_hot.append(
-                jnp.concatenate([jnp.where(n == column, one, nothing) for n in counts], axis=0)
-            )
-        return lax.dot_general(
-            jnp.concatenate(row_values, axis=1),
-            jnp.concatenate(column_hot, axis=1),
-            (((1,), (1,)), ((), ())),
-            preferred_element_type=F32,
-        )
+            for block in range(2)
+        ]
 
     steps = message.shape[0] // group
-    for block in range(2):
-        if steps <= 4:
-            total = deposit(block, 0)
-            for step in range(1, steps):
-                total = total + deposit(block, step)
-            momentum_sum[block] = total
-        else:
-            momentum_sum[block] = jnp.zeros(momentum_sum.shape[1:], F32)
-
-            def add_step(step, carry):
-                momentum_sum[block] += deposit(block, step)
-                return carry
-
-            lax.fori_loop(0, steps, add_step, 0)
+    if steps <= 4:
+        totals = deposit(0)
+        for step in range(1, steps):
+            totals = [x + y for x, y in zip(totals, deposit(step))]
+        for block in range(2):
+            momentum_sum[block] = totals[block]
+    else:
+        momentum_sum[...] = jnp.zeros(momentum_sum.shape, F32)
+
+        def add_step(step, carry):
+            for block, total in enumerate(deposit(step)):
+                momentum_sum[block] += total
+            return carry
+
+        lax.fori_loop(0, steps, add_step, 0)
 
 
 def fill_coefficients(courant, slab, slabs, batch, copies, rows, side, block):
@@ -668,7 +685,7 @@
     height = rows * copies
     tile = cell_ids.shape[0] // slabs
     assert rows % 8 == 0 and width == 128 and copies % 2 == 0 and slabs % 2 == 0
-    assert planes * height <= 256 and 2 * DEPTH <= height - rows
+    assert planes * height <= 128 and 2 * DEPTH <= height - rows
     field = jax.ShapeDtypeStruct((COMPS, planes, wide, width), F32)
     quad = jax.ShapeDtypeStruct((2, 4, planes, wide, width), F32)
     both = jax.ShapeDtypeStruct((2, COMPS, planes, wide, width), F32)
@@ -694,7 +711,7 @@
     message, fields = call(
         pack,
         (
-            jax.ShapeDtypeStruct((slabs * copies, 16, tile), jnp.bfloat16),
+            jax.ShapeDtypeStruct((slabs * copies, 2 * (COMPS + 1), tile), jnp.bfloat16),
             jax.ShapeDtypeStruct((2, *velocity_old.shape), F32),
         ),
         [ANY] * 5,

time: 44.1 us -> 39.9 us (0.905)
  starting transfers between devices: 13.3 us -> 10.8 us
  waiting for transfers between devices: 15.5 us -> 14.3 us
  blocking collectives: 9.41 us -> 8.86 us
    all_to_all x1, waiting for transfers between devices: 1.61 us -> 5.82 us  [local(): received = lax.all_to_all(message, everyone, 0, 0, tiled=True)]
    ppermute x1, waiting for transfers between devices: 3.98 us -> 0.01 us  [local(): beside = lax.ppermute(fields, 'slab', [(s, s ^ 1) for s in range(slabs)])]
    all_to_all x1, starting transfers between devices: 7.33 us -> 4.89 us  [local(): received = lax.all_to_all(message, everyone, 0, 0, tiled=True)]
    ppermute x4, starting transfers between devices: 3.43 us -> 1.28 us  [race(): return lax.ppermute(array, ('slab', 'batch'), sorted(pairs))]
    ppermute x2, waiting for transfers between devices: 1.26 us -> 0.01 us  [ring(): lax.ppermute(array, axis, [(i, (i + step) % count) for i in range(count)])]
    ppermute x1, starting transfers between devices: 1.83 us -> 3.06 us  [local(): beside = lax.ppermute(fields, 'slab', [(s, s ^ 1) for s in range(slabs)])]
    ppermute x2, starting transfers between devices: 0.74 us -> 1.54 us  [ring(): lax.ppermute(array, axis, [(i, (i + step) % count) for i in range(count)])]
    all_to_all x1, blocking collectives: 9.41 us -> 8.86 us  [local(): gathered = lax.all_to_all(message, everyone, 0, 0, tiled=True)]
  transfers between devices with their start and end apart: 8 -> 8, of which waited for: 7 -> 5; matrix products, arithmetic and copies ran while one was open for 0% -> 0% of each run, Pallas kernels for 2% -> 3%
where the time goes in v7:
time: 39.9 us; the launch traced here: 39.6 us
  waiting for transfers between devices  14.3 us (36%)
  starting transfers between devices  10.8 us (27%)
  blocking collectives  8.86 us (22%)
  Pallas kernels  4.99 us (13%)
  between operations  0.7 us (2%)
    all_to_all x1, blocking collectives, local(): gathered = lax.all_to_all(message, everyone, 0, 0, tiled=True)  8.86 us
    ppermute x4, waiting for transfers between devices, race(): return lax.ppermute(array, ('slab', 'batch'), sorted(pairs))  8.48 us
    all_to_all x1, waiting for transfers between devices, local(): received = lax.all_to_all(message, everyone, 0, 0, tiled=True)  5.82 us
    all_to_all x1, starting transfers between devices, local(): received = lax.all_to_all(message, everyone, 0, 0, tiled=True)  4.89 us
    ppermute x1, starting transfers between devices, local(): beside = lax.ppermute(fields, 'slab', [(s, s ^ 1) for s in range(slabs)])  3.06 us
    ppermute x2, starting transfers between devices, ring(): lax.ppermute(array, axis, [(i, (i + step) % count) for i in range(count)])  1.54 us
    pallas_call x1, Pallas kernels, local(): call(pack, (jax.ShapeDtypeStruct((slabs * copies, 2 * (COMPS + 1), tile),...  1.53 us
    ppermute x4, starting transfers between devices, race(): return lax.ppermute(array, ('slab', 'batch'), sorted(pairs))  1.28 us
  transfers between devices with their start and end apart: 8, of which 5 were waited for; matrix products, arithmetic and copies ran while one was open for 0% of the time, Pallas kernels for 3%

profile of v7, /device:TPU:0, one launch (start us, length us, event | category | flops | bytes accessed | tf_op | source)
XLA Modules:
  0.0 39.6 jit_solution(17468223698320012415)
XLA Ops:
  0.6 1.5 %shard_map.68 = (bf16[32,8,128]{2,1,0:T(8,128)(2,1)}, f32[2,3,2,16,128]{4,3,2,1,0:T(8,128)S(1)}) custom-call(s32[8,128]{1,0:T(8,128)} %bitcast.8, f32[3,1024]{1,0:T(4,128)} %refs_1_.1, f32[8,128]{1,0:T(8,128)} %bitcast.9, f32[3,2,16,128]{3,2,1,0:T(8,128)} %refs_3_.1, f32[3,2,16,128]{3,2,1,0:T(8,128)} %refs_4_.1), custom_call_target="tpu_custom_call" | custom-call | tf_op jit(solution)/shard_map/pallas_call | solution.py:711
  2.2 3.1 %collective-permute-start = (f32[2,3,2,16,128]{4,3,2,1,0:T(8,128)S(1)}, f32[2,3,2,16,128]{4,3,2,1,0:T(8,128)S(1)}, u32[]{:S(2)}, u32[]{:S(2)}) collective-permute-start(f32[2,3,2,16,128]{4,3,2,1,0:T(8,128)S(1)} %get-tuple-element.28.here.refs_0_), channel_id=1, source_target_pairs={{0,4},{4,0},{8,12},{12,8},{16,20},{20,16},{24,28},{28,24},{1,5},{5... | collective-permute-start | bytes 294920 | tf_op jit(solution)/shard_map/ppermute | solution.py:737
  5.2 4.9 %all-to-all-start = ((bf16[32,8,128]{2,1,0:T(8,128)(2,1)}), bf16[32,8,128]{2,1,0:T(8,128)(2,1)S(1)}, u32[]{:S(2)}, u32[]{:S(2)}) async-start(bf16[32,8,128]{2,1,0:T(8,128)(2,1)} %get-tuple-element.31), calls=%async_computation | async-start | bytes 131072 | tf_op jit(solution)/shard_map/all_to_all | solution.py:738
  10.1 0.0 collective-permute-done.beside.refs_1_
  10.2 1.5 %collective-permute-start.1 = (f32[2,6,2,4,128]{4,3,2,1,0:T(4,128)S(1)}, f32[2,6,2,4,128]{4,3,2,1,0:T(4,128)S(1)}, u32[]{:S(2)}, u32[]{:S(2)}) collective-permute-start(f32[2,6,2,4,128]{4,3,2,1,0:T(4,128)S(1)} %get-tuple-element.29), channel_id=1, source_target_pairs={{0,3},{1,0},{2,1},{3,2},{4,7},{5,4},{6,5},{7,6},{8,11},{9,8},{10,9... | collective-permute-start | bytes 147464 | tf_op jit(solution)/shard_map/ppermute | solution.py:664
  11.7 0.0 collective-permute-start.2
  11.7 5.8 %all-to-all-done.refs_0_ = bf16[32,8,128]{2,1,0:T(8,128)(2,1)S(1)} async-done(((bf16[32,8,128]{2,1,0:T(8,128)(2,1)}), bf16[32,8,128]{2,1,0:T(8,128)(2,1)S(1)}, u32[]{:S(2)}, u32[]{:S(2)}) %all-to-all-start) | async-done | bytes 65568 | tf_op jit(solution)/shard_map/all_to_all | solution.py:738
  17.5 0.8 %shard_map.70.refs_4_ = f32[2,144,128]{2,1,0:T(8,128)S(1)} custom-call(bf16[32,8,128]{2,1,0:T(8,128)(2,1)S(1)} %all-to-all-done.refs_0_), custom_call_target="tpu_custom_call" | custom-call | tf_op jit(solution)/shard_map/pallas_call | solution.py:746
  18.3 0.0 collective-permute-done.1.refs_2_
  18.4 0.0 collective-permute-done.2.refs_3_
  18.4 0.2 shard_map.71
  18.6 0.6 %collective-permute-start.3 = (f32[168,128]{1,0:T(8,128)S(1)}, f32[168,128]{1,0:T(8,128)S(1)}, u32[]{:S(2)}, u32[]{:S(2)}) collective-permute-start(f32[168,128]{1,0:T(8,128)S(1)} %get-tuple-element.34), channel_id=1, source_target_pairs={{0,8},{1,0},{2,10},{3,2},{4,12},{5,4},{6,14},{7,6},{8,16},{9,1},{1... | collective-permute-start | bytes 258056 | tf_op jit(solution)/shard_map/ppermute | solution.py:677
  19.2 0.0 collective-permute-start.4
  19.2 2.6 %collective-permute-done.3.refs_2_.refs_4_ = f32[168,128]{1,0:T(8,128)S(1)} collective-permute-done((f32[168,128]{1,0:T(8,128)S(1)}, f32[168,128]{1,0:T(8,128)S(1)}, u32[]{:S(2)}, u32[]{:S(2)}) %collective-permute-start.3) | collective-permute-done | bytes 86048 | tf_op jit(solution)/shard_map/ppermute | solution.py:677
  21.8 1.9 %collective-permute-done.4.refs_3_.refs_5_ = f32[168,128]{1,0:T(8,128)S(1)} collective-permute-done((f32[168,128]{1,0:T(8,128)S(1)}, f32[168,128]{1,0:T(8,128)S(1)}, u32[]{:S(2)}, u32[]{:S(2)}) %collective-permute-start.4) | collective-permute-done | bytes 86048 | tf_op jit(solution)/shard_map/ppermute | solution.py:677
  23.7 0.3 shard_map.72
  24.0 0.7 %collective-permute-start.5 = (f32[120,128]{1,0:T(8,128)S(1)}, f32[120,128]{1,0:T(8,128)S(1)}, u32[]{:S(2)}, u32[]{:S(2)}) collective-permute-start(f32[120,128]{1,0:T(8,128)S(1)} %get-tuple-element.40), channel_id=1, source_target_pairs={{0,8},{1,0},{2,10},{3,2},{4,12},{5,4},{6,14},{7,6},{8,16},{9,1},{1... | collective-permute-start | bytes 184328 | tf_op jit(solution)/shard_map/ppermute | solution.py:677
  24.6 0.0 collective-permute-start.6
  24.6 0.2 shard_map.73
  24.8 1.6 %collective-permute-done.5.refs_2_ = f32[120,128]{1,0:T(8,128)S(1)} collective-permute-done((f32[120,128]{1,0:T(8,128)S(1)}, f32[120,128]{1,0:T(8,128)S(1)}, u32[]{:S(2)}, u32[]{:S(2)}) %collective-permute-start.5) | collective-permute-done | bytes 61472 | tf_op jit(solution)/shard_map/ppermute | solution.py:677
  26.5 2.4 %collective-permute-done.6.refs_3_ = f32[120,128]{1,0:T(8,128)S(1)} collective-permute-done((f32[120,128]{1,0:T(8,128)S(1)}, f32[120,128]{1,0:T(8,128)S(1)}, u32[]{:S(2)}, u32[]{:S(2)}) %collective-permute-start.6) | collective-permute-done | bytes 61472 | tf_op jit(solution)/shard_map/ppermute | solution.py:677
  28.8 0.7 %shard_map.74 = (f32[3,2,24,128]{3,2,1,0:T(8,128)S(1)}, f32[3,2,24,128]{3,2,1,0:T(8,128)S(1)}, f32[3,2,24,128]{3,2,1,0:T(8,128)S(1)}, f32[32,128]{1,0:T(8,128)S(1)}) custom-call(f32[2,3,2,24,128]{4,3,2,1,0:T(8,128)S(1)} %get-tuple-element.38.refs_0_, f32[2,3,2,24,128]{4,3,2,1,0:T(8,128)S(1)} %get-tuple-element.39.refs_1_, ...), custom_call_target="tpu_custom_call" | custom-call | tf_op jit(solution)/shard_map/pallas_call | solution.py:790
  29.5 8.9 %all_to_all.16 = f32[32,1,128]{2,1,0:T(1,128)S(1)} all-to-all(f32[32,1,128]{2,1,0:T(1,128)S(1)} %bitcast.7), channel_id=1, replica_groups=mesh['slab'=8,'batch'=4] {'slab','batch'}, dimensions={0} | all-to-all | bytes 32768 | tf_op jit(solution)/shard_map/all_to_all | solution.py:795
  38.4 1.3 %shard_map.75 = (f32[3,2,16,128]{3,2,1,0:T(8,128)}, f32[3,2,16,128]{3,2,1,0:T(8,128)}) custom-call(f32[32,128]{1,0:T(8,128)S(1)} %bitcast.6, f32[3,2,24,128]{3,2,1,0:T(8,128)S(1)} %get-tuple-element.42.refs_0_.refs_8_.refs_1_, f32[3,2,24,128]{3,2,1,0:T(8,128)S(1)} %get-tuple-element.43.refs_1_.refs_9_.refs_2_, ...), custom_call_target="tpu_custom_call" | custom-call | tf_op jit(solution)/shard_map/pallas_call | solution.py:796
  (1 shorter events, 0.0 us)
Async XLA Ops:
  2.2 8.0 %collective-permute-start = (f32[2,3,2,16,128]{4,3,2,1,0:T(8,128)S(1)}, f32[2,3,2,16,128]{4,3,2,1,0:T(8,128)S(1)}, u32[]{:S(2)}, u32[]{:S(2)}) collective-permute-start(f32[2,3,2,16,128]{4,3,2,1,0:T(8,128)S(1)} %get-tuple-element.28.here.refs_0_), channel_id=1, source_target_pairs={{0,4},{4,0},{8,12},{12,8},{16,20},{20,16},{24,28},{28,24},{1,5},{5... | collective-permute-start | bytes 294920 | tf_op jit(solution)/shard_map/ppermute | solution.py:737
  5.2 12.3 %all-to-all-start = ((bf16[32,8,128]{2,1,0:T(8,128)(2,1)}), bf16[32,8,128]{2,1,0:T(8,128)(2,1)S(1)}, u32[]{:S(2)}, u32[]{:S(2)}) async-start(bf16[32,8,128]{2,1,0:T(8,128)(2,1)} %get-tuple-element.31), calls=%async_computation | async-start | bytes 131072 | tf_op jit(solution)/shard_map/all_to_all | solution.py:738
  10.2 8.2 %collective-permute-start.1 = (f32[2,6,2,4,128]{4,3,2,1,0:T(4,128)S(1)}, f32[2,6,2,4,128]{4,3,2,1,0:T(4,128)S(1)}, u32[]{:S(2)}, u32[]{:S(2)}) collective-permute-start(f32[2,6,2,4,128]{4,3,2,1,0:T(4,128)S(1)} %get-tuple-element.29), channel_id=1, source_target_pairs={{0,3},{1,0},{2,1},{3,2},{4,7},{5,4},{6,5},{7,6},{8,11},{9,8},{10,9... | collective-permute-start | bytes 147464 | tf_op jit(solution)/shard_map/ppermute | solution.py:664
  11.7 6.6 %collective-permute-start.2 = (f32[2,6,2,4,128]{4,3,2,1,0:T(4,128)S(1)}, f32[2,6,2,4,128]{4,3,2,1,0:T(4,128)S(1)}, u32[]{:S(2)}, u32[]{:S(2)}) collective-permute-start(f32[2,6,2,4,128]{4,3,2,1,0:T(4,128)S(1)} %get-tuple-element.30), channel_id=1, source_target_pairs={{0,1},{1,2},{2,3},{3,0},{4,5},{5,6},{6,7},{7,4},{8,9},{9,10},{10,1... | collective-permute-start | bytes 147464 | tf_op jit(solution)/shard_map/ppermute | solution.py:664
  18.6 3.3 %collective-permute-start.3 = (f32[168,128]{1,0:T(8,128)S(1)}, f32[168,128]{1,0:T(8,128)S(1)}, u32[]{:S(2)}, u32[]{:S(2)}) collective-permute-start(f32[168,128]{1,0:T(8,128)S(1)} %get-tuple-element.34), channel_id=1, source_target_pairs={{0,8},{1,0},{2,10},{3,2},{4,12},{5,4},{6,14},{7,6},{8,16},{9,1},{1... | collective-permute-start | bytes 258056 | tf_op jit(solution)/shard_map/ppermute | solution.py:677
  19.2 4.5 %collective-permute-start.4 = (f32[168,128]{1,0:T(8,128)S(1)}, f32[168,128]{1,0:T(8,128)S(1)}, u32[]{:S(2)}, u32[]{:S(2)}) collective-permute-start(f32[168,128]{1,0:T(8,128)S(1)} %get-tuple-element.35), channel_id=1, source_target_pairs={{0,1},{1,9},{2,3},{3,11},{4,5},{5,13},{6,7},{7,15},{8,0},{9,17},{1... | collective-permute-start | bytes 258056 | tf_op jit(solution)/shard_map/ppermute | solution.py:677
  24.0 2.5 %collective-permute-start.5 = (f32[120,128]{1,0:T(8,128)S(1)}, f32[120,128]{1,0:T(8,128)S(1)}, u32[]{:S(2)}, u32[]{:S(2)}) collective-permute-start(f32[120,128]{1,0:T(8,128)S(1)} %get-tuple-element.40), channel_id=1, source_target_pairs={{0,8},{1,0},{2,10},{3,2},{4,12},{5,4},{6,14},{7,6},{8,16},{9,1},{1... | collective-permute-start | bytes 184328 | tf_op jit(solution)/shard_map/ppermute | solution.py:677
  24.6 4.2 %collective-permute-start.6 = (f32[120,128]{1,0:T(8,128)S(1)}, f32[120,128]{1,0:T(8,128)S(1)}, u32[]{:S(2)}, u32[]{:S(2)}) collective-permute-start(f32[120,128]{1,0:T(8,128)S(1)} %get-tuple-element.41), channel_id=1, source_target_pairs={{0,1},{1,9},{2,3},{3,11},{4,5},{5,13},{6,7},{7,15},{8,0},{9,17},{1... | collective-permute-start | bytes 184328 | tf_op jit(solution)/shard_map/ppermute | solution.py:677

commit v8 on v7

--- a/solution.py
+++ b/solution.py
@@ -103,7 +103,7 @@
 
 def pack_kernel(
     slabs, copies, ids_in, forces_in, weights_in, velocity_in, courant_in,
-    message_out, fields_out, ids, forces, weights, arrived,
+    message_out, fields_out, ids, forces, weights, arrived, message, sent,
 ):
     moves = [
         pltpu.make_async_copy(source, target, arrived.at[n])
@@ -128,6 +128,7 @@
     code = code * 2.0**LOWEST
     for k in range(7):
         code = code * jnp.where((high >> k) & 1 == 1, 2.0 ** (2**k), 1.0)
+    leaving = []
     for pair in range(0, slabs, 2):
         blocks = []
         for s in (pair, pair + 1):
@@ -135,9 +136,13 @@
             blocks.append(forces[:, at] * weights[s : s + 1])
         blocks.append(code[pair : pair + 2])
         block = jnp.concatenate(blocks, axis=0).astype(jnp.bfloat16)
+        at = pl.ds(pair * copies, 2 * copies)
         for k in range(2 * copies):
-            message_out[pair * copies + k] = block
-    for move in moves[3:]:
+            message[pair * copies + k] = block
+        leave = pltpu.make_async_copy(message.at[at], message_out.at[at], sent.at[pair // 2])
+        leave.start()
+        leaving.append(leave)
+    for move in moves[3:] + leaving:
         move.wait()
 
 
@@ -699,7 +704,7 @@
             kernel,
             out_shape=out_shape,
             in_specs=in_specs,
-            out_specs=[out_space] * len(out_shape),
+            out_specs=out_space if isinstance(out_space, list) else [out_space] * len(out_shape),
             cost_estimate=cost,
             scratch_shapes=list(scratch),
             compiler_params=pltpu.CompilerParams(vmem_limit_bytes=mib << 20),
@@ -721,7 +726,10 @@
             pltpu.VMEM(forces.shape, F32),
             pltpu.VMEM((slabs, tile), F32),
             pltpu.SemaphoreType.DMA((5,)),
+            pltpu.VMEM((slabs * copies, 2 * (COMPS + 1), tile), jnp.bfloat16),
+            pltpu.SemaphoreType.DMA((slabs // 2,)),
         ],
+        [ANY, VMEM],
     )(
         *(
             pltpu.with_memory_space_constraint(x, pltpu.HBM)
@@ -792,7 +800,7 @@
             )(*known, *values, *sums)
             solves += [one_solved]
         values += [value, second]
-    gathered = lax.all_to_all(message, everyone, 0, 0, tiled=True)
+    gathered = lax.all_to_all(message, ("batch", "slab"), 0, 0, tiled=True)
     return call(
         finish_kernel,
         (own, own),

time: 39.9 us -> 39.8 us (level)
  no operation moved by 1% of the time
where the time goes in v8:
time: 39.8 us; the launch traced here: 39.5 us
  waiting for transfers between devices  14.3 us (36%)
  starting transfers between devices  10.8 us (27%)
  blocking collectives  8.83 us (22%)
  Pallas kernels  4.93 us (12%)
  between operations  0.7 us (2%)
    all_to_all x1, blocking collectives, local(): gathered = lax.all_to_all(message, ('batch', 'slab'), 0, 0, tiled=True)  8.83 us
    ppermute x4, waiting for transfers between devices, race(): return lax.ppermute(array, ('slab', 'batch'), sorted(pairs))  8.48 us
    all_to_all x1, waiting for transfers between devices, local(): received = lax.all_to_all(message, everyone, 0, 0, tiled=True)  5.82 us
    all_to_all x1, starting transfers between devices, local(): received = lax.all_to_all(message, everyone, 0, 0, tiled=True)  4.89 us
    ppermute x1, starting transfers between devices, local(): beside = lax.ppermute(fields, 'slab', [(s, s ^ 1) for s in range(slabs)])  3.06 us
    ppermute x2, starting transfers between devices, ring(): lax.ppermute(array, axis, [(i, (i + step) % count) for i in range(count)])  1.54 us
    pallas_call x1, Pallas kernels, local(): call(pack, (jax.ShapeDtypeStruct((slabs * copies, 2 * (COMPS + 1), tile),...  1.47 us
    ppermute x4, starting transfers between devices, race(): return lax.ppermute(array, ('slab', 'batch'), sorted(pairs))  1.28 us
  transfers between devices with their start and end apart: 8, of which 5 were waited for; matrix products, arithmetic and copies ran while one was open for 0% of the time, Pallas kernels for 3%

profile of v8, /device:TPU:0, one launch (start us, length us, event | category | flops | bytes accessed | tf_op | source)
XLA Modules:
  0.0 39.5 jit_solution(14830317789747407180)
XLA Ops:
  0.6 1.5 %shard_map.68 = (bf16[32,8,128]{2,1,0:T(8,128)(2,1)}, f32[2,3,2,16,128]{4,3,2,1,0:T(8,128)S(1)}) custom-call(s32[8,128]{1,0:T(8,128)} %bitcast.8, f32[3,1024]{1,0:T(4,128)} %refs_1_.1, f32[8,128]{1,0:T(8,128)} %bitcast.9, f32[3,2,16,128]{3,2,1,0:T(8,128)} %refs_3_.1, f32[3,2,16,128]{3,2,1,0:T(8,128)} %refs_4_.1), custom_call_target="tpu_custom_call" | custom-call | tf_op jit(solution)/shard_map/pallas_call | solution.py:716
  2.1 3.1 %collective-permute-start = (f32[2,3,2,16,128]{4,3,2,1,0:T(8,128)S(1)}, f32[2,3,2,16,128]{4,3,2,1,0:T(8,128)S(1)}, u32[]{:S(2)}, u32[]{:S(2)}) collective-permute-start(f32[2,3,2,16,128]{4,3,2,1,0:T(8,128)S(1)} %get-tuple-element.28.here.refs_0_), channel_id=1, source_target_pairs={{0,4},{4,0},{8,12},{12,8},{16,20},{20,16},{24,28},{28,24},{1,5},{5... | collective-permute-start | bytes 294920 | tf_op jit(solution)/shard_map/ppermute | solution.py:745
  5.2 4.9 %all-to-all-start = ((bf16[32,8,128]{2,1,0:T(8,128)(2,1)}), bf16[32,8,128]{2,1,0:T(8,128)(2,1)S(1)}, u32[]{:S(2)}, u32[]{:S(2)}) async-start(bf16[32,8,128]{2,1,0:T(8,128)(2,1)} %get-tuple-element.31), calls=%async_computation | async-start | bytes 131072 | tf_op jit(solution)/shard_map/all_to_all | solution.py:746
  10.1 0.0 collective-permute-done.beside.refs_1_
  10.1 1.5 %collective-permute-start.1 = (f32[2,6,2,4,128]{4,3,2,1,0:T(4,128)S(1)}, f32[2,6,2,4,128]{4,3,2,1,0:T(4,128)S(1)}, u32[]{:S(2)}, u32[]{:S(2)}) collective-permute-start(f32[2,6,2,4,128]{4,3,2,1,0:T(4,128)S(1)} %get-tuple-element.29), channel_id=1, source_target_pairs={{0,3},{1,0},{2,1},{3,2},{4,7},{5,4},{6,5},{7,6},{8,11},{9,8},{10,9... | collective-permute-start | bytes 147464 | tf_op jit(solution)/shard_map/ppermute | solution.py:669
  11.7 0.0 collective-permute-start.2
  11.7 5.8 %all-to-all-done.refs_0_ = bf16[32,8,128]{2,1,0:T(8,128)(2,1)S(1)} async-done(((bf16[32,8,128]{2,1,0:T(8,128)(2,1)}), bf16[32,8,128]{2,1,0:T(8,128)(2,1)S(1)}, u32[]{:S(2)}, u32[]{:S(2)}) %all-to-all-start) | async-done | bytes 65568 | tf_op jit(solution)/shard_map/all_to_all | solution.py:746
  17.5 0.8 %shard_map.70.refs_4_ = f32[2,144,128]{2,1,0:T(8,128)S(1)} custom-call(bf16[32,8,128]{2,1,0:T(8,128)(2,1)S(1)} %all-to-all-done.refs_0_), custom_call_target="tpu_custom_call" | custom-call | tf_op jit(solution)/shard_map/pallas_call | solution.py:754
  18.3 0.0 collective-permute-done.1.refs_2_
  18.3 0.0 collective-permute-done.2.refs_3_
  18.3 0.2 shard_map.71
  18.5 0.6 %collective-permute-start.3 = (f32[168,128]{1,0:T(8,128)S(1)}, f32[168,128]{1,0:T(8,128)S(1)}, u32[]{:S(2)}, u32[]{:S(2)}) collective-permute-start(f32[168,128]{1,0:T(8,128)S(1)} %get-tuple-element.34), channel_id=1, source_target_pairs={{0,8},{1,0},{2,10},{3,2},{4,12},{5,4},{6,14},{7,6},{8,16},{9,1},{1... | collective-permute-start | bytes 258056 | tf_op jit(solution)/shard_map/ppermute | solution.py:682
  19.1 0.0 collective-permute-start.4
  19.1 2.6 %collective-permute-done.3.refs_2_.refs_4_ = f32[168,128]{1,0:T(8,128)S(1)} collective-permute-done((f32[168,128]{1,0:T(8,128)S(1)}, f32[168,128]{1,0:T(8,128)S(1)}, u32[]{:S(2)}, u32[]{:S(2)}) %collective-permute-start.3) | collective-permute-done | bytes 86048 | tf_op jit(solution)/shard_map/ppermute | solution.py:682
  21.8 1.9 %collective-permute-done.4.refs_3_.refs_5_ = f32[168,128]{1,0:T(8,128)S(1)} collective-permute-done((f32[168,128]{1,0:T(8,128)S(1)}, f32[168,128]{1,0:T(8,128)S(1)}, u32[]{:S(2)}, u32[]{:S(2)}) %collective-permute-start.4) | collective-permute-done | bytes 86048 | tf_op jit(solution)/shard_map/ppermute | solution.py:682
  23.6 0.3 shard_map.72
  23.9 0.7 %collective-permute-start.5 = (f32[120,128]{1,0:T(8,128)S(1)}, f32[120,128]{1,0:T(8,128)S(1)}, u32[]{:S(2)}, u32[]{:S(2)}) collective-permute-start(f32[120,128]{1,0:T(8,128)S(1)} %get-tuple-element.40), channel_id=1, source_target_pairs={{0,8},{1,0},{2,10},{3,2},{4,12},{5,4},{6,14},{7,6},{8,16},{9,1},{1... | collective-permute-start | bytes 184328 | tf_op jit(solution)/shard_map/ppermute | solution.py:682
  24.5 0.0 collective-permute-start.6
  24.5 0.2 shard_map.73
  24.8 1.6 %collective-permute-done.5.refs_2_ = f32[120,128]{1,0:T(8,128)S(1)} collective-permute-done((f32[120,128]{1,0:T(8,128)S(1)}, f32[120,128]{1,0:T(8,128)S(1)}, u32[]{:S(2)}, u32[]{:S(2)}) %collective-permute-start.5) | collective-permute-done | bytes 61472 | tf_op jit(solution)/shard_map/ppermute | solution.py:682
  26.4 2.4 %collective-permute-done.6.refs_3_ = f32[120,128]{1,0:T(8,128)S(1)} collective-permute-done((f32[120,128]{1,0:T(8,128)S(1)}, f32[120,128]{1,0:T(8,128)S(1)}, u32[]{:S(2)}, u32[]{:S(2)}) %collective-permute-start.6) | collective-permute-done | bytes 61472 | tf_op jit(solution)/shard_map/ppermute | solution.py:682
  28.8 0.7 %shard_map.74 = (f32[3,2,24,128]{3,2,1,0:T(8,128)S(1)}, f32[3,2,24,128]{3,2,1,0:T(8,128)S(1)}, f32[3,2,24,128]{3,2,1,0:T(8,128)S(1)}, f32[32,128]{1,0:T(8,128)S(1)}) custom-call(f32[2,3,2,24,128]{4,3,2,1,0:T(8,128)S(1)} %get-tuple-element.38.refs_0_, f32[2,3,2,24,128]{4,3,2,1,0:T(8,128)S(1)} %get-tuple-element.39.refs_1_, ...), custom_call_target="tpu_custom_call" | custom-call | tf_op jit(solution)/shard_map/pallas_call | solution.py:798
  29.4 8.8 %all_to_all.16 = f32[32,1,128]{2,1,0:T(1,128)S(1)} all-to-all(f32[32,1,128]{2,1,0:T(1,128)S(1)} %bitcast.7), channel_id=1, replica_groups=mesh['slab'=8,'batch'=4] {'batch','slab'}, dimensions={0} | all-to-all | bytes 32768 | tf_op jit(solution)/shard_map/all_to_all | solution.py:803
  38.3 1.3 %shard_map.75 = (f32[3,2,16,128]{3,2,1,0:T(8,128)}, f32[3,2,16,128]{3,2,1,0:T(8,128)}) custom-call(f32[32,128]{1,0:T(8,128)S(1)} %bitcast.6, f32[3,2,24,128]{3,2,1,0:T(8,128)S(1)} %get-tuple-element.42.refs_0_.refs_8_.refs_1_, f32[3,2,24,128]{3,2,1,0:T(8,128)S(1)} %get-tuple-element.43.refs_1_.refs_9_.refs_2_, ...), custom_call_target="tpu_custom_call" | custom-call | tf_op jit(solution)/shard_map/pallas_call | solution.py:804
  (1 shorter events, 0.0 us)
Async XLA Ops:
  2.1 8.0 %collective-permute-start = (f32[2,3,2,16,128]{4,3,2,1,0:T(8,128)S(1)}, f32[2,3,2,16,128]{4,3,2,1,0:T(8,128)S(1)}, u32[]{:S(2)}, u32[]{:S(2)}) collective-permute-start(f32[2,3,2,16,128]{4,3,2,1,0:T(8,128)S(1)} %get-tuple-element.28.here.refs_0_), channel_id=1, source_target_pairs={{0,4},{4,0},{8,12},{12,8},{16,20},{20,16},{24,28},{28,24},{1,5},{5... | collective-permute-start | bytes 294920 | tf_op jit(solution)/shard_map/ppermute | solution.py:745
  5.2 12.3 %all-to-all-start = ((bf16[32,8,128]{2,1,0:T(8,128)(2,1)}), bf16[32,8,128]{2,1,0:T(8,128)(2,1)S(1)}, u32[]{:S(2)}, u32[]{:S(2)}) async-start(bf16[32,8,128]{2,1,0:T(8,128)(2,1)} %get-tuple-element.31), calls=%async_computation | async-start | bytes 131072 | tf_op jit(solution)/shard_map/all_to_all | solution.py:746
  10.1 8.2 %collective-permute-start.1 = (f32[2,6,2,4,128]{4,3,2,1,0:T(4,128)S(1)}, f32[2,6,2,4,128]{4,3,2,1,0:T(4,128)S(1)}, u32[]{:S(2)}, u32[]{:S(2)}) collective-permute-start(f32[2,6,2,4,128]{4,3,2,1,0:T(4,128)S(1)} %get-tuple-element.29), channel_id=1, source_target_pairs={{0,3},{1,0},{2,1},{3,2},{4,7},{5,4},{6,5},{7,6},{8,11},{9,8},{10,9... | collective-permute-start | bytes 147464 | tf_op jit(solution)/shard_map/ppermute | solution.py:669
  11.7 6.6 %collective-permute-start.2 = (f32[2,6,2,4,128]{4,3,2,1,0:T(4,128)S(1)}, f32[2,6,2,4,128]{4,3,2,1,0:T(4,128)S(1)}, u32[]{:S(2)}, u32[]{:S(2)}) collective-permute-start(f32[2,6,2,4,128]{4,3,2,1,0:T(4,128)S(1)} %get-tuple-element.30), channel_id=1, source_target_pairs={{0,1},{1,2},{2,3},{3,0},{4,5},{5,6},{6,7},{7,4},{8,9},{9,10},{10,1... | collective-permute-start | bytes 147464 | tf_op jit(solution)/shard_map/ppermute | solution.py:669
  18.5 3.3 %collective-permute-start.3 = (f32[168,128]{1,0:T(8,128)S(1)}, f32[168,128]{1,0:T(8,128)S(1)}, u32[]{:S(2)}, u32[]{:S(2)}) collective-permute-start(f32[168,128]{1,0:T(8,128)S(1)} %get-tuple-element.34), channel_id=1, source_target_pairs={{0,8},{1,0},{2,10},{3,2},{4,12},{5,4},{6,14},{7,6},{8,16},{9,1},{1... | collective-permute-start | bytes 258056 | tf_op jit(solution)/shard_map/ppermute | solution.py:682
  19.1 4.5 %collective-permute-start.4 = (f32[168,128]{1,0:T(8,128)S(1)}, f32[168,128]{1,0:T(8,128)S(1)}, u32[]{:S(2)}, u32[]{:S(2)}) collective-permute-start(f32[168,128]{1,0:T(8,128)S(1)} %get-tuple-element.35), channel_id=1, source_target_pairs={{0,1},{1,9},{2,3},{3,11},{4,5},{5,13},{6,7},{7,15},{8,0},{9,17},{1... | collective-permute-start | bytes 258056 | tf_op jit(solution)/shard_map/ppermute | solution.py:682
  23.9 2.5 %collective-permute-start.5 = (f32[120,128]{1,0:T(8,128)S(1)}, f32[120,128]{1,0:T(8,128)S(1)}, u32[]{:S(2)}, u32[]{:S(2)}) collective-permute-start(f32[120,128]{1,0:T(8,128)S(1)} %get-tuple-element.40), channel_id=1, source_target_pairs={{0,8},{1,0},{2,10},{3,2},{4,12},{5,4},{6,14},{7,6},{8,16},{9,1},{1... | collective-permute-start | bytes 184328 | tf_op jit(solution)/shard_map/ppermute | solution.py:682
  24.5 4.2 %collective-permute-start.6 = (f32[120,128]{1,0:T(8,128)S(1)}, f32[120,128]{1,0:T(8,128)S(1)}, u32[]{:S(2)}, u32[]{:S(2)}) collective-permute-start(f32[120,128]{1,0:T(8,128)S(1)} %get-tuple-element.41), channel_id=1, source_target_pairs={{0,1},{1,9},{2,3},{3,11},{4,5},{5,13},{6,7},{7,15},{8,0},{9,17},{1... | collective-permute-start | bytes 184328 | tf_op jit(solution)/shard_map/ppermute | solution.py:682
